TPU v7x, 32 devices: a whole 2x2x4 slice. The times are simulated.
32 devices in a mesh: dp: 8 (over y, x, core), mp: 4 (over z).
Axes of the slice: x: 2, y: 2, z: 4, core: 2. Of those that a mesh axis runs over, the one named last changes fastest.
Arguments:
- layer_input: float32 [12288, 1024], P(('dp', 'mp')), may hold values from -6 to 6
- norm_gains: bfloat16 [2, 1024], replicated, may hold values from 0.5 to 1.5
- query_weight: bfloat16 [1024, 1024], P(None, 'mp'), may hold values from -0.03125 to 0.03125
- key_value_weight: bfloat16 [1024, 2, 1024], P(None, None, 'mp'), may hold values from -0.1875 to 0.1875
- output_weight: bfloat16 [1024, 1024], P('mp'), may hold values from -1 to 1
- gate_up_weight: bfloat16 [1024, 2, 2816], P(None, None, 'mp'), may hold values from -0.1875 to 0.1875
- down_weight: bfloat16 [2816, 1024], P('mp'), may hold values from -0.15625 to 0.15625
- bias_tables: bfloat16 [3, 32, 16], P(None, None, 'mp'), may hold values from -3 to 3
- doc_lengths: int32 [16], P('dp'), may hold values from 522 to 768, as said below
- box_bins: int32 [2, 12288], P(None, 'dp'), may hold values from 0 to 63
- cotangent: float32 [12288, 1024], P(('dp', 'mp')), may hold values from -6 to 6
Outputs:
- layer_output: float32 [12288, 1024], P(('dp', 'mp'))
- input_grad: float32 [12288, 1024], P(('dp', 'mp'))
- gain_grad: float32 [2, 1024], P(None, ('dp', 'mp'))
- query_grad: float32 [1024, 1024], P('dp', 'mp')
- key_value_grad: float32 [1024, 2, 1024], P('dp', None, 'mp')
- output_grad: float32 [1024, 1024], P('mp', 'dp')
- gate_up_grad: float32 [1024, 2, 2816], P('dp', None, 'mp')
- down_grad: float32 [2816, 1024], P('mp', 'dp')
- table_grad: float32 [3, 32, 16], P(None, 'dp', 'mp')
Inputs may be any that keep to these rules, and one draw needn't show every extreme that they name: `doc_lengths`: each aligned block of 8 slots holds exactly one table slot of 768 tokens; the others are forms of 522 to 706 tokens; positions at or beyond a slot's length are padding.
All inputs are finite; a program needn't handle non-finite values.
Results may differ from a plain program's by a relative error of at most 0.02.
Values may be sent and summed in bfloat16 or wider, within the bound.
A program may use at most 256 MiB of HBM per device.

v0:
```python
from functools import partial

import jax
import jax.numpy as jnp
from jax import lax
from jax.sharding import PartitionSpec as P

NBIN = 64


EPSILON = 1e-06
THRESHOLDS = (8, 12, 16, 23, 32, 46, 64, 91)
NEG_FILL = -1e30


def bucket_of(relative):
    distance = jnp.abs(relative)
    bucket = jnp.minimum(distance, 7)
    for threshold in THRESHOLDS:
        bucket = bucket + (distance >= threshold).astype(jnp.int32)
    return bucket + 16 * (relative > 0).astype(jnp.int32)


def norm_rows(values, gain_vector):
    return (
        values
        * lax.rsqrt(jnp.mean(values * values, axis=-1, keepdims=True) + EPSILON)
        * gain_vector
    )


def gelu_tanh(values):
    return jax.nn.gelu(values, approximate=True)


def line_table(line_weights, slot_span):
    offsets = jnp.arange(2 * slot_span - 1, dtype=jnp.int32) - (slot_span - 1)
    bucket_ids = jnp.arange(line_weights.shape[0], dtype=jnp.int32)
    onehot = (bucket_of(offsets)[:, None] == bucket_ids[None, :]).astype(jnp.float32)
    diagonal_values = jnp.dot(onehot, line_weights, precision=lax.Precision.HIGHEST).T
    padded = jnp.pad(diagonal_values, ((0, 0), (0, 1)))
    repeated = jnp.tile(padded, (1, slot_span))
    skewed = repeated[:, : slot_span * (2 * slot_span - 1)].reshape(
        -1, slot_span, 2 * slot_span - 1
    )
    return skewed[:, :, slot_span - 1 :]


def layout_table(table_values, bin_count):
    bin_ids = jnp.arange(bin_count, dtype=jnp.int32)
    offsets = bin_ids[None, :] - bin_ids[:, None]
    bucket_ids = jnp.arange(table_values.shape[1], dtype=jnp.int32)
    onehot = (bucket_of(offsets)[:, :, None] == bucket_ids[None, None, :]).astype(jnp.float32)
    x_part = jnp.einsum("abn,nh->hab", onehot, table_values[1], precision=lax.Precision.HIGHEST)
    y_part = jnp.einsum("abn,nh->hab", onehot, table_values[2], precision=lax.Precision.HIGHEST)
    empty_block = jnp.zeros_like(x_part)
    upper_rows = jnp.concatenate([x_part, empty_block], axis=2)
    lower_rows = jnp.concatenate([empty_block, y_part], axis=2)
    return jnp.concatenate([upper_rows, lower_rows], axis=1)


def build_tables(table_values, slot_span, bin_count):
    return (line_table(table_values[0], slot_span), layout_table(table_values, bin_count))


def project_ffn(full_rows, w_gate_up, ff_here):
    gate_up = jnp.dot(full_rows, w_gate_up, preferred_element_type=jnp.float32)
    return (gate_up[:, :ff_here], gate_up[:, ff_here:])


def contract_rows(left_rows, right_rows):
    return lax.dot_general(
        left_rows, right_rows, (((0,), (0,)), ((), ())), preferred_element_type=jnp.float32
    )


def contract_cols(left_rows, right_rows):
    return lax.dot_general(
        left_rows, right_rows, (((1,), (1,)), ((), ())), preferred_element_type=jnp.float32
    )


def per_device(
    layer_input,
    norm_gains,
    query_weight,
    key_value_weight,
    output_weight,
    gate_up_weight,
    down_weight,
    bias_tables,
    doc_lengths,
    box_bins,
    cotangent,
):
    row_count, model_width = layer_input.shape
    doc_count = doc_lengths.shape[0]
    group_rows = box_bins.shape[1]
    slot_span = group_rows // doc_count
    heads_here = bias_tables.shape[2]
    inner_cols = query_weight.shape[1]
    head_size = inner_cols // heads_here
    ff_here = gate_up_weight.shape[2]
    bin_count = NBIN
    gain_first = norm_gains[0].astype(jnp.float32)
    gain_second = norm_gains[1].astype(jnp.float32)
    w_inner = jnp.concatenate(
        [query_weight, key_value_weight.reshape(model_width, 2 * inner_cols)], axis=1
    )
    w_gate_up = gate_up_weight.reshape(model_width, 2 * ff_here)
    (line_bias, layout_full), table_pull = jax.vjp(
        partial(build_tables, slot_span=slot_span, bin_count=bin_count),
        bias_tables.astype(jnp.float32),
    )
    layout_weights = layout_full.astype(jnp.bfloat16)
    box_coords = box_bins.reshape(2, doc_count, slot_span)
    bin_ids = jnp.arange(bin_count, dtype=jnp.int32)
    placed = jnp.concatenate(
        [box_coords[0][..., None] == bin_ids, box_coords[1][..., None] == bin_ids], axis=-1
    ).astype(jnp.bfloat16)
    key_valid = jnp.arange(slot_span, dtype=jnp.int32)[None, :] < doc_lengths[:, None]

    def doc_scores(query_part, key_part, placed_doc, valid_doc):
        layout_rows = jnp.einsum(
            "sa,hab->hsb", placed_doc, layout_weights, preferred_element_type=jnp.float32
        ).astype(jnp.bfloat16)
        layout_bias = jnp.einsum(
            "hsb,tb->hst", layout_rows, placed_doc, preferred_element_type=jnp.float32
        )
        scores = (
            jnp.einsum("ihd,jhd->hij", query_part, key_part, preferred_element_type=jnp.float32)
            + line_bias
            + layout_bias
        )
        return jnp.where(valid_doc[None, None, :], scores, NEG_FILL)

    def split_heads(inner_rows):
        parts = inner_rows.reshape(doc_count, slot_span, 3, heads_here, head_size)
        return (parts[:, :, 0], parts[:, :, 1], parts[:, :, 2])

    normed_first = norm_rows(layer_input, gain_first).astype(jnp.bfloat16)
    full_first = lax.all_gather(normed_first, "mp", axis=0, tiled=True)
    inner_rows = jnp.dot(full_first, w_inner, preferred_element_type=jnp.float32).astype(
        jnp.bfloat16
    )
    queries, key_rows, value_rows = split_heads(inner_rows)

    def attend_doc(doc_items):
        query_part, key_part, value_part, placed_doc, valid_doc = doc_items
        scores = doc_scores(query_part, key_part, placed_doc, valid_doc)
        row_max = jnp.max(scores, axis=-1, keepdims=True)
        row_total = jnp.sum(jnp.exp(scores - row_max), axis=-1, keepdims=True)
        log_total = row_max + jnp.log(row_total)
        attn_probs = jnp.exp(scores - log_total).astype(jnp.bfloat16)
        mixed_heads = jnp.einsum(
            "hij,jhd->ihd", attn_probs, value_part, preferred_element_type=jnp.float32
        )
        return (mixed_heads.reshape(slot_span, inner_cols).astype(jnp.bfloat16), log_total[..., 0])

    heads_out, log_totals = lax.map(attend_doc, (queries, key_rows, value_rows, placed, key_valid))
    heads_out = heads_out.reshape(group_rows, inner_cols)
    branch = lax.psum_scatter(
        jnp.dot(heads_out, output_weight, preferred_element_type=jnp.float32),
        "mp",
        scatter_dimension=0,
        tiled=True,
    )
    residual = layer_input + branch
    normed_second = norm_rows(residual, gain_second).astype(jnp.bfloat16)
    full_second = lax.all_gather(normed_second, "mp", axis=0, tiled=True)
    gate_part, up_part = project_ffn(full_second, w_gate_up, ff_here)
    activated = (gelu_tanh(gate_part) * up_part).astype(jnp.bfloat16)
    layer_output = residual + lax.psum_scatter(
        jnp.dot(activated, down_weight, preferred_element_type=jnp.float32).astype(jnp.bfloat16),
        "mp",
        scatter_dimension=0,
        tiled=True,
    ).astype(jnp.float32)
    back_second, gate_back, up_back, act_back = (full_second, gate_part, up_part, activated)
    out_low = cotangent.astype(jnp.bfloat16)
    shard_piece = lax.all_gather(out_low, "mp", axis=0, tiled=True)
    grad_down = contract_rows(act_back, shard_piece)
    grad_act = contract_cols(shard_piece, down_weight)
    grad_down, grad_act = (grad_down, grad_act)
    gelu_value, gelu_pull = jax.vjp(gelu_tanh, gate_back)
    grad_gate = gelu_pull(grad_act * up_back)[0]
    grad_up = grad_act * gelu_value
    grad_gate_up = jnp.concatenate([grad_gate, grad_up], axis=1).astype(jnp.bfloat16)
    grad_w_gate_up = contract_rows(back_second, grad_gate_up).reshape(model_width, 2, ff_here)
    grad_normed_second = lax.psum_scatter(
        contract_cols(grad_gate_up, w_gate_up), "mp", scatter_dimension=0, tiled=True
    )
    unused_second, second_pull = jax.vjp(norm_rows, residual, gain_second)
    grad_res_part, grad_gain_second = second_pull(grad_normed_second)
    grad_residual = cotangent + grad_res_part
    branch_low = grad_residual.astype(jnp.bfloat16)
    shard_piece = lax.all_gather(branch_low, "mp", axis=0, tiled=True)
    grad_output = contract_rows(heads_out, shard_piece)
    grad_heads = contract_cols(shard_piece, output_weight)
    grad_output, grad_heads = (grad_output, grad_heads)
    grad_heads = grad_heads.astype(jnp.bfloat16).reshape(
        doc_count, slot_span, heads_here, head_size
    )
    back_first, back_inner = (full_first, inner_rows)
    queries_back, keys_back, values_back = split_heads(back_inner)

    def attend_back(carry_state, doc_items):
        grad_line, grad_layout = carry_state
        query_part, key_part, value_part, placed_doc, valid_doc, log_total, grad_mixed = doc_items
        scores = doc_scores(query_part, key_part, placed_doc, valid_doc)
        attn_probs = jnp.exp(scores - log_total[..., None])
        probs_low = attn_probs.astype(jnp.bfloat16)
        grad_probs = jnp.einsum(
            "ihd,jhd->hij", grad_mixed, value_part, preferred_element_type=jnp.float32
        )
        row_dot = jnp.sum(attn_probs * grad_probs, axis=-1, keepdims=True)
        grad_scores = (attn_probs * (grad_probs - row_dot)).astype(jnp.bfloat16)
        grad_query = jnp.einsum(
            "hij,jhd->ihd", grad_scores, key_part, preferred_element_type=jnp.float32
        )
        grad_key = jnp.einsum(
            "hij,ihd->jhd", grad_scores, query_part, preferred_element_type=jnp.float32
        )
        grad_value = jnp.einsum(
            "hij,ihd->jhd", probs_low, grad_mixed, preferred_element_type=jnp.float32
        )
        grad_line = grad_line + grad_scores.astype(jnp.float32)
        key_bins = jnp.einsum(
            "hst,tb->hsb", grad_scores, placed_doc, preferred_element_type=jnp.float32
        )
        grad_layout = grad_layout + jnp.einsum(
            "sa,hsb->hab", placed_doc.astype(jnp.float32), key_bins, precision=lax.Precision.HIGHEST
        )
        stacked = jnp.stack([grad_query, grad_key, grad_value], axis=1).reshape(
            slot_span, 3 * inner_cols
        )
        return ((grad_line, grad_layout), stacked.astype(jnp.bfloat16))

    back_start = (
        jnp.zeros((heads_here, slot_span, slot_span), jnp.float32),
        jnp.zeros((heads_here, 2 * bin_count, 2 * bin_count), jnp.float32),
    )
    (grad_line, grad_layout), grad_inner = lax.scan(
        attend_back,
        back_start,
        (queries_back, keys_back, values_back, placed, key_valid, log_totals, grad_heads),
    )
    grad_inner = grad_inner.reshape(group_rows, 3 * inner_cols)
    grad_w_inner = contract_rows(back_first, grad_inner)
    grad_normed_first = lax.psum_scatter(
        contract_cols(grad_inner, w_inner).astype(jnp.bfloat16),
        "mp",
        scatter_dimension=0,
        tiled=True,
    ).astype(jnp.float32)
    unused_first, first_pull = jax.vjp(norm_rows, layer_input, gain_first)
    grad_in_part, grad_gain_first = first_pull(grad_normed_first)
    input_grad = grad_residual + grad_in_part
    grad_tables = table_pull((grad_line, grad_layout))[0]
    gain_grad = lax.psum_scatter(
        jnp.stack([grad_gain_first, grad_gain_second]),
        ("dp", "mp"),
        scatter_dimension=1,
        tiled=True,
    )
    grad_w_query = grad_w_inner[:, :inner_cols]
    grad_w_key_value = grad_w_inner[:, inner_cols:].reshape(model_width, 2, inner_cols)
    summed = (
        lax.psum_scatter(
            grad_w_query.astype(jnp.bfloat16), "dp", scatter_dimension=0, tiled=True
        ).astype(jnp.float32),
        lax.psum_scatter(
            grad_w_key_value.astype(jnp.bfloat16), "dp", scatter_dimension=0, tiled=True
        ).astype(jnp.float32),
        lax.psum_scatter(
            grad_output.astype(jnp.bfloat16), "dp", scatter_dimension=1, tiled=True
        ).astype(jnp.float32),
        lax.psum_scatter(
            grad_w_gate_up.astype(jnp.bfloat16), "dp", scatter_dimension=0, tiled=True
        ).astype(jnp.float32),
        lax.psum_scatter(
            grad_down.astype(jnp.bfloat16), "dp", scatter_dimension=1, tiled=True
        ).astype(jnp.float32),
        lax.psum_scatter(
            grad_tables.astype(jnp.bfloat16), "dp", scatter_dimension=1, tiled=True
        ).astype(jnp.float32),
    )
    query_grad, key_value_grad, output_grad, gate_up_grad, down_grad, table_grad = summed
    return (
        layer_output,
        input_grad,
        gain_grad,
        query_grad,
        key_value_grad,
        output_grad,
        gate_up_grad,
        down_grad,
        table_grad,
    )


def solution(mesh):
    return jax.shard_map(
        per_device,
        mesh=mesh,
        in_specs=(
            P(("dp", "mp"), None),
            P(),
            P(None, "mp"),
            P(None, None, "mp"),
            P("mp", None),
            P(None, None, "mp"),
            P("mp", None),
            P(None, None, "mp"),
            P("dp"),
            P(None, "dp"),
            P(("dp", "mp"), None),
        ),
        out_specs=(
            P(("dp", "mp"), None),
            P(("dp", "mp"), None),
            P(None, ("dp", "mp")),
            P("dp", "mp"),
            P("dp", None, "mp"),
            P("mp", "dp"),
            P("dp", None, "mp"),
            P("mp", "dp"),
            P(None, "dp", "mp"),
        ),
        check_vma=False,
    )
```

profile of v0, /device:TPU:0, one launch (start us, length us, event | category | flops | bytes accessed | tf_op | source)
XLA Modules:
  0.0 1217.4 jit_solution(18136132169187697657)
XLA Ops:
  11.5 2.5 multiply_convert_fusion.4
  17.8 9.4 broadcast_bitcast_fusion
  27.3 21.2 %copy.120 = f32[1,4,768,1536]{3,1,2,0:T(4,128)S(1)} copy(f32[1,4,768,1536]{3,2,1,0:T(8,128)} %broadcast_bitcast_fusion) | data formatting | bytes 37748736
  48.5 7.5 slice.77
  56.1 54.1 %reshape.274 = f32[4715520]{0:T(1024)} reshape(f32[4,1178880]{1,0:T(4,128)} %slice.77) | data formatting | bytes 37724160
  110.1 29.7 %reshape.238 = f32[4,768,1535]{2,1,0:T(8,128)} reshape(f32[4715520]{0:T(1024)} %reshape.274) | data formatting | bytes 37724160 | tf_op jit(solution)/shard_map/jvp()/reshape | solution.py:43
  139.9 10.3 slice.78
  150.2 9.7 copy.72
  164.9 6.4 convolution_convert_fusion.7
  171.4 4.3 copy.68
  175.7 6.0 reshape.237
  181.6 2.9 slice_bitcast_fusion
  187.5 61.0 %while.27 = (s32[]{:T(128)}, bf16[2,768,256]{2,1,0:T(8,128)(2,1)}, f32[2,4,768]{2,1,0:T(4,128)S(1)}, bf16[2,768,4,64]{1,3,2,0:T(8,128)(2,1)}, pred[2,768]{1,0:T(...) while((s32[]{:T(128)}, bf16[2,768,256]{2,1,0:T(8,128)(2,1)}, ...), condition=%wide.region_4.5_spmd, body=%wide.region_1.4_spmd.sunk | while | flops 1328083968 | bytes 98144672 | solution.py:160
  187.7 6.2 fusion.196
  193.9 10.8 fusion.197
  204.7 5.1 exponential_reduce_fusion.2
  211.0 3.3 fusion.198
  218.1 6.2 fusion.196
  224.3 10.8 fusion.197
  235.1 5.1 exponential_reduce_fusion.2
  241.4 3.3 fusion.198
  248.5 4.9 fusion.130
  253.5 113.6 %reduce-scatter.21.cloned.1.call-done = f32[384,1024]{1,0:T(8,128)} async-done(((f32[1536,1024]{1,0:T(8,128)}), f32[384,1024]{1,0:T(8,128)}) %reduce-scatter.21.cloned.1.call-update) | async-done | bytes 1572880 | tf_op jit(solution)/shard_map/reduce_scatter | solution.py:162
  371.5 2.4 convert_element_type.338
  374.0 61.6 %all-gather.7.cloned.1.call-done = bf16[1536,1024]{1,0:T(8,128)(2,1)} async-done(((bf16[384,1024]{1,0:T(8,128)(2,1)}), bf16[1536,1024]{1,0:T(8,128)(2,1)}) %all-gather.7.cloned.1.call-update) | async-done | bytes 3145744 | tf_op jit(solution)/shard_map/all_gather | solution.py:170
  435.6 9.0 fusion.131
  444.6 54.6 %all-gather.9.cloned.1.call-done = bf16[1536,1024]{1,0:T(8,128)(2,1)} async-done(((bf16[384,1024]{1,0:T(8,128)(2,1)}), bf16[1536,1024]{1,0:T(8,128)(2,1)}) %all-gather.9.cloned.1.call-update) | async-done | bytes 3145744 | tf_op jit(solution)/shard_map/all_gather | solution.py:181
  499.2 10.3 fusion.71
  511.5 7.0 fusion.72
  519.9 5.8 convolution_convert_fusion.6
  525.8 102.4 %reduce-scatter.25.cloned.1.call-done = f32[384,1024]{1,0:T(8,128)} async-done(((f32[1536,1024]{1,0:T(8,128)}), f32[384,1024]{1,0:T(8,128)}) %reduce-scatter.25.cloned.1.call-update) | async-done | bytes 1572880 | tf_op jit(solution)/shard_map/reduce_scatter | solution.py:190
  630.5 60.6 %reduce-scatter.23.cloned.1.call-done = bf16[384,1024]{1,0:T(8,128)(2,1)} async-done(((bf16[1536,1024]{1,0:T(8,128)(2,1)}), bf16[384,1024]{1,0:T(8,128)(2,1)}) %reduce-scatter.23.cloned.1.call-update) | async-done | bytes 786448 | tf_op jit(solution)/shard_map/reduce_scatter | solution.py:173
  691.1 4.5 fusion.123
  695.7 4.9 convolution_convert_fusion.10
  702.3 10.0 convolution_convert_fusion.4
  712.4 46.9 %all-gather.11.cloned.1.call-done = bf16[1536,1024]{1,0:T(8,128)(2,1)} async-done(((bf16[384,1024]{1,0:T(8,128)(2,1)}), bf16[1536,1024]{1,0:T(8,128)(2,1)}) %all-gather.11.cloned.1.call-update) | async-done | bytes 3145744 | tf_op jit(solution)/shard_map/all_gather | solution.py:197
  759.3 2.9 convolution_convert_fusion.8
  764.8 108.4 %while.28 = (s32[]{:T(128)}, f32[4,768,768]{1,2,0:T(8,128)}, f32[4,128,128]{1,2,0:T(8,128)}, bf16[2,768,768]{2,1,0:T(8,128)(2,1)}, pred[2,768]{1,0:T(4,128)(4,1)...) while((s32[]{:T(128)}, f32[4,768,768]{1,2,0:T(8,128)}, ...), condition=%wide.region_12.13_spmd.clone, body=%wide.region_10.12_spmd.clone.sunk | while | flops 3455513600 | bytes 176096720 | solution.py:243
  764.9 6.3 fusion.215
  771.1 6.3 fusion.216
  777.4 15.2 %multiply_reduce_fusion.6 = (f32[4,768]{1,0:T(4,128)S(1)}, f32[4,768,768]{1,2,0:T(8,128)}) fusion(f32[4,768,768]{1,2,0:T(8,128)} %fusion.215, f32[4,768]{1,0:T(4,128)S(1)} %dynamic-slice_bitcast_fusion.2, bf16[2,768,128]{2,1,0:T(8,128)(2,1)S(1)} %get-tuple-element.576, s32[]{:T(128)S(6)} %copy.144, bf16[4,128,128]{2,1,0:T(8,128)(2,1)S(1)} %get-tuple-element.577, ...), kind=kOutput, calls=%fused_computation.26.clone.1 | convolution fusion | flops 719188992 | bytes 38299392 | tf_op jit(solution)/shard_map/while/body/eval_jaxpr/hsb,tb->hst/dot_general | solution.py:127
  792.6 5.6 fusion.219
  799.2 9.4 select_add_fusion.4
  810.5 2.6 fusion.220
  817.5 6.3 fusion.215
  823.7 6.4 fusion.216
  830.1 15.1 %multiply_reduce_fusion.6 = (f32[4,768]{1,0:T(4,128)S(1)}, f32[4,768,768]{1,2,0:T(8,128)}) fusion(f32[4,768,768]{1,2,0:T(8,128)} %fusion.215, f32[4,768]{1,0:T(4,128)S(1)} %dynamic-slice_bitcast_fusion.2, bf16[2,768,128]{2,1,0:T(8,128)(2,1)S(1)} %get-tuple-element.576, s32[]{:T(128)S(6)} %copy.144, bf16[4,128,128]{2,1,0:T(8,128)(2,1)S(1)} %get-tuple-element.577, ...), kind=kOutput, calls=%fused_computation.26.clone.1 | convolution fusion | flops 719188992 | bytes 38299392 | tf_op jit(solution)/shard_map/while/body/eval_jaxpr/hsb,tb->hst/dot_general | solution.py:127
  845.3 5.6 fusion.219
  851.8 11.5 select_add_fusion.4
  865.3 2.5 fusion.220
  868.6 2.5 fusion.218
  873.2 5.3 convolution_convert_fusion.9
  880.7 3.1 convolution_convert_fusion.11
  886.0 6.4 convolution_convert_fusion.5
  900.1 9.9 copy.118
  910.0 12.2 %pad.31.clone = f32[4,768,1535]{2,1,0:T(8,128)} pad(f32[4,768,768]{2,1,0:T(8,128)} %copy.118, f32[]{:T(128)} %constant.33.clone.1), padding=0_0x0_0x767_0 | pad | bytes 28299268 | tf_op jit(solution)/shard_map/transpose(jvp())/pad | solution.py:46
  922.2 28.8 %reshape.276 = f32[4715520]{0:T(1024)} reshape(f32[4,768,1535]{2,1,0:T(8,128)} %pad.31.clone) | data formatting | bytes 37724160
  951.1 23.5 %reshape.245 = f32[4,1178880]{1,0:T(4,128)} reshape(f32[4715520]{0:T(1024)} %reshape.276) | data formatting | bytes 37724160 | tf_op jit(solution)/shard_map/transpose(jvp())/reshape | solution.py:43
  974.5 17.8 %pad.32 = f32[4,1179648]{1,0:T(4,128)} pad(f32[4,1178880]{1,0:T(4,128)} %reshape.245, f32[]{:T(128)} %constant.33.clone.1), padding=0_0x0_768 | pad | bytes 37736452 | tf_op jit(solution)/shard_map/transpose(jvp())/pad | solution.py:43
  992.3 11.4 bitcast_reduce_fusion
  1005.6 13.4 %all-reduce.9 = bf16[3,32,4]{1,2,0:T(4,128)(2,1)S(1)} all-reduce(bf16[3,32,4]{1,2,0:T(4,128)(2,1)S(1)} %add_convert_fusion.1), channel_id=12, replica_groups=mesh['dp'=8,'mp'=4] {'dp'}, use_global_device_ids=true, to_apply=%region_24.25.clone | all-reduce | flops 384 | bytes 1536
  1024.8 47.5 %reduce-scatter.27.cloned.1.call-done = bf16[384,1024]{1,0:T(8,128)(2,1)} async-done(((bf16[1536,1024]{1,0:T(8,128)(2,1)}), bf16[384,1024]{1,0:T(8,128)(2,1)}) %reduce-scatter.27.cloned.1.call-update) | async-done | bytes 786448 | tf_op jit(solution)/shard_map/reduce_scatter | solution.py:250
  1075.1 3.7 fusion.78
  1078.7 130.5 %reduce-scatter.29.cloned.1.call-done = f32[32,2]{1,0:T(8,128)} async-done(((f32[1024,2]{1,0:T(8,128)}), f32[32,2]{1,0:T(8,128)}) %reduce-scatter.29.cloned.1.call-update) | async-done | bytes 272
  (178 shorter events, 76.2 us)
Async XLA Ops:
  7.2 428.4 %copy-start = (bf16[1024,2,704]{0,2,1:T(8,128)(2,1)S(1)}, bf16[1024,2,704]{0,2,1:T(8,128)(2,1)}, u32[]{:S(2)}) copy-start(bf16[1024,2,704]{0,2,1:T(8,128)(2,1)} %param.20) | copy-start | bytes 8650756
  7.2 6.9 copy-start.18
  7.2 7.1 copy-start.23
  7.2 157.7 %all-gather.5.cloned.1.call-start = ((), (), s32[]{:S(2)}) async-start(), calls=%async_computation.9 | async-start | bytes 3932160 | tf_op jit(solution)/shard_map/all_gather | solution.py:142
  9.0 0.6 copy-start.15
  9.6 1.4 copy-start.13
  10.9 0.6 copy-start.9
  14.1 353.0 %reduce-scatter.21.cloned.1.call-start = ((), (), s32[]{:S(2)}) async-start(), calls=%async_computation.10 | async-start | bytes 7864320 | tf_op jit(solution)/shard_map/reduce_scatter | solution.py:162
  14.3 0.7 copy-start.11
  17.4 9.9 copy-start.19
  159.9 5.0 copy-start.21
  204.7 6.4 copy-start.3
  235.1 6.4 copy-start.3
  253.4 116.9 %copy-start.8 = (f32[1,1024]{1,0:T(1,128)S(1)}, f32[1,1024]{1,0:T(1,128)}, u32[]{:S(2)}) copy-start(f32[1,1024]{1,0:T(1,128)} %get-tuple-element.345) | copy-start | bytes 12292
  253.4 182.2 %all-gather.7.cloned.1.call-start = ((), (), s32[]{:S(2)}) async-start(), calls=%async_computation.11 | async-start | bytes 3932160 | tf_op jit(solution)/shard_map/all_gather | solution.py:170
  369.2 1.1 copy-start.5
  371.4 127.8 %all-gather.9.cloned.1.call-start = ((), (), s32[]{:S(2)}) async-start(), calls=%async_computation.13 | async-start | bytes 3932160 | tf_op jit(solution)/shard_map/all_gather | solution.py:181
  373.9 254.2 %reduce-scatter.25.cloned.1.call-start = ((), (), s32[]{:S(2)}) async-start(), calls=%async_computation.14 | async-start | bytes 7864320 | tf_op jit(solution)/shard_map/reduce_scatter | solution.py:190
  509.5 1.4 copy-start.25
  509.5 2.0 copy-start.26
  518.5 1.4 copy-start.22
  518.6 172.5 %reduce-scatter.23.cloned.1.call-start = ((), (), s32[]{:S(2)}) async-start(), calls=%async_computation.12 | async-start | bytes 3932160 | tf_op jit(solution)/shard_map/reduce_scatter | solution.py:173
  525.7 102.4 %copy-start.6 = (f32[384,1024]{1,0:T(8,128)S(1)}, f32[384,1024]{1,0:T(8,128)}, u32[]{:S(2)}) copy-start(f32[384,1024]{1,0:T(8,128)} %copy-done.5) | copy-start | bytes 4718596
  525.7 233.6 %all-gather.11.cloned.1.call-start = ((), (), s32[]{:S(2)}) async-start(), calls=%async_computation.15 | async-start | bytes 3932160 | tf_op jit(solution)/shard_map/all_gather | solution.py:197
  695.6 199.4 %reduce-scatter.37.cloned.1.call-start = ((), (), s32[]{:S(2)}) async-start(), calls=%async_computation.21 | async-start | bytes 1769472
  702.2 194.7 %reduce-scatter.35.cloned.1.call-start = ((), (), s32[]{:S(2)}) async-start(), calls=%async_computation.20 | async-start | bytes 3244032
  702.3 57.0 %copy-start.7 = (bf16[256,1024]{1,0:T(8,128)(2,1)S(1)}, bf16[256,1024]{1,0:T(8,128)(2,1)}, u32[]{:S(2)}) copy-start(bf16[256,1024]{1,0:T(8,128)(2,1)} %param.19) | copy-start | bytes 1572868
  712.4 307.4 %all-reduce.12.cloned.1.call-start = ((), (), s32[]{:S(2)}) async-start(), calls=%async_computation.22 | async-start | bytes 2097152
  792.6 6.6 copy-start.2
  845.3 6.6 copy-start.2
  880.6 140.8 %reduce-scatter.33.cloned.1.call-start = ((), (), s32[]{:S(2)}) async-start(), calls=%async_computation.19 | async-start | bytes 589824
  884.9 138.2 %reduce-scatter.31.cloned.1.call-start = ((), (), s32[]{:S(2)}) async-start(), calls=%async_computation.18 | async-start | bytes 589824
  886.0 186.3 %reduce-scatter.27.cloned.1.call-start = ((), (), s32[]{:S(2)}) async-start(), calls=%async_computation.16 | async-start | bytes 3932160 | tf_op jit(solution)/shard_map/reduce_scatter | solution.py:250
  892.5 0.7 copy-start.24
  892.5 316.8 %reduce-scatter.29.cloned.1.call-start = ((), (), s32[]{:S(2)}) async-start(), calls=%async_computation.17 | async-start | bytes 540672
  992.3 11.4 copy-start.20
  992.3 11.9 copy-start.12
  992.3 80.0 %copy-start.10 = (f32[1,1024]{1,0:T(1,128)S(1)}, f32[1,1024]{1,0:T(1,128)}, u32[]{:S(2)}) copy-start(f32[1,1024]{1,0:T(1,128)} %copy-done.9) | copy-start | bytes 12292
  992.3 80.0 %copy-start.14 = (f32[384]{0:T(512)S(1)}, f32[384]{0:T(512)}, u32[]{:S(2)}) copy-start(f32[384]{0:T(512)} %copy-done.13) | copy-start | bytes 4612
  1003.7 68.6 %copy-start.4 = (f32[384,1024]{1,0:T(8,128)S(1)}, f32[384,1024]{1,0:T(8,128)}, u32[]{:S(2)}) copy-start(f32[384,1024]{1,0:T(8,128)} %param.15) | copy-start | bytes 4718596
  1003.7 70.2 %copy-start.16 = (f32[384]{0:T(512)S(1)}, f32[384]{0:T(512)}, u32[]{:S(2)}) copy-start(f32[384]{0:T(512)} %copy-done.15) | copy-start | bytes 4612
  1003.7 70.2 %copy-start.17 = (f32[1024]{0:T(1024)S(1)}, f32[1024]{0:T(1024)}, u32[]{:S(2)}) copy-start(f32[1024]{0:T(1024)} %get-tuple-element.274) | copy-start | bytes 12292
  1074.0 136.6 %copy-start.1 = (bf16[1024,2,704]{0,2,1:T(8,128)(2,1)S(1)}, bf16[1024,2,704]{0,2,1:T(8,128)(2,1)}, u32[]{:S(2)}) copy-start(bf16[1024,2,704]{0,2,1:T(8,128)(2,1)} %param.20) | copy-start | bytes 8650756
Sparse Core Ops, SparseCore 0:
  14.2 66.1 all-gather.4
  253.5 113.4 reduce-scatter.20
  371.5 64.0 all-gather.6
  437.0 62.1 all-gather.8
  518.7 109.3 reduce-scatter.24
  630.3 60.7 reduce-scatter.22
  695.7 63.5 all-gather.10
  762.6 37.0 reduce-scatter.36
  803.1 44.9 reduce-scatter.34
  880.7 55.1 all-reduce.11
  939.3 33.1 reduce-scatter.32
  975.5 34.0 reduce-scatter.30
  1012.0 60.2 reduce-scatter.26
  1075.2 134.0 reduce-scatter.28
where the time goes:
time: 1220 us
  waiting for transfers between devices  618 us (51%)
  local copies, waits for them, and re-layouts  297 us (24%)
  matrix products  201 us (16%)
  other arithmetic  71.4 us (6%)
  between operations  16 us (1%)
  blocking collectives  13.4 us (1%)
    unnamed x70, local copies, waits for them, and re-layouts  148 us
    unnamed x20, waiting for transfers between devices  131 us
    reduce_scatter x1, waiting for transfers between devices, per_device(): lax.psum_scatter(jnp.dot(heads_out, output_weight, preferred_element_type...  114 us
    reduce_scatter x1, waiting for transfers between devices, per_device(): lax.psum_scatter(contract_cols(grad_gate_up, w_gate_up), 'mp', scatter_di...  102 us
    all_gather x1, waiting for transfers between devices, per_device(): full_second = lax.all_gather(normed_second, 'mp', axis=0, tiled=True)  61.6 us
    reduce_scatter x1, waiting for transfers between devices, per_device(): lax.psum_scatter(jnp.dot(activated, down_weight, preferred_element_type=j...  60.6 us
    all_gather x1, waiting for transfers between devices, per_device(): shard_piece = lax.all_gather(out_low, 'mp', axis=0, tiled=True)  54.6 us
    reshape x2, local copies, waits for them, and re-layouts, line_table(): repeated[:, :slot_span * (2 * slot_span - 1)]  53.2 us
  transfers between devices with their start and end apart: 14, of which 8 were waited for; matrix products, arithmetic and copies ran while one was open for 36% of the time, Pallas kernels for 0%

commit v1 on v0

v1 whole, which is shorter than its diff:
```python
from functools import partial

import jax
import jax.numpy as jnp
import numpy as np
from jax import lax
from jax.experimental import pallas as pl
from jax.experimental.pallas import tpu as pltpu
from jax.sharding import PartitionSpec as P

NBIN = 64
EPSILON = 1e-06
THRESHOLDS = (8, 12, 16, 23, 32, 46, 64, 91)
NEG_FILL = -1e30
LANES = 128
MESH = pl.DeviceIdType.MESH
HBM = pltpu.MemorySpace.HBM
BF16 = jnp.bfloat16
F32 = jnp.float32


def bucket_of(relative):
    distance = jnp.abs(relative)
    bucket = jnp.minimum(distance, 7)
    for threshold in THRESHOLDS:
        bucket = bucket + (distance >= threshold).astype(jnp.int32)
    return bucket + 16 * (relative > 0).astype(jnp.int32)


def inverse_rms(values):
    return lax.rsqrt(jnp.mean(values * values, axis=-1, keepdims=True) + EPSILON)


def dot_f32(left, right, left_dim, right_dim):
    return lax.dot_general(
        left, right, (((left_dim,), (right_dim,)), ((), ())), preferred_element_type=F32
    )


def three_parts(values):
    high = values.astype(BF16)
    rest = values - high.astype(F32)
    middle = rest.astype(BF16)
    low = (rest - middle.astype(F32)).astype(BF16)
    return high, middle, low


def lane_ids(shape):
    return lax.broadcasted_iota(jnp.int32, shape, 1)


def row_ids(shape):
    return lax.broadcasted_iota(jnp.int32, shape, 0)


def attend_kernel(
    q_ref, k_ref, v_ref, layout_ref, line_ref, key_extra_ref, query_bins_ref,
    out_ref, lse_ref,
    key_aug, query_aug, strip, scores, probs,
):
    head_size, rows = q_ref.shape
    keys = k_ref.shape[1]
    blocks = keys // LANES
    width = strip.shape[1]

    @pl.when(pl.program_id(0) == 0)
    def _():
        key_aug[...] = key_extra_ref[...]
        tail = row_ids((64, rows))
        query_aug[pl.ds(192, 64), :] = jnp.where(tail == 0, 1.0, 0.0).astype(BF16)

    both = jnp.concatenate([k_ref[...], v_ref[...]], axis=0).T
    low_lanes = lane_ids((keys, LANES)) < head_size
    key_aug[:, 0:LANES] = jnp.where(low_lanes, both, key_extra_ref[:, 0:LANES])
    query_aug[pl.ds(0, 64), :] = q_ref[...]
    query_aug[pl.ds(64, 128), :] = jnp.dot(
        layout_ref[0], query_bins_ref[...], preferred_element_type=F32
    ).astype(BF16)
    strip[...] = pltpu.roll(
        jnp.broadcast_to(line_ref[0], (LANES, width)), 0, 1, stride=1, stride_axis=0
    )
    query_all = query_aug[...]
    top = jnp.full((1, rows), -jnp.inf, F32)
    for block in range(blocks):
        here = pl.ds(block * LANES, LANES)
        part = jnp.dot(key_aug[here, :], query_all, preferred_element_type=F32)
        part = part + strip[:, pl.ds((blocks - 1 - block) * LANES, rows)]
        scores[here, :] = part
        top = jnp.maximum(top, jnp.max(part, axis=0, keepdims=True))
    total = jnp.zeros((1, rows), F32)
    for block in range(blocks):
        here = pl.ds(block * LANES, LANES)
        part = jnp.exp(scores[here, :] - top)
        total = total + jnp.sum(part, axis=0, keepdims=True)
        probs[here, :] = part.astype(BF16)
    mixed = jnp.dot(v_ref[...], probs[...], preferred_element_type=F32)
    out_ref[...] = (mixed / total).astype(BF16)
    lse_ref[0] = top + jnp.log(total)


def attend_back_kernel(
    q_ref, k_ref, v_ref, out_ref, out_grad_ref, lse_ref, layout_ref, line_ref,
    key_extra_ref, key_extra_t_ref, query_bins_ref, query_bins_t_ref,
    dq_ref, dk_ref, dv_ref, line_grad_ref, layout_grad_ref,
    key_aug, key_aug_t, query_aug, value_aug, grad_aug, strip, strip_grad, probs_grad,
):
    head_size, rows = q_ref.shape
    keys = k_ref.shape[1]
    blocks = keys // LANES
    width = strip.shape[1]

    @pl.when(pl.program_id(0) == 0)
    def _():
        key_aug[...] = key_extra_ref[...]
        key_aug_t[pl.ds(64, 128), :] = key_extra_t_ref[...]
        tail = row_ids((64, rows))
        query_aug[pl.ds(192, 64), :] = jnp.where(tail == 0, 1.0, 0.0).astype(BF16)

    both = jnp.concatenate([k_ref[...], v_ref[...]], axis=0).T
    lanes = lane_ids((keys, LANES))
    key_aug[:, 0:LANES] = jnp.where(lanes < head_size, both, key_extra_ref[:, 0:LANES])
    ones = jnp.where(lanes < 3, 1.0, 0.0).astype(BF16)
    value_aug[...] = jnp.where(lanes < head_size, ones, both)
    key_aug_t[pl.ds(0, 64), :] = k_ref[...]
    query_aug[pl.ds(0, 64), :] = q_ref[...]
    query_aug[pl.ds(64, 128), :] = jnp.dot(
        layout_ref[0], query_bins_ref[...], preferred_element_type=F32
    ).astype(BF16)
    high, middle, low = three_parts(-lse_ref[0])
    tail = row_ids((64, rows))
    rows_of = lambda part: jnp.broadcast_to(part.astype(F32), (64, rows))
    query_aug[pl.ds(192, 64), :] = jnp.where(
        tail == 0, 1.0,
        jnp.where(
            tail == 1, rows_of(high),
            jnp.where(tail == 2, rows_of(middle), jnp.where(tail == 3, rows_of(low), 0.0)),
        ),
    ).astype(BF16)
    row_dot = jnp.sum(
        out_grad_ref[...].astype(F32) * out_ref[...].astype(F32), axis=0, keepdims=True
    )
    high, middle, low = three_parts(-row_dot)
    grad_aug[pl.ds(0, 64), :] = jnp.where(
        tail == 0, rows_of(high),
        jnp.where(tail == 1, rows_of(middle), jnp.where(tail == 2, rows_of(low), 0.0)),
    ).astype(BF16)
    grad_aug[pl.ds(64, 64), :] = out_grad_ref[...]
    strip[...] = pltpu.roll(
        jnp.broadcast_to(line_ref[0], (LANES, width)), 0, 1, stride=1, stride_axis=0
    )
    strip_grad[...] = jnp.zeros_like(strip_grad)
    query_and_grad = jnp.concatenate([q_ref[...], out_grad_ref[...]], axis=0).T
    query_all = query_aug[...]
    grad_all = grad_aug[...]
    half = lane_ids((LANES, LANES)) < head_size
    for block in range(blocks):
        here = pl.ds(block * LANES, LANES)
        band = pl.ds((blocks - 1 - block) * LANES, rows)
        part = jnp.dot(key_aug[here, :], query_all, preferred_element_type=F32)
        part = jnp.exp(part + strip[:, band])
        slope = part * jnp.dot(value_aug[here, :], grad_all, preferred_element_type=F32)
        strip_grad[:, band] = strip_grad[:, band] + slope
        slope = slope.astype(BF16)
        probs_grad[here, :] = slope
        key_part = jnp.dot(slope, query_and_grad, preferred_element_type=F32)
        value_part = jnp.dot(part.astype(BF16), query_and_grad, preferred_element_type=F32)
        turned = jnp.where(half, key_part, value_part).T.astype(BF16)
        dk_ref[:, here] = turned[0:64]
        dv_ref[:, here] = turned[64:128]
    query_part = jnp.dot(key_aug_t[...], probs_grad[...], preferred_element_type=F32)
    dq_ref[...] = query_part[0:64].astype(BF16)
    layout_grad_ref[0] = jnp.dot(
        query_part[64:192].astype(BF16), query_bins_t_ref[...], preferred_element_type=F32
    )
    folded = strip_grad[pl.ds(0, 8), :]
    for group in range(1, LANES // 8):
        folded = folded + pltpu.roll(strip_grad[pl.ds(group * 8, 8), :], width - group * 8, 1)
    line = folded[0:1]
    for row in range(1, 8):
        line = line + pltpu.roll(folded[row : row + 1], width - row, 1)
    line_grad_ref[0] = line


class Place:
    def __init__(self, mp_size):
        self.dp = lax.axis_index("dp")
        self.mp = lax.axis_index("mp")
        self.mp_size = mp_size
        self.core = lax.rem(self.dp, 2)
        self.x = lax.rem(lax.div(self.dp, 2), 2)
        self.y = lax.div(self.dp, 4)
        self.to_core = (self.dp + 1 - 2 * self.core, self.mp)
        self.to_x = (self.dp + 2 - 4 * self.x, self.mp)
        self.to_y = (self.dp + 4 - 8 * self.y, self.mp)

    def to_mp(self, step):
        return (self.dp, lax.rem(self.mp + step, self.mp_size))

    def from_mp(self, step):
        return lax.rem(self.mp + self.mp_size - step, self.mp_size)

    def partners(self):
        others = [self.to_mp(step) for step in range(1, self.mp_size)]
        return [self.to_core, self.to_x, self.to_y] + others


def meet(place):
    barrier = pltpu.get_barrier_semaphore()
    partners = place.partners()
    for partner in partners:
        pl.semaphore_signal(barrier, inc=1, device_id=partner, device_id_type=MESH)
    pl.semaphore_wait(barrier, len(partners))


class Copy:
    def __init__(self, source, target, send, receive=None, partner=None):
        self.parts = (source, target, send, receive, partner)

    def made(self):
        source, target, send, receive, partner = self.parts
        if partner is None:
            return pltpu.make_async_copy(source, target, send)
        return pltpu.make_async_remote_copy(
            src_ref=source, dst_ref=target, send_sem=send, recv_sem=receive,
            device_id=partner, device_id_type=MESH,
        )

    def start(self):
        self.made().start()

    def wait(self):
        self.made().wait()

    def wait_send(self):
        self.made().wait_send()

    def wait_recv(self):
        self.made().wait_recv()


def remote(source, target, send, receive, partner):
    return Copy(source, target, send, receive, partner)


def lanes_at(block, count):
    return pl.ds(pl.multiple_of(block * LANES, LANES), count * LANES)


class Gather:
    LAGS = 4

    def __init__(self, place, pieces, outs, sems):
        self.place, self.pieces, self.outs = place, pieces, outs
        self.z_send, self.z_recv, self.own_sem, self.send, self.recv = sems
        self.items = [(c, k) for c in range(len(pieces)) for k in range(place.mp_size)]
        self.steps = len(self.items) + self.LAGS

    @staticmethod
    def semaphores(count, mp_size):
        dma = pltpu.SemaphoreType.DMA
        items = count * mp_size
        return [
            dma((count, mp_size)), dma((count, mp_size)), dma((count,)), dma((items, 6)), dma((items, 6))
        ]

    def rows(self, c, source, half):
        n = self.pieces[c].shape[1]
        if half is None:
            return pl.ds(pl.multiple_of(source * n, 16), n)
        return pl.ds(pl.multiple_of(source * n + half * (n // 2), 16), n // 2)

    def window(self, c, source, half, block, count):
        return self.outs[c].at[:, self.rows(c, source, half), lanes_at(block, count)]

    def own(self, c):
        place = self.place
        block = place.core * 4 + place.y * 2 + place.x
        return Copy(
            self.pieces[c], self.window(c, place.mp, None, block, 1), self.own_sem.at[c]
        )

    def along_mp(self, c, step):
        place = self.place
        block = place.core * 4 + place.y * 2 + place.x
        return remote(
            self.pieces[c], self.window(c, place.mp, None, block, 1),
            self.z_send.at[c, step], self.z_recv.at[c, step], place.to_mp(step),
        )

    def start_chunk(self, c):
        self.own(c).start()
        for step in range(1, self.place.mp_size):
            self.along_mp(c, step).start()

    def copies(self, t):
        c, k = self.items[t]
        place = self.place
        source = place.from_mp(k)
        base = place.core * 4
        mine = base + place.y * 2 + place.x
        turned = base + (1 - place.y) * 2 + place.x

        def copy(i, half, block, count, partner):
            here = self.window(c, source, half, block, count)
            return remote(here, here, self.send.at[t, i], self.recv.at[t, i], partner)

        first = [copy(0, 0, mine, 1, place.to_x), copy(1, 1, mine, 1, place.to_y)]
        second = [
            copy(2, 0, base + place.y * 2, 2, place.to_y),
            copy(3, 1, mine, 1, place.to_x),
            copy(4, 1, turned, 1, place.to_x),
        ]
        third = [copy(5, None, base, 4, place.to_core)]
        return first, second, third

    def step(self, s):
        count = len(self.items)
        if s == 0:
            self.start_chunk(0)
            if len(self.pieces) > 1:
                self.start_chunk(1)
        if s < count:
            c, k = self.items[s]
            if k == 0:
                self.own(c).wait()
                if s > 0 and c + 1 < len(self.pieces):
                    self.start_chunk(c + 1)
            else:
                self.along_mp(c, k).wait_recv()
            for copy in self.copies(s)[0]:
                copy.start()
        if 0 <= s - 1 < count:
            first, second, _ = self.copies(s - 1)
            for copy in first:
                copy.wait_recv()
            for copy in second:
                copy.start()
        if 0 <= s - 2 < count:
            _, second, third = self.copies(s - 2)
            for copy in second:
                copy.wait_recv()
            third[0].start()
        if 0 <= s - 4 < count:
            first, second, third = self.copies(s - 4)
            third[0].wait_recv()
            for copy in first + second + third:
                copy.wait_send()
            c, k = self.items[s - 4]
            if k > 0:
                self.along_mp(c, k).wait_send()


def add_rows(target, target_index, source, source_index):
    lead, rows, lanes = target_index
    source_rows, source_lanes = source_index
    row_start, count = rows
    source_start = source_rows
    size = 32
    while count % size:
        size //= 2

    def body(i, carry):
        here = pl.ds(pl.multiple_of(row_start + i * size, size), size)
        there = pl.ds(pl.multiple_of(source_start + i * size, size), size)
        for part in range(lead):
            target[part, here, lanes] = target[part, here, lanes] + source[part, there, source_lanes]
        return carry

    lax.fori_loop(0, count // size, body, 0)


class Scatter:
    LAGS = 4

    def __init__(self, place, fulls, outs, buffers, sems):
        self.place, self.fulls, self.outs = place, fulls, outs
        self.sums, self.from_core, self.from_first, self.from_second, self.from_mp = buffers
        self.own_sem, self.send, self.recv = sems
        self.items = [
            (c, k) for c in range(len(fulls)) for k in list(range(1, place.mp_size)) + [0]
        ]
        self.steps = len(self.items) + self.LAGS + 1

    @staticmethod
    def semaphores(count, mp_size):
        dma = pltpu.SemaphoreType.DMA
        items = count * mp_size
        return [dma((items,)), dma((items, 7)), dma((items, 7))]

    @staticmethod
    def buffers(shapes, mp_size):
        out = []
        for blocks in (4, 4, 2, 1, 1):
            for lead, n in shapes:
                out.append(pltpu.VMEM((mp_size, lead, n, blocks * LANES), BF16))
        return out

    @staticmethod
    def group(refs, count):
        return [refs[i * count : (i + 1) * count] for i in range(5)]

    def size(self, c):
        return self.fulls[c].shape[0], self.fulls[c].shape[1] // self.place.mp_size

    def copies(self, t):
        c, k = self.items[t]
        place = self.place
        lead, n = self.size(c)
        target = lax.rem(place.mp + k, place.mp_size)
        rows = pl.ds(pl.multiple_of(target * n, 16), n)
        top, bottom = pl.ds(0, n // 2), pl.ds(n // 2, n // 2)
        every = pl.ds(0, lead)
        sums = self.sums[c].at[k]
        full = self.fulls[c]

        def copy(i, source, landing, partner):
            return remote(source, landing, self.send.at[t, i], self.recv.at[t, i], partner)

        own = Copy(
            full.at[:, rows, lanes_at(place.core * 4, 4)], sums, self.own_sem.at[t]
        )
        core = copy(
            0, full.at[:, rows, lanes_at((1 - place.core) * 4, 4)], self.from_core[c].at[k], place.to_core
        )
        landing = self.from_first[c].at[k]
        first = [
            copy(
                1, sums.at[every, top, lanes_at((1 - place.y) * 2, 2)],
                landing.at[every, top, pl.ds(0, 256)], place.to_y,
            ),
            copy(
                2, sums.at[every, bottom, lanes_at(1 - place.x, 1)],
                landing.at[every, bottom, pl.ds(0, 128)], place.to_x,
            ),
            copy(
                3, sums.at[every, bottom, lanes_at(3 - place.x, 1)],
                landing.at[every, bottom, pl.ds(128, 128)], place.to_x,
            ),
        ]
        landing = self.from_second[c].at[k]
        second = [
            copy(
                4, sums.at[every, top, lanes_at(place.y * 2 + 1 - place.x, 1)],
                landing.at[every, top, pl.ds(0, 128)], place.to_x,
            ),
            copy(
                5, sums.at[every, bottom, lanes_at((1 - place.y) * 2 + place.x, 1)],
                landing.at[every, bottom, pl.ds(0, 128)], place.to_y,
            ),
        ]
        third = None
        if k > 0:
            third = copy(
                6, sums.at[:, :, lanes_at(place.y * 2 + place.x, 1)], self.from_mp[c].at[k],
                place.to_mp(k),
            )
        return own, core, first, second, third

    def step(self, s):
        count = len(self.items)
        place = self.place
        if s < count:
            own, core, *_ = self.copies(s)
            core.start()
            own.start()
        if 0 <= s - 1 < count:
            t = s - 1
            c, k = self.items[t]
            lead, n = self.size(c)
            own, core, first, *_ = self.copies(t)
            own.wait()
            core.wait_recv()
            add_rows(
                self.sums[c].at[k], (lead, (0, n), pl.ds(0, 512)), self.from_core[c].at[k], (0, pl.ds(0, 512))
            )
            for copy in first:
                copy.start()
        if 0 <= s - 2 < count:
            t = s - 2
            c, k = self.items[t]
            lead, n = self.size(c)
            _, _, first, second, _ = self.copies(t)
            for copy in first:
                copy.wait_recv()
            sums, landing = self.sums[c].at[k], self.from_first[c].at[k]
            half = n // 2
            add_rows(sums, (lead, (0, half), lanes_at(place.y * 2, 2)), landing, (0, pl.ds(0, 256)))
            add_rows(sums, (lead, (half, half), lanes_at(place.x, 1)), landing, (half, pl.ds(0, 128)))
            add_rows(
                sums, (lead, (half, half), lanes_at(2 + place.x, 1)), landing, (half, pl.ds(128, 128))
            )
            for copy in second:
                copy.start()
        if 0 <= s - 3 < count:
            t = s - 3
            c, k = self.items[t]
            lead, n = self.size(c)
            _, _, _, second, third = self.copies(t)
            for copy in second:
                copy.wait_recv()
            sums, landing = self.sums[c].at[k], self.from_second[c].at[k]
            mine = lanes_at(place.y * 2 + place.x, 1)
            add_rows(sums, (lead, (0, n), mine), landing, (0, pl.ds(0, 128)))
            if third is not None:
                third.start()
        if 0 <= s - 5 < count:
            t = s - 5
            c, k = self.items[t]
            _, core, first, second, third = self.copies(t)
            for copy in [core] + first + second:
                copy.wait_send()
            if third is not None:
                third.wait_send()
                third.wait_recv()
            else:
                self.finish(c)

    def finish(self, c):
        place = self.place
        lead, n = self.size(c)
        mine = lanes_at(place.y * 2 + place.x, 1)
        sums, landing, out = self.sums[c], self.from_mp[c], self.outs[c]
        size = 32
        while n % size:
            size //= 2

        def body(i, carry):
            here = pl.ds(pl.multiple_of(i * size, size), size)
            for part in range(lead):
                total = sums[0, part, here, mine].astype(F32)
                for k in range(1, place.mp_size):
                    total = total + landing[k, part, here, :].astype(F32)
                out[part, here, :] = total
            return carry

        lax.fori_loop(0, n // size, body, 0)


def attention_shapes(head_count, head_size, rows, keys, width):
    whole = lambda shape: pl.BlockSpec(shape, lambda head: (0,) * len(shape))
    column = lambda size: pl.BlockSpec((head_size, size), lambda head: (head, 0))
    page = lambda a, b: pl.BlockSpec((1, a, b), lambda head: (head, 0, 0))
    return whole, column, page


def attend(mp_size, pieces, queries, keys_t, values_t, layout, line, key_extra, query_bins):
    inner, rows = queries.shape
    keys = keys_t.shape[1]
    head_count, _, width = line.shape
    head_size = inner // head_count
    whole, column, page = attention_shapes(head_count, head_size, rows, keys, width)
    hbm = pl.BlockSpec(memory_space=HBM)
    return pl.pallas_call(
        partial(attend_gather_kernel, mp_size, head_count, len(pieces)) if pieces else attend_kernel,
        grid=(head_count,),
        out_shape=(
            jax.ShapeDtypeStruct((inner, rows), BF16),
            jax.ShapeDtypeStruct((head_count, 1, rows), F32),
        )
        + tuple(
            jax.ShapeDtypeStruct((p.shape[0], p.shape[1] * mp_size, 8 * LANES), BF16) for p in pieces
        ),
        in_specs=[
            column(rows), column(keys), column(keys), page(128, 128), page(1, width),
            whole((keys, 256)), whole((128, rows)),
        ]
        + [hbm] * len(pieces),
        out_specs=(column(rows), page(1, rows)) + (hbm,) * len(pieces),
        scratch_shapes=[
            pltpu.VMEM((keys, 256), BF16),
            pltpu.VMEM((256, rows), BF16),
            pltpu.VMEM((LANES, width), F32),
            pltpu.VMEM((keys, rows), F32),
            pltpu.VMEM((keys, rows), BF16),
        ]
        + (Gather.semaphores(len(pieces), mp_size) if pieces else []),
        compiler_params=pltpu.CompilerParams(
            dimension_semantics=("arbitrary",), vmem_limit_bytes=32 << 20,
            **(dict(collective_id=1, has_side_effects=True) if pieces else {}),
        ),
        name="attend",
    )(queries, keys_t, values_t, layout, line, key_extra, query_bins, *pieces)


def attend_back(
    mp_size, fulls, queries, keys_t, values_t, heads_out, heads_grad, lse, layout, line,
    key_extra, key_extra_t, query_bins, query_bins_t,
):
    inner, rows = queries.shape
    keys = keys_t.shape[1]
    head_count, _, width = line.shape
    head_size = inner // head_count
    whole, column, page = attention_shapes(head_count, head_size, rows, keys, width)
    hbm = pl.BlockSpec(memory_space=HBM)
    sizes = [(full.shape[0], full.shape[1] // mp_size) for full in fulls]
    return pl.pallas_call(
        partial(attend_back_scatter_kernel, mp_size, head_count, len(fulls))
        if fulls
        else attend_back_kernel,
        grid=(head_count,),
        out_shape=(
            jax.ShapeDtypeStruct((inner, rows), BF16),
            jax.ShapeDtypeStruct((inner, keys), BF16),
            jax.ShapeDtypeStruct((inner, keys), BF16),
            jax.ShapeDtypeStruct((head_count, 1, width), F32),
            jax.ShapeDtypeStruct((head_count, 128, 128), F32),
        )
        + tuple(jax.ShapeDtypeStruct((lead, n, LANES), F32) for lead, n in sizes),
        in_specs=[
            column(rows), column(keys), column(keys), column(rows), column(rows),
            page(1, rows), page(128, 128), page(1, width),
            whole((keys, 256)), whole((128, keys)), whole((128, rows)), whole((rows, 128)),
        ]
        + [hbm] * len(fulls),
        out_specs=(column(rows), column(keys), column(keys), page(1, width), page(128, 128))
        + tuple(whole((lead, n, LANES)) for lead, n in sizes),
        scratch_shapes=[
            pltpu.VMEM((keys, 256), BF16),
            pltpu.VMEM((192, keys), BF16),
            pltpu.VMEM((256, rows), BF16),
            pltpu.VMEM((keys, 128), BF16),
            pltpu.VMEM((128, rows), BF16),
            pltpu.VMEM((LANES, width), F32),
            pltpu.VMEM((LANES, width), F32),
            pltpu.VMEM((keys, rows), BF16),
        ]
        + (Scatter.buffers(sizes, mp_size) + Scatter.semaphores(len(fulls), mp_size) if fulls else []),
        compiler_params=pltpu.CompilerParams(
            dimension_semantics=("arbitrary",), vmem_limit_bytes=56 << 20,
            **(dict(collective_id=2, has_side_effects=True) if fulls else {}),
        ),
        name="attend_back",
    )(
        queries, keys_t, values_t, heads_out, heads_grad, lse, layout, line,
        key_extra, key_extra_t, query_bins, query_bins_t, *fulls,
    )


def spread(step_count, heads):
    if step_count <= heads:
        return [[s] if s < step_count else [] for s in range(heads)]
    return [[s for s in range(step_count) if s * heads // step_count == h] for h in range(heads)]


def run_steps(task, heads):
    head = pl.program_id(0)
    for h, steps in enumerate(spread(task.steps, heads)):
        if steps:

            @pl.when(head == h)
            def _(steps=steps):
                for s in steps:
                    task.step(s)


def attend_gather_kernel(mp_size, heads, count, *refs):
    ins, refs = refs[:7], refs[7:]
    pieces, refs = refs[:count], refs[count:]
    outs, refs = refs[:2], refs[2:]
    fulls, refs = refs[:count], refs[count:]
    scratch, sems = refs[:5], refs[5:]
    place = Place(mp_size)

    @pl.when(pl.program_id(0) == 0)
    def _():
        meet(place)

    run_steps(Gather(place, pieces, fulls, sems), heads)
    attend_kernel(*ins, *outs, *scratch)


def attend_back_scatter_kernel(mp_size, heads, count, *refs):
    ins, refs = refs[:12], refs[12:]
    fulls, refs = refs[:count], refs[count:]
    outs, refs = refs[:5], refs[5:]
    sums, refs = refs[:count], refs[count:]
    scratch, refs = refs[:8], refs[8:]
    buffers, sems = Scatter.group(refs[: 5 * count], count), refs[5 * count :]
    place = Place(mp_size)

    @pl.when(pl.program_id(0) == 0)
    def _():
        meet(place)

    run_steps(Scatter(place, fulls, sums, buffers, sems), heads)
    attend_back_kernel(*ins, *outs, *scratch)


def gather_first_kernel(mp_size, group, *refs):
    weights, normed, table, full, slot_rows, tables, *sems = refs
    row_sems, table_sems, sems = sems[:3], sems[3:6], sems[6:]
    place = Place(mp_size)
    rows = normed.shape[0]
    first = lax.div(place.mp, group) * group
    member = lax.rem(place.mp, group)
    window = slot_rows.at[pl.ds(pl.multiple_of(member * rows, 16), rows), :]
    copies = []
    for k in range(1, group):
        peer = (place.dp, first + lax.rem(member + k, group))
        copies.append(remote(normed, window, row_sems[0].at[k], row_sems[1].at[k], peer))
    for k in range(1, mp_size):
        copies.append(
            remote(table, tables.at[place.mp], table_sems[0].at[k], table_sems[1].at[k], place.to_mp(k))
        )
    own = [
        Copy(normed, window, row_sems[2].at[0]),
        Copy(table, tables.at[place.mp], table_sems[2].at[0]),
    ]
    gather = Gather(place, [weights], [full], sems)
    for copy in own:
        copy.start()
    meet(place)
    gather.step(0)
    for copy in copies:
        copy.start()
    for s in range(1, gather.steps):
        gather.step(s)
    for copy in own:
        copy.wait()
    for copy in copies:
        copy.wait_send()
        copy.wait_recv()


def gather_first(mp_size, group, weights, normed, table):
    lead, n, _ = weights.shape
    rows, model_width = normed.shape
    dma = pltpu.SemaphoreType.DMA
    hbm = pl.BlockSpec(memory_space=HBM)
    return pl.pallas_call(
        partial(gather_first_kernel, mp_size, group),
        out_shape=(
            jax.ShapeDtypeStruct((lead, mp_size * n, model_width), BF16),
            jax.ShapeDtypeStruct((group * rows, model_width), BF16),
            jax.ShapeDtypeStruct((mp_size, 8, LANES), F32),
        ),
        in_specs=[hbm] * 3,
        out_specs=(hbm,) * 3,
        scratch_shapes=[dma((group,)), dma((group,)), dma((1,)), dma((mp_size,)), dma((mp_size,)), dma((1,))]
        + Gather.semaphores(1, mp_size),
        compiler_params=pltpu.CompilerParams(collective_id=0, has_side_effects=True),
        name="gather_first",
    )(weights, normed, table)


def last_kernel(mp_size, group, *refs):
    (full, slot_grad, own_grad, layer_input, residual_grad, gains, small,
     out, input_grad, small_out, *refs) = refs
    buffers, refs = Scatter.group(refs[:5], 1), refs[5:]
    peers, stage, stage_in, row_sems, stage_sems = refs[:3] + [refs[3:5], refs[5:7]]
    sems = refs[7:]
    place = Place(mp_size)
    rows, model_width = own_grad.shape
    first = lax.div(place.mp, group) * group
    member = lax.rem(place.mp, group)
    rows_out = []
    for k in range(1, group):
        other = lax.rem(member + k, group)
        rows_out.append(
            remote(
                slot_grad.at[pl.ds(pl.multiple_of(other * rows, 16), rows), :], peers.at[k - 1],
                row_sems[0].at[k], row_sems[1].at[k], (place.dp, first + other),
            )
        )
    partners = [place.to_core, place.to_x, place.to_y]
    bit = 1
    while bit < mp_size:
        flipped = place.mp + bit - 2 * bit * lax.rem(lax.div(place.mp, bit), 2)
        partners.append((place.dp, flipped))
        bit *= 2
    stages = [
        remote(stage.at[i], stage_in.at[i], stage_sems[0].at[i], stage_sems[1].at[i], partner)
        for i, partner in enumerate(partners)
    ]
    scatter = Scatter(place, [full], [out], buffers, sems)
    meet(place)
    for copy in rows_out:
        copy.start()
    for s in range(5):
        scatter.step(s)
    for copy in rows_out:
        copy.wait_recv()
    size = 16

    def body(i, total):
        here = pl.ds(pl.multiple_of(i * size, size), size)
        grad = own_grad[here, :]
        for k in range(group - 1):
            grad = grad + peers[k, here, :].astype(F32)
        values = layer_input[here, :]
        scale = lax.rsqrt(jnp.mean(values * values, axis=1, keepdims=True) + EPSILON)
        scaled = gains[0:1, :] * grad
        mean = jnp.mean(scaled * values, axis=1, keepdims=True)
        input_grad[here, :] = (
            residual_grad[here, :] + scale * scaled - values * (scale * scale * scale * mean)
        )
        product = grad * values * scale
        return total + product[0:8] + product[8:16]

    total = lax.fori_loop(0, rows // size, body, jnp.zeros((8, model_width), F32))
    gain = jnp.sum(total, axis=0, keepdims=True)
    for i in range(model_width // LANES):
        stage[0, i : i + 1, :] = gain[:, i * LANES : (i + 1) * LANES]
    gain_rows = model_width // LANES
    stage[0, gain_rows : small.shape[0] + gain_rows, :] = small[...]
    stages[0].start()
    at = 5
    for i, copy in enumerate(stages):
        if at < scatter.steps:
            scatter.step(at)
            at += 1
        copy.wait_recv()
        if i + 1 < len(stages):
            stage[i + 1] = stage[i] + stage_in[i]
            stages[i + 1].start()
        else:
            small_out[...] = stage[i] + stage_in[i]
    for s in range(at, scatter.steps):
        scatter.step(s)
    for copy in rows_out + stages:
        copy.wait_send()


def last_step(mp_size, group, full, slot_grad, own_grad, layer_input, residual_grad, gains, small):
    lead, total_rows, model_width = full.shape
    n = total_rows // mp_size
    rows = own_grad.shape[0]
    small_rows = small.shape[0] + model_width // LANES
    count = 3 + (mp_size - 1).bit_length()
    dma = pltpu.SemaphoreType.DMA
    hbm = pl.BlockSpec(memory_space=HBM)
    vmem = pl.BlockSpec(memory_space=pltpu.VMEM)
    return pl.pallas_call(
        partial(last_kernel, mp_size, group),
        out_shape=(
            jax.ShapeDtypeStruct((lead, n, LANES), F32),
            jax.ShapeDtypeStruct((rows, model_width), F32),
            jax.ShapeDtypeStruct((small_rows, LANES), F32),
        ),
        in_specs=[hbm, hbm] + [vmem] * 5,
        out_specs=(vmem,) * 3,
        scratch_shapes=Scatter.buffers([(lead, n)], mp_size)
        + [
            pltpu.VMEM((max(group - 1, 1), rows, model_width), BF16),
            pltpu.VMEM((count, small_rows, LANES), F32),
            pltpu.VMEM((count, small_rows, LANES), F32),
            dma((group,)), dma((group,)), dma((count,)), dma((count,)),
        ]
        + Scatter.semaphores(1, mp_size),
        compiler_params=pltpu.CompilerParams(
            collective_id=3, has_side_effects=True, vmem_limit_bytes=48 << 20
        ),
        name="last_step",
    )(full, slot_grad, own_grad, layer_input, residual_grad, gains, small)


def line_onehot(first_row, width, key_blocks):
    place = jnp.arange(width, dtype=jnp.int32)
    place = jnp.where(place >= width - LANES, place - width, place)
    offset = LANES * (key_blocks - 1) - place - first_row
    return (bucket_of(offset)[:, None] == jnp.arange(32, dtype=jnp.int32)[None, :]).astype(F32)


def bin_onehot():
    bins = np.arange(NBIN)
    offset = bins[:, None] - bins[None, :]
    distance = np.abs(offset)
    bucket = np.minimum(distance, 7) + sum((distance >= t).astype(np.int64) for t in THRESHOLDS)
    bucket = bucket + 16 * (offset > 0)
    return jnp.asarray(bucket[:, :, None] == np.arange(32), F32)


def gather_rows(local, axis_name):
    return lax.all_gather(local, axis_name, axis=0, tiled=True)


def scatter_grad(full):
    summed = lax.psum_scatter(full, "dp", scatter_dimension=1, tiled=True)
    return lax.psum_scatter(summed, "mp", scatter_dimension=0, tiled=True)


def per_device(
    dp_size, mp_size,
    layer_input, norm_gains, query_weight, key_value_weight, output_weight,
    gate_up_weight, down_weight, bias_tables, doc_lengths, box_bins, cotangent,
):
    rows, model_width = layer_input.shape
    doc_count = doc_lengths.shape[0]
    slot_span = box_bins.shape[1] // doc_count
    group = mp_size // doc_count
    mp_index = lax.axis_index("mp")
    doc = mp_index // group
    first_row = (mp_index % group) * rows
    key_blocks = slot_span // LANES
    width = LANES * (key_blocks + (rows + LANES - 1) // LANES)
    groups = [[d * group + i for i in range(group)] for d in range(doc_count)]
    gain_first = norm_gains[0].astype(F32)
    gain_second = norm_gains[1].astype(F32)

    scale_first = inverse_rms(layer_input)
    normed = (layer_input * scale_first * gain_first).astype(BF16)
    heads_here = bias_tables.shape[2]
    head_count = heads_here * mp_size
    custom = dp_size == 8 and model_width == 8 * LANES and mp_size & (mp_size - 1) == 0
    custom = custom and 3 * 32 * heads_here <= 8 * LANES

    if custom:
        dp_index = lax.axis_index("dp")
        column = ((dp_index % 2) * 4 + dp_index // 2) * LANES
        piece = lambda weight, axis: lax.dynamic_slice_in_dim(weight, column, LANES, axis)
        key_value_piece = jnp.transpose(piece(key_value_weight, 0), (1, 2, 0))
        first_pieces = jnp.stack(
            [
                piece(query_weight, 0).T, key_value_piece[0], key_value_piece[1], piece(output_weight, 1)
            ]
        )
        pieces = [
            jnp.transpose(piece(gate_up_weight, 0), (1, 2, 0)), piece(down_weight, 1)[None]
        ]
        table_piece = bias_tables.astype(F32).reshape(-1)
        table_piece = jnp.pad(table_piece, (0, 8 * LANES - table_piece.shape[0])).reshape(8, LANES)
        w_first, slot_normed, tables = gather_first(
            mp_size, group, first_pieces, normed, table_piece
        )
        w_query, w_key, w_value, w_output = w_first
        tables = tables.reshape(mp_size, -1)[:, : bias_tables.size]
        tables = jnp.moveaxis(tables.reshape(mp_size, 3, 32, heads_here), 0, 2)
        tables = tables.reshape(3, 32, head_count)
    else:
        pieces = []
        w_query = gather_rows(query_weight.T, "mp")
        w_key = gather_rows(key_value_weight[:, 0].T, "mp")
        w_value = gather_rows(key_value_weight[:, 1].T, "mp")
        w_output = gather_rows(output_weight, "mp")
        w_gate = gather_rows(gate_up_weight[:, 0].T, "mp")
        w_up = gather_rows(gate_up_weight[:, 1].T, "mp")
        w_down = gather_rows(down_weight, "mp")
        tables = lax.all_gather(bias_tables, "mp", axis=2, tiled=True).astype(F32)
        slot_normed = lax.all_gather(normed, "mp", axis=0, tiled=True, axis_index_groups=groups)

    onehot_line = line_onehot(first_row, width, key_blocks)
    line = jnp.dot(onehot_line, tables[0], precision=lax.Precision.HIGHEST)
    line = line.T.reshape(head_count, 1, width)
    onehot_bin = bin_onehot()
    x_part = jnp.einsum("ban,nh->hba", onehot_bin, tables[1], precision=lax.Precision.HIGHEST)
    y_part = jnp.einsum("ban,nh->hba", onehot_bin, tables[2], precision=lax.Precision.HIGHEST)
    empty = jnp.zeros_like(x_part)
    layout = jnp.concatenate(
        [jnp.concatenate([x_part, empty], axis=2), jnp.concatenate([empty, y_part], axis=2)], axis=1
    ).astype(BF16)
    key_bins = lax.dynamic_slice(box_bins, (0, doc * slot_span), (2, slot_span))
    own_bins = lax.dynamic_slice(key_bins, (0, first_row), (2, rows))
    bin_ids = jnp.arange(NBIN, dtype=jnp.int32)

    def placed_rows(bins):
        return jnp.concatenate(
            [bins[0][:, None] == bin_ids, bins[1][:, None] == bin_ids], axis=1
        ).astype(BF16)

    def placed_lanes(bins):
        return jnp.concatenate(
            [bin_ids[:, None] == bins[0][None], bin_ids[:, None] == bins[1][None]], axis=0
        ).astype(BF16)

    length = lax.dynamic_index_in_dim(doc_lengths, doc, keepdims=False)
    masked = jnp.arange(slot_span, dtype=jnp.int32)[:, None] >= length
    key_placed = placed_rows(key_bins)
    key_extra = jnp.concatenate(
        [
            jnp.zeros((slot_span, 64), BF16),
            key_placed,
            jnp.where(masked, NEG_FILL, 0.0).astype(BF16),
            jnp.ones((slot_span, 3), BF16),
            jnp.zeros((slot_span, 60), BF16),
        ],
        axis=1,
    )
    key_extra_t = placed_lanes(key_bins)
    query_bins_t = placed_rows(own_bins)
    query_bins = placed_lanes(own_bins)

    queries = dot_f32(w_query, normed, 1, 1).astype(BF16)
    keys_t = dot_f32(w_key, slot_normed, 1, 1).astype(BF16)
    values_t = dot_f32(w_value, slot_normed, 1, 1).astype(BF16)
    heads_out, lse, *gathered = attend(
        mp_size, pieces, queries, keys_t, values_t, layout, line, key_extra, query_bins
    )
    if custom:
        (w_gate, w_up), (w_down,) = gathered
    residual = layer_input + dot_f32(heads_out, w_output, 0, 0)
    scale_second = inverse_rms(residual)
    normed_second = (residual * scale_second * gain_second).astype(BF16)
    gate = dot_f32(normed_second, w_gate, 1, 1)
    up = dot_f32(normed_second, w_up, 1, 1)
    gelu_value, gelu_pull = jax.vjp(lambda v: jax.nn.gelu(v, approximate=True), gate)
    activated = (gelu_value * up).astype(BF16)
    layer_output = residual + dot_f32(activated, w_down, 1, 0)

    def by_owner(values):
        if not custom:
            return values
        parts = values.reshape(-1, 4, 2, LANES)
        return jnp.swapaxes(parts, 1, 2).reshape(values.shape)

    out_low = cotangent.astype(BF16)
    down_full = dot_f32(activated, by_owner(out_low), 0, 0).astype(BF16)
    act_grad = dot_f32(out_low, w_down, 1, 1)
    gate_low = gelu_pull(act_grad * up)[0].astype(BF16)
    up_low = (act_grad * gelu_value).astype(BF16)
    second_by_owner = by_owner(normed_second)
    gate_full = dot_f32(gate_low, second_by_owner, 0, 0).astype(BF16)
    up_full = dot_f32(up_low, second_by_owner, 0, 0).astype(BF16)
    second_grad = dot_f32(gate_low, w_gate, 1, 0) + dot_f32(up_low, w_up, 1, 0)
    gain_second_grad = jnp.sum(second_grad * residual * scale_second, axis=0)
    scaled = gain_second * second_grad
    residual_grad = (
        cotangent
        + scale_second * scaled
        - residual * scale_second**3 * jnp.mean(scaled * residual, axis=-1, keepdims=True)
    )

    branch_low = residual_grad.astype(BF16)
    output_full = dot_f32(heads_out, by_owner(branch_low), 1, 0).astype(BF16)
    heads_grad = dot_f32(w_output, branch_low, 1, 1).astype(BF16)
    fulls = [jnp.stack([gate_full, up_full]), down_full[None]] if custom else []
    dq, dk, dv, line_grad, layout_grad, *scattered = attend_back(
        mp_size, fulls, queries, keys_t, values_t, heads_out, heads_grad, lse, layout, line,
        key_extra, key_extra_t, query_bins, query_bins_t,
    )
    slot_by_owner = by_owner(slot_normed)
    query_full = dot_f32(dq, by_owner(normed), 1, 0).astype(BF16)
    key_full = dot_f32(dk, slot_by_owner, 1, 0).astype(BF16)
    value_full = dot_f32(dv, slot_by_owner, 1, 0).astype(BF16)
    slot_grad = dot_f32(dk, w_key, 0, 0) + dot_f32(dv, w_value, 0, 0)
    query_part = dot_f32(dq, w_query, 0, 0)

    line_part = jnp.dot(onehot_line.T, line_grad[:, 0].T, precision=lax.Precision.HIGHEST)
    x_part = jnp.einsum(
        "ban,hba->nh", onehot_bin, layout_grad[:, :64, :64], precision=lax.Precision.HIGHEST
    )
    y_part = jnp.einsum(
        "ban,hba->nh", onehot_bin, layout_grad[:, 64:, 64:], precision=lax.Precision.HIGHEST
    )
    table_full = jnp.stack([line_part, x_part, y_part])

    if custom:
        own_grad = query_part + lax.dynamic_slice_in_dim(slot_grad, first_row, rows, 0)
        first_full = jnp.stack([query_full, key_full, value_full, output_full])
        small = jnp.concatenate([gain_second_grad, table_full.reshape(-1)])
        small_rows = small.shape[0] // LANES
        small = jnp.pad(small.reshape(small_rows, LANES), ((0, -small_rows % 8), (0, 0)))
        summed, input_grad, small = last_step(
            mp_size, group, first_full, slot_grad.astype(BF16), own_grad, layer_input,
            residual_grad, norm_gains.astype(F32), small,
        )
        small = small.reshape(-1)
        gains = small[: 2 * model_width].reshape(2, model_width)
        share = model_width // (dp_size * mp_size)
        at = (dp_index * mp_size + mp_index) * share
        gain_grad = lax.dynamic_slice(gains, (0, at), (2, share))
        table = small[2 * model_width : 2 * model_width + 3 * 32 * head_count]
        table_grad = lax.dynamic_slice(
            table.reshape(3, 32, head_count),
            (0, dp_index * (32 // dp_size), mp_index * heads_here),
            (3, 32 // dp_size, heads_here),
        )
        (gate_up_sum, (down_grad,)) = scattered
        query_grad = summed[0].T
        key_value_grad = jnp.transpose(summed[1:3], (2, 0, 1))
        output_grad = summed[3]
        gate_up_grad = jnp.transpose(gate_up_sum, (2, 0, 1))
    else:
        first_grad = query_part + lax.psum_scatter(
            slot_grad.astype(BF16), "mp", scatter_dimension=0, tiled=True, axis_index_groups=groups
        ).astype(F32)
        gain_first_grad = jnp.sum(first_grad * layer_input * scale_first, axis=0)
        scaled = gain_first * first_grad
        input_grad = (
            residual_grad
            + scale_first * scaled
            - layer_input * scale_first**3 * jnp.mean(scaled * layer_input, axis=-1, keepdims=True)
        )
        gain_grad = lax.psum_scatter(
            jnp.stack([gain_first_grad, gain_second_grad]), ("dp", "mp"), scatter_dimension=1,
            tiled=True,
        )
        table_grad = lax.psum_scatter(
            lax.psum_scatter(table_full, "mp", scatter_dimension=2, tiled=True),
            "dp", scatter_dimension=1, tiled=True,
        )
        query_grad = scatter_grad(query_full).T.astype(F32)
        key_value_grad = jnp.stack(
            [scatter_grad(key_full).T, scatter_grad(value_full).T], axis=1
        ).astype(F32)
        output_grad = scatter_grad(output_full).astype(F32)
        gate_up_grad = jnp.stack(
            [scatter_grad(gate_full).T, scatter_grad(up_full).T], axis=1
        ).astype(F32)
        down_grad = scatter_grad(down_full).astype(F32)
    return (
        layer_output, input_grad, gain_grad, query_grad, key_value_grad,
        output_grad, gate_up_grad, down_grad, table_grad,
    )


def solution(mesh):
    return jax.shard_map(
        partial(per_device, mesh.shape["dp"], mesh.shape["mp"]),
        mesh=mesh,
        in_specs=(
            P(("dp", "mp"), None),
            P(),
            P(None, "mp"),
            P(None, None, "mp"),
            P("mp", None),
            P(None, None, "mp"),
            P("mp", None),
            P(None, None, "mp"),
            P("dp"),
            P(None, "dp"),
            P(("dp", "mp"), None),
        ),
        out_specs=(
            P(("dp", "mp"), None),
            P(("dp", "mp"), None),
            P(None, ("dp", "mp")),
            P("dp", "mp"),
            P("dp", None, "mp"),
            P("mp", "dp"),
            P("dp", None, "mp"),
            P("mp", "dp"),
            P(None, "dp", "mp"),
        ),
        check_vma=False,
    )
```

time: 1220 us -> 510 us (0.42)
  waiting for transfers between devices: 618 us -> 0 us
  Pallas kernels: 0 us -> 342 us
  local copies, waits for them, and re-layouts: 297 us -> 44.7 us
  matrix products: 201 us -> 89.2 us
  other arithmetic: 71.4 us -> 25.1 us
  between operations: 16 us -> 1.94 us
  blocking collectives: 13.4 us -> 0 us
    pallas_call x0 -> x4, Pallas kernels: none -> 342 us  [the longest x1 112 us: attend_back(): pl.pallas_call(partial(attend_back_scatter_kernel, mp_size, head_count, l...]
    reduce_scatter x4 -> x0, waiting for transfers between devices: 324 us -> none  [the longest x1 114 us: per_device(): lax.psum_scatter(jnp.dot(heads_out, output_weight, preferred_element_type...]
    all_gather x4 -> x0, waiting for transfers between devices: 163 us -> none  [the longest x1 61.6 us: per_device(): full_second = lax.all_gather(normed_second, 'mp', axis=0, tiled=True)]
    unnamed x20 -> x0, waiting for transfers between devices: 131 us -> none
    unnamed x70 -> x108, local copies, waits for them, and re-layouts: 148 us -> 21.1 us
    dot_general x40 -> x27, matrix products: 201 us -> 89.2 us  [the longest x21 82.2 us: dot_f32(): lax.dot_general(left, right, (((left_dim,), (right_dim,)), ((), ())), pre...]
    reshape x4 -> x14, local copies, waits for them, and re-layouts: 59.8 us -> 8.86 us  [the longest x8 7.67 us: by_owner(): parts = values.reshape(-1, 4, 2, LANES)]
    pad x3 -> x1, local copies, waits for them, and re-layouts: 30 us -> 0.01 us  [per_device(): jnp.pad(small.reshape(small_rows, LANES), ((0, -small_rows % 8), (0, 0)))]
  transfers between devices with their start and end apart: 14 -> 0, of which waited for: 8 -> 0; matrix products, arithmetic and copies ran while one was open for 36% -> 0% of each run, Pallas kernels for 0% -> 0%
where the time goes in v1:
time: 510 us; the launch traced here: 503 us
  Pallas kernels  342 us (67%)
  matrix products  89.2 us (17%)
  local copies, waits for them, and re-layouts  44.7 us (9%)
  other arithmetic  25.1 us (5%)
    pallas_call x1, Pallas kernels, attend_back(): pl.pallas_call(partial(attend_back_scatter_kernel, mp_size, head_count, l...  112 us
    pallas_call x1, Pallas kernels, attend(): pl.pallas_call(partial(attend_gather_kernel, mp_size, head_count, len(pie...  94.1 us
    dot_general x21, matrix products, dot_f32(): lax.dot_general(left, right, (((left_dim,), (right_dim,)), ((), ())), pre...  82.2 us
    pallas_call x1, Pallas kernels, gather_first(): pl.pallas_call(partial(gather_first_kernel, mp_size, group), out_shape=(j...  73.9 us
    pallas_call x1, Pallas kernels, last_step(): pl.pallas_call(partial(last_kernel, mp_size, group), out_shape=(jax.Shape...  62.2 us
    unnamed x108, local copies, waits for them, and re-layouts  21.1 us

profile of v1, /device:TPU:0, one launch (start us, length us, event | category | flops | bytes accessed | tf_op | source)
XLA Modules:
  0.0 503.2 jit_solution(4337928551070582314)
XLA Ops:
  0.7 0.9 slice_convert_fusion
  1.5 1.7 multiply_reduce_fusion.3
  3.3 1.1 multiply_convert_fusion.3.refs_1_
  4.4 0.8 dynamic-slice_bitcast_fusion.2
  5.2 1.0 constant_dynamic-slice_fusion.3
  6.4 0.9 constant_dynamic-slice_fusion.4
  8.9 73.9 %gather_first.1 = (bf16[4,1024,1024]{2,1,0:T(8,128)(2,1)}, bf16[768,1024]{1,0:T(8,128)(2,1)}, f32[4,8,128]{2,1,0:T(8,128)}) custom-call(bf16[4,256,128]{2,1,0:T(8,128)(2,1)} %pad_maximum_fusion.2.refs_0_, bf16[384,1024]{1,0:T(8,128)(2,1)} %multiply_convert_fusion.3.refs_1_, f32[8,128]{1,0:T(8,128)} %bitcast_convert_fusion.refs_2_), custom_call_target="tpu_custom_call" | custom-call | tf_op jit(solution)/shard_map/gather_first/pallas_call | solution.py:730
  82.9 4.1 fusion.70.refs_0_
  86.9 4.6 fusion.53.refs_1_
  91.5 4.6 fusion.56.refs_2_
  96.4 1.9 fusion.104
  98.3 0.8 copy.88
  99.2 1.9 fusion.103
  101.1 1.1 fusion.79.refs_3_.refs_6_
  104.0 0.9 add_convert_fusion
  105.4 1.4 select_convert_fusion
  108.9 2.6 concatenate.32.refs_5_.refs_8_
  111.8 0.9 dynamic-slice_bitcast_fusion.1.refs_8_
  112.8 1.4 copy-done.2
  114.2 1.4 copy-done.3
  115.6 1.0 copy-done.5
  116.6 1.1 copy-done.6
  117.7 0.9 copy-done.10
  118.6 94.1 %attend.1 = (bf16[1024,384]{1,0:T(8,128)(2,1)S(1)}, f32[16,1,384]{2,1,0:T(1,128)S(1)}, bf16[2,2816,1024]{2,1,0:T(8,128)(2,1)}, bf16[1,2816,1024]{2,1,0:T(8,128)(2,1)S(1)}) custom-call(bf16[1024,384]{1,0:T(8,128)(2,1)S(1)} %copy-done.6, bf16[1024,768]{1,0:T(8,128)(2,1)S(1)} %copy-done.2, bf16[1024,768]{1,0:T(8,128)(2,1)S(1)} %copy-done.3, ...), custom_call_target="tpu_custom_call" | custom-call | tf_op jit(solution)/shard_map/attend/pallas_call | solution.py:553
  212.8 2.5 copy-done.13
  215.3 3.7 multiply_reduce_fusion.2
  219.0 1.8 copy.60
  220.8 7.4 %fusion.16 = f32[384,2816]{1,0:T(8,128)} fusion(bf16[384,1024]{0,1:T(8,128)(2,1)S(1)} %copy.60, bf16[1,2816,1024]{2,1,0:T(8,128)(2,1)} %copy-done.13), kind=kOutput, calls=%fused_computation.23 | convolution fusion | flops 2214592512 | bytes 10878976 | tf_op jit(solution)/shard_map/dot_general | solution.py:35
  228.5 2.4 fusion.6
  231.0 9.6 %fusion.25 = (bf16[384,2816]{1,0:T(8,128)(2,1)}, bf16[384,2816]{1,0:T(8,128)(2,1)}, bf16[384,2816]{1,0:T(8,128)(2,1)}) fusion(f32[384,2816]{1,0:T(8,128)} %fusion.16, f32[384,2816]{1,0:T(8,128)S(1)} %fusion.6, bf16[384,1024]{1,0:T(8,128)(2,1)S(1)} %multiply_convert_fusion.2, bf16[2,2816,1024]{2,1,0:T(8,128)(2,1)S(1)} %bitcast.206), kind=kOutput, calls=%fused_computation.30 | convolution fusion | flops 2242707456 | bytes 21692416 | tf_op jit(solution)/shard_map/dot_general | solution.py:35
  240.6 5.3 %fusion.67 = f32[384,1024]{1,0:T(8,128)} fusion(f32[384,1024]{1,0:T(8,128)S(1)} %copy-done.19, bf16[384,2816]{1,0:T(8,128)(2,1)} %get-tuple-element.80, bf16[1,2816,1024]{2,1,0:T(8,128)(2,1)S(1)} %bitcast.182), kind=kOutput, calls=%fused_computation.75 | convolution fusion | flops 2214985728 | bytes 11075584 | tf_op jit(solution)/shard_map/dot_general | solution.py:35
  245.9 2.4 fusion.4
  248.3 2.7 multiply_reduce_fusion
  251.0 1.7 fusion.99
  253.3 1.8 copy.66
  255.1 3.7 convert_bitcast_fusion.3
  258.8 3.8 fusion.73.refs_4_
  263.6 0.8 add_convert_fusion.3.refs_11_
  265.7 5.2 %convert_bitcast_fusion.1 = bf16[1,2816,1024]{2,1,0:T(8,128)(2,1)S(1)} fusion(bf16[384,2816]{1,0:T(8,128)(2,1)} %get-tuple-element.79, bf16[384,1024]{0,1:T(8,128)(2,1)S(1)} %bitcast.186), kind=kOutput, calls=%fused_computation.17 | convolution fusion | flops 2217476096 | bytes 8716288 | tf_op jit(solution)/shard_map/dot_general | solution.py:35
  270.9 3.7 convert_bitcast_fusion.2
  274.6 5.1 %pad_maximum_fusion.refs_12_ = bf16[2,2816,1024]{2,1,0:T(8,128)(2,1)} fusion(bf16[1,2816,1024]{2,1,0:T(8,128)(2,1)S(1)} %convert_bitcast_fusion.1, bf16[1,2816,1024]{2,1,0:T(8,128)(2,1)S(1)} %convert_bitcast_fusion.2), kind=kLoop, calls=%fused_computation | loop fusion | flops 5767168 | bytes 23068672 | tf_op jit(solution)/shard_map/stack | solution.py:1025
  279.8 5.2 %convert_bitcast_fusion.refs_13_ = bf16[1,2816,1024]{2,1,0:T(8,128)(2,1)} fusion(bf16[384,2816]{1,0:T(8,128)(2,1)S(1)} %copy-done.38, bf16[384,1024]{0,1:T(8,128)(2,1)S(1)} %bitcast.188), kind=kOutput, calls=%fused_computation.16 | convolution fusion | flops 2217476096 | bytes 8716288 | tf_op jit(solution)/shard_map/dot_general | solution.py:35
  284.9 112.0 %attend_back.1 = (bf16[1024,384]{1,0:T(8,128)(2,1)}, bf16[1024,768]{1,0:T(8,128)(2,1)}, bf16[1024,768]{1,0:T(8,128)(2,1)}, f32[16,1,1152]{2,1,0:T(1,128)}, f32[1...) custom-call(bf16[1024,384]{1,0:T(8,128)(2,1)} %fusion.70.refs_0_, ...), custom_call_target="tpu_custom_call" | custom-call | tf_op jit(solution)/shard_map/attend_back/pallas_call | solution.py:596
  396.9 1.1 reshape.187
  398.1 1.6 copy.65
  399.6 4.7 convert_bitcast_fusion.4
  404.3 3.2 convert_bitcast_fusion.5
  408.8 1.3 convert_bitcast_fusion.6
  410.4 7.7 %pad_maximum_fusion.1.refs_0_ = bf16[4,1024,1024]{2,1,0:T(8,128)(2,1)} fusion(bf16[1,1024,1024]{2,1,0:T(8,128)(2,1)S(1)} %copy-done.22, bf16[1,1024,1024]{2,1,0:T(8,128)(2,1)} %convert_bitcast_fusion.4, bf16[1,1024,1024]{2,1,0:T(8,128)(2,1)} %convert_bitcast_fusion.5, bf16[1,1024,1024]{2,1,0:T(8,128)(2,1)S(1)} %convert_bitcast_fusion.6), kind=kLoop, calls=%fused_computation.1 | loop fusion | flops 12582912 | bytes 16777216 | tf_op jit(solution)/shard_map/stack | solution.py:1048
  418.2 1.9 fusion.30
  420.1 1.9 fusion.102
  422.0 1.0 dynamic-slice_add_fusion.refs_2_
  423.4 0.9 copy-done.14
  424.3 1.2 convolution_bitcast_fusion
  425.4 1.2 convolution_bitcast_fusion.1
  427.2 62.2 %last_step.1 = (f32[4,256,128]{2,1,0:T(8,128)S(1)}, f32[384,1024]{1,0:T(8,128)S(1)}, f32[32,128]{1,0:T(8,128)S(1)}) custom-call(bf16[4,1024,1024]{2,1,0:T(8,128)(2,1)} %pad_maximum_fusion.1.refs_0_, bf16[768,1024]{1,0:T(8,128)(2,1)S(1)} %get-tuple-element.95.refs_1_, f32[384,1024]{1,0:T(8,128)S(1)} %dynamic-slice_add_fusion.refs_2_, f32[384,1024]{1,0:T(8,128)} %refs_3_.1, ...), custom_call_target="tpu_custom_call" | custom-call | tf_op jit(solution)/shard_map/last_step/pallas_call | solution.py:833
  489.5 1.2 copy-done.7
  490.7 0.8 copy-done.11
  492.1 1.6 slice_bitcast_fusion.1
  493.7 0.8 copy.70
  494.5 1.0 slice_bitcast_fusion
  495.5 0.8 copy.71
  497.1 2.9 copy.94
  500.0 2.0 copy.95
  (147 shorter events, 14.9 us)
Async XLA Ops:
  0.6 111.0 %copy-start = (bf16[1024,2,704]{0,2,1:T(8,128)(2,1)S(1)}, bf16[1024,2,704]{0,2,1:T(8,128)(2,1)}, u32[]{:S(2)}) copy-start(bf16[1024,2,704]{0,2,1:T(8,128)(2,1)} %param.17) | copy-start | bytes 8650756
  0.7 2.6 copy-start.15
  3.3 4.8 copy-start.30
  82.9 4.1 copy-start.23
  91.5 4.6 copy-start.28
  98.3 5.3 %copy-start.29 = (s32[2,1536]{1,0:T(2,128)S(1)}, s32[2,1536]{1,0:T(2,128)}, u32[]{:S(2)}) copy-start(s32[2,1536]{1,0:T(2,128)} %param.21) | copy-start | bytes 36868
  98.3 6.5 %copy-start.37 = (s32[2]{0:T(128)S(1)}, s32[2]{0:T(128)}, u32[]{:S(2)}) copy-start(s32[2]{0:T(128)} %param.20) | copy-start | bytes 28
  102.3 10.5 %copy-start.4 = (bf16[16,128,128]{2,1,0:T(8,128)(2,1)}, bf16[16,128,128]{2,1,0:T(8,128)(2,1)S(1)}, u32[]{:S(2)}) copy-start(bf16[16,128,128]{2,1,0:T(8,128)(2,1)S(1)} %fusion.79.refs_3_.refs_6_) | copy-start | bytes 1572868
  111.7 101.1 %copy-start.8 = (bf16[128,384]{1,0:T(8,128)(2,1)}, bf16[128,384]{1,0:T(8,128)(2,1)S(1)}, u32[]{:S(2)}) copy-start(bf16[128,384]{1,0:T(8,128)(2,1)S(1)} %add_convert_fusion.2.refs_6_.refs_10_) | copy-start | bytes 294916
  112.8 1.4 copy-start.2
  114.2 1.4 copy-start.3
  115.6 1.0 copy-start.5
  116.6 1.1 copy-start.6
  117.7 0.9 copy-start.10
  118.6 96.7 %copy-start.16 = (f32[384,1024]{1,0:T(8,128)S(1)}, f32[384,1024]{1,0:T(8,128)}, u32[]{:S(2)}) copy-start(f32[384,1024]{1,0:T(8,128)} %refs_3_.1) | copy-start | bytes 4718596
  212.8 2.5 copy-start.13
  212.8 6.2 %copy-start.12 = (f32[16,1,384]{2,1,0:T(1,128)}, f32[16,1,384]{2,1,0:T(1,128)S(1)}, u32[]{:S(2)}) copy-start(f32[16,1,384]{2,1,0:T(1,128)S(1)} %get-tuple-element.32.refs_5_) | copy-start | bytes 73732
  212.8 42.3 %copy-start.9 = (bf16[1024,384]{1,0:T(8,128)(2,1)}, bf16[1024,384]{1,0:T(8,128)(2,1)S(1)}, u32[]{:S(2)}) copy-start(bf16[1024,384]{1,0:T(8,128)(2,1)S(1)} %get-tuple-element.29.refs_3_) | copy-start | bytes 2359300
  220.8 7.7 %slice-start.2 = ((s8[11534336]{0:T(1024)(128)(4,1)}), s8[4194304]{0:T(1024)(128)(4,1)S(1)}, s32[]{:S(2)}) async-start(s8[11534336]{0:T(1024)(128)(4,1)} %bitcast.205), calls=%async_computation.2 | async-start | bytes 8388608
  220.8 7.4 %copy-start.19 = (f32[384,1024]{1,0:T(8,128)S(1)}, f32[384,1024]{1,0:T(8,128)}, u32[]{:S(2)}) copy-start(f32[384,1024]{1,0:T(8,128)} %get-tuple-element.93) | copy-start | bytes 4718596
  220.8 7.7 %slice-start.3 = ((s8[11534336]{0:T(1024)(128)(4,1)}), s8[4194304]{0:T(1024)(128)(4,1)S(1)}, s32[]{:S(2)}) async-start(s8[11534336]{0:T(1024)(128)(4,1)} %bitcast.205), calls=%async_computation.3 | async-start | bytes 8388608
  220.8 7.7 %slice-start.4 = ((s8[11534336]{0:T(1024)(128)(4,1)}), s8[3145728]{0:T(1024)(128)(4,1)S(1)}, s32[]{:S(2)}) async-start(s8[11534336]{0:T(1024)(128)(4,1)} %bitcast.205), calls=%async_computation.4 | async-start | bytes 6291456
  228.4 2.5 copy-start.20
  228.5 12.1 %slice-start = ((s8[5767168]{0:T(1024)(128)(4,1)}), s8[4194304]{0:T(1024)(128)(4,1)S(1)}, s32[]{:S(2)}) async-start(s8[5767168]{0:T(1024)(128)(4,1)} %bitcast.181), calls=%async_computation | async-start | bytes 8388608
  230.9 9.6 %slice-start.1 = ((s8[5767168]{0:T(1024)(128)(4,1)}), s8[1572864]{0:T(1024)(128)(4,1)S(1)}, s32[]{:S(2)}) async-start(s8[5767168]{0:T(1024)(128)(4,1)} %bitcast.181), calls=%async_computation.1 | async-start | bytes 3145728
  240.6 5.3 %copy-start.41 = (bf16[384,2816]{1,0:T(8,128)(2,1)S(1)}, bf16[384,2816]{1,0:T(8,128)(2,1)}, u32[]{:S(2)}) copy-start(bf16[384,2816]{1,0:T(8,128)(2,1)} %get-tuple-element.79) | copy-start | bytes 6488068
  245.9 2.4 copy-start.39
  248.3 2.7 copy-start.18
  258.8 5.5 %copy-start.21 = (bf16[384,1024]{1,0:T(8,128)(2,1)S(1)}, bf16[384,1024]{1,0:T(8,128)(2,1)}, u32[]{:S(2)}) copy-start(bf16[384,1024]{1,0:T(8,128)(2,1)} %copy-done.20) | copy-start | bytes 2359300
  265.7 5.2 %copy-start.40 = (bf16[384,2816]{1,0:T(8,128)(2,1)S(1)}, bf16[384,2816]{1,0:T(8,128)(2,1)}, u32[]{:S(2)}) copy-start(bf16[384,2816]{1,0:T(8,128)(2,1)} %get-tuple-element.78) | copy-start | bytes 6488068
  274.6 5.2 %copy-start.38 = (bf16[384,2816]{1,0:T(8,128)(2,1)S(1)}, bf16[384,2816]{1,0:T(8,128)(2,1)}, u32[]{:S(2)}) copy-start(bf16[384,2816]{1,0:T(8,128)(2,1)} %get-tuple-element.80) | copy-start | bytes 6488068
  284.9 112.0 %copy-start.24 = (bf16[768,1024]{1,0:T(8,128)(2,1)S(1)}, bf16[768,1024]{1,0:T(8,128)(2,1)}, u32[]{:S(2)}) copy-start(bf16[768,1024]{1,0:T(8,128)(2,1)} %get-tuple-element.27) | copy-start | bytes 4718596
  399.6 4.7 copy-start.31
  404.3 3.2 copy-start.17
  407.5 1.3 copy-start.34
  408.8 1.6 copy-start.22
  408.8 9.3 %slice-start.5 = ((s8[8388608]{0:T(1024)(128)(4,1)}), s8[4194304]{0:T(1024)(128)(4,1)S(1)}, s32[]{:S(2)}) async-start(s8[8388608]{0:T(1024)(128)(4,1)} %bitcast.207), calls=%async_computation.5 | async-start | bytes 8388608
  410.4 7.8 %slice-start.6 = ((s8[8388608]{0:T(1024)(128)(4,1)}), s8[4194304]{0:T(1024)(128)(4,1)S(1)}, s32[]{:S(2)}) async-start(s8[8388608]{0:T(1024)(128)(4,1)} %bitcast.207), calls=%async_computation.6 | async-start | bytes 8388608
  410.4 7.8 %copy-start.33 = (bf16[1024,768]{1,0:T(8,128)(2,1)S(1)}, bf16[1024,768]{1,0:T(8,128)(2,1)}, u32[]{:S(2)}) copy-start(bf16[1024,768]{1,0:T(8,128)(2,1)} %get-tuple-element.35) | copy-start | bytes 4718596
  418.2 1.9 copy-start.32
  420.1 1.9 copy-start.35
  422.0 1.1 copy-start.27
  422.0 1.2 copy-start.25
  423.0 1.3 copy-start.14
  423.2 3.4 copy-start.36
  489.5 1.2 copy-start.7
  490.6 0.8 copy-start.11
  496.4 6.4 %copy-start.1 = (bf16[1024,2,704]{0,2,1:T(8,128)(2,1)S(1)}, bf16[1024,2,704]{0,2,1:T(8,128)(2,1)}, u32[]{:S(2)}) copy-start(bf16[1024,2,704]{0,2,1:T(8,128)(2,1)} %param.17) | copy-start | bytes 8650756
  497.1 4.9 copy-start.26

commit v2 on v1

v2 whole, which is shorter than its diff:
```python
from functools import partial

import jax
import jax.numpy as jnp
import numpy as np
from jax import lax
from jax.experimental import pallas as pl
from jax.experimental.pallas import tpu as pltpu
from jax.sharding import PartitionSpec as P

NBIN = 64
EPSILON = 1e-06
THRESHOLDS = (8, 12, 16, 23, 32, 46, 64, 91)
NEG_FILL = -1e30
LANES = 128
MESH = pl.DeviceIdType.MESH
HBM = pltpu.MemorySpace.HBM
BF16 = jnp.bfloat16
F32 = jnp.float32


def bucket_of(relative):
    distance = jnp.abs(relative)
    bucket = jnp.minimum(distance, 7)
    for threshold in THRESHOLDS:
        bucket = bucket + (distance >= threshold).astype(jnp.int32)
    return bucket + 16 * (relative > 0).astype(jnp.int32)


def inverse_rms(values):
    return lax.rsqrt(jnp.mean(values * values, axis=-1, keepdims=True) + EPSILON)


def dot_f32(left, right, left_dim, right_dim):
    return lax.dot_general(
        left, right, (((left_dim,), (right_dim,)), ((), ())), preferred_element_type=F32
    )


def three_parts(values):
    high = values.astype(BF16)
    rest = values - high.astype(F32)
    middle = rest.astype(BF16)
    low = (rest - middle.astype(F32)).astype(BF16)
    return high, middle, low


def lane_ids(shape):
    return lax.broadcasted_iota(jnp.int32, shape, 1)


def row_ids(shape):
    return lax.broadcasted_iota(jnp.int32, shape, 0)


def attend_kernel(
    q_ref, k_ref, v_ref, layout_ref, line_ref, key_extra_ref, query_bins_ref,
    out_ref, lse_ref,
    key_aug, query_aug, strip, scores, probs,
):
    head_size, rows = q_ref.shape
    keys = k_ref.shape[1]
    blocks = keys // LANES
    width = strip.shape[1]

    @pl.when(pl.program_id(0) == 0)
    def _():
        key_aug[...] = key_extra_ref[...]
        tail = row_ids((64, rows))
        query_aug[pl.ds(192, 64), :] = jnp.where(tail == 0, 1.0, 0.0).astype(BF16)

    both = jnp.concatenate([k_ref[...], v_ref[...]], axis=0).T
    low_lanes = lane_ids((keys, LANES)) < head_size
    key_aug[:, 0:LANES] = jnp.where(low_lanes, both, key_extra_ref[:, 0:LANES])
    query_aug[pl.ds(0, 64), :] = q_ref[...]
    query_aug[pl.ds(64, 128), :] = jnp.dot(
        layout_ref[0], query_bins_ref[...], preferred_element_type=F32
    ).astype(BF16)
    strip[...] = pltpu.roll(
        jnp.broadcast_to(line_ref[0], (LANES, width)), 0, 1, stride=1, stride_axis=0
    )
    query_all = query_aug[...]
    top = jnp.full((1, rows), -jnp.inf, F32)
    for block in range(blocks):
        here = pl.ds(block * LANES, LANES)
        part = jnp.dot(key_aug[here, :], query_all, preferred_element_type=F32)
        part = part + strip[:, pl.ds((blocks - 1 - block) * LANES, rows)]
        scores[here, :] = part
        top = jnp.maximum(top, jnp.max(part, axis=0, keepdims=True))
    total = jnp.zeros((1, rows), F32)
    for block in range(blocks):
        here = pl.ds(block * LANES, LANES)
        part = jnp.exp(scores[here, :] - top)
        total = total + jnp.sum(part, axis=0, keepdims=True)
        probs[here, :] = part.astype(BF16)
    mixed = jnp.dot(v_ref[...], probs[...], preferred_element_type=F32)
    out_ref[...] = (mixed / total).astype(BF16)
    lse_ref[0] = top + jnp.log(total)


def attend_back_kernel(
    q_ref, k_ref, v_ref, out_ref, out_grad_ref, lse_ref, layout_ref, line_ref,
    key_extra_ref, key_extra_t_ref, query_bins_ref, query_bins_t_ref,
    dq_ref, dk_ref, dv_ref, line_grad_ref, layout_grad_ref,
    key_aug, key_aug_t, query_aug, value_aug, grad_aug, strip, strip_grad, probs_grad,
):
    head_size, rows = q_ref.shape
    keys = k_ref.shape[1]
    blocks = keys // LANES
    width = strip.shape[1]

    @pl.when(pl.program_id(0) == 0)
    def _():
        key_aug[...] = key_extra_ref[...]
        key_aug_t[pl.ds(64, 128), :] = key_extra_t_ref[...]
        tail = row_ids((64, rows))
        query_aug[pl.ds(192, 64), :] = jnp.where(tail == 0, 1.0, 0.0).astype(BF16)

    both = jnp.concatenate([k_ref[...], v_ref[...]], axis=0).T
    lanes = lane_ids((keys, LANES))
    key_aug[:, 0:LANES] = jnp.where(lanes < head_size, both, key_extra_ref[:, 0:LANES])
    ones = jnp.where(lanes < 3, 1.0, 0.0).astype(BF16)
    value_aug[...] = jnp.where(lanes < head_size, ones, both)
    key_aug_t[pl.ds(0, 64), :] = k_ref[...]
    query_aug[pl.ds(0, 64), :] = q_ref[...]
    query_aug[pl.ds(64, 128), :] = jnp.dot(
        layout_ref[0], query_bins_ref[...], preferred_element_type=F32
    ).astype(BF16)
    high, middle, low = three_parts(-lse_ref[0])
    tail = row_ids((64, rows))
    rows_of = lambda part: jnp.broadcast_to(part.astype(F32), (64, rows))
    query_aug[pl.ds(192, 64), :] = jnp.where(
        tail == 0, 1.0,
        jnp.where(
            tail == 1, rows_of(high),
            jnp.where(tail == 2, rows_of(middle), jnp.where(tail == 3, rows_of(low), 0.0)),
        ),
    ).astype(BF16)
    row_dot = jnp.sum(
        out_grad_ref[...].astype(F32) * out_ref[...].astype(F32), axis=0, keepdims=True
    )
    high, middle, low = three_parts(-row_dot)
    grad_aug[pl.ds(0, 64), :] = jnp.where(
        tail == 0, rows_of(high),
        jnp.where(tail == 1, rows_of(middle), jnp.where(tail == 2, rows_of(low), 0.0)),
    ).astype(BF16)
    grad_aug[pl.ds(64, 64), :] = out_grad_ref[...]
    strip[...] = pltpu.roll(
        jnp.broadcast_to(line_ref[0], (LANES, width)), 0, 1, stride=1, stride_axis=0
    )
    strip_grad[...] = jnp.zeros_like(strip_grad)
    query_and_grad = jnp.concatenate([q_ref[...], out_grad_ref[...]], axis=0).T
    query_all = query_aug[...]
    grad_all = grad_aug[...]
    half = lane_ids((LANES, LANES)) < head_size
    for block in range(blocks):
        here = pl.ds(block * LANES, LANES)
        band = pl.ds((blocks - 1 - block) * LANES, rows)
        part = jnp.dot(key_aug[here, :], query_all, preferred_element_type=F32)
        part = jnp.exp(part + strip[:, band])
        slope = part * jnp.dot(value_aug[here, :], grad_all, preferred_element_type=F32)
        strip_grad[:, band] = strip_grad[:, band] + slope
        slope = slope.astype(BF16)
        probs_grad[here, :] = slope
        key_part = jnp.dot(slope, query_and_grad, preferred_element_type=F32)
        value_part = jnp.dot(part.astype(BF16), query_and_grad, preferred_element_type=F32)
        turned = jnp.where(half, key_part, value_part).T.astype(BF16)
        dk_ref[:, here] = turned[0:64]
        dv_ref[:, here] = turned[64:128]
    query_part = jnp.dot(key_aug_t[...], probs_grad[...], preferred_element_type=F32)
    dq_ref[...] = query_part[0:64].astype(BF16)
    layout_grad_ref[0] = jnp.dot(
        query_part[64:192].astype(BF16), query_bins_t_ref[...], preferred_element_type=F32
    )
    folded = strip_grad[pl.ds(0, 8), :]
    for group in range(1, LANES // 8):
        folded = folded + pltpu.roll(strip_grad[pl.ds(group * 8, 8), :], width - group * 8, 1)
    line = folded[0:1]
    for row in range(1, 8):
        line = line + pltpu.roll(folded[row : row + 1], width - row, 1)
    line_grad_ref[0] = line


class Place:
    def __init__(self, mp_size):
        self.dp = lax.axis_index("dp")
        self.mp = lax.axis_index("mp")
        self.mp_size = mp_size
        self.core = lax.rem(self.dp, 2)
        self.x = lax.rem(lax.div(self.dp, 2), 2)
        self.y = lax.div(self.dp, 4)
        self.to_core = (self.dp + 1 - 2 * self.core, self.mp)
        self.to_x = (self.dp + 2 - 4 * self.x, self.mp)
        self.to_y = (self.dp + 4 - 8 * self.y, self.mp)

    def to_mp(self, step):
        return (self.dp, lax.rem(self.mp + step, self.mp_size))

    def from_mp(self, step):
        return lax.rem(self.mp + self.mp_size - step, self.mp_size)

    def partners(self):
        others = [self.to_mp(step) for step in range(1, self.mp_size)]
        return [self.to_core, self.to_x, self.to_y] + others


def meet(place):
    barrier = pltpu.get_barrier_semaphore()
    partners = place.partners()
    for partner in partners:
        pl.semaphore_signal(barrier, inc=1, device_id=partner, device_id_type=MESH)
    pl.semaphore_wait(barrier, len(partners))


class Copy:
    def __init__(self, source, target, send, receive=None, partner=None):
        self.parts = (source, target, send, receive, partner)

    def made(self):
        source, target, send, receive, partner = self.parts
        if partner is None:
            return pltpu.make_async_copy(source, target, send)
        return pltpu.make_async_remote_copy(
            src_ref=source, dst_ref=target, send_sem=send, recv_sem=receive,
            device_id=partner, device_id_type=MESH,
        )

    def start(self):
        self.made().start()

    def wait(self):
        self.made().wait()

    def wait_send(self):
        self.made().wait_send()

    def wait_recv(self):
        self.made().wait_recv()


def remote(source, target, send, receive, partner):
    return Copy(source, target, send, receive, partner)


def lanes_at(block, count):
    return pl.ds(pl.multiple_of(block * LANES, LANES), count * LANES)


class Gather:
    LAGS = 2

    def __init__(self, place, pieces, outs, sems, items=None):
        self.place, self.pieces, self.outs = place, pieces, outs
        self.z_send, self.z_recv, self.own_sem, self.send, self.recv = sems
        self.items = items or [(c, k) for c in range(len(pieces)) for k in range(place.mp_size)]
        self.steps = len(self.items) + self.LAGS

    @staticmethod
    def semaphores(count, mp_size):
        dma = pltpu.SemaphoreType.DMA
        items = count * mp_size
        return [
            dma((count, mp_size)), dma((count, mp_size)), dma((count,)), dma((items, 6)), dma((items, 6))
        ]

    def rows(self, c, source, half):
        n = self.pieces[c].shape[1]
        if half is None:
            return pl.ds(pl.multiple_of(source * n, 16), n)
        return pl.ds(pl.multiple_of(source * n + half * (n // 2), 16), n // 2)

    def window(self, c, source, half, block, count):
        return self.outs[c].at[:, self.rows(c, source, half), lanes_at(block, count)]

    def own(self, c):
        place = self.place
        block = place.core * 4 + place.y * 2 + place.x
        return Copy(
            self.pieces[c], self.window(c, place.mp, None, block, 1), self.own_sem.at[c]
        )

    def along_mp(self, c, step):
        place = self.place
        block = place.core * 4 + place.y * 2 + place.x
        return remote(
            self.pieces[c], self.window(c, place.mp, None, block, 1),
            self.z_send.at[c, step], self.z_recv.at[c, step], place.to_mp(step),
        )

    def start_chunk(self, c):
        self.own(c).start()
        for step in range(1, self.place.mp_size):
            self.along_mp(c, step).start()

    def copies(self, t):
        c, k = self.items[t]
        place = self.place
        source = place.from_mp(k)
        base = place.core * 4
        mine = base + place.y * 2 + place.x
        turned = base + (1 - place.y) * 2 + place.x

        def copy(i, half, block, count, partner):
            here = self.window(c, source, half, block, count)
            return remote(here, here, self.send.at[t, i], self.recv.at[t, i], partner)

        first = [copy(0, 0, mine, 1, place.to_x), copy(1, 1, mine, 1, place.to_y)]
        second = [
            copy(2, 0, base + place.y * 2, 2, place.to_y),
            copy(3, 1, mine, 1, place.to_x),
            copy(4, 1, turned, 1, place.to_x),
        ]
        third = [copy(5, None, base, 4, place.to_core)]
        return first, second, third

    def step(self, s):
        count = len(self.items)
        if 0 <= s - 2 < count:
            _, second, third = self.copies(s - 2)
            for copy in second:
                copy.wait_recv()
            third[0].start()
        if 0 <= s - 1 < count:
            first, second, _ = self.copies(s - 1)
            for copy in first:
                copy.wait_recv()
            for copy in second:
                copy.start()
        if s < count:
            c, k = self.items[s]
            if k == 0:
                self.own(c).wait()
            else:
                self.along_mp(c, k).wait_recv()
            for copy in self.copies(s)[0]:
                copy.start()

    def done(self, t):
        self.copies(t)[2][0].wait_recv()

    def close(self):
        for t, (c, k) in enumerate(self.items):
            first, second, third = self.copies(t)
            for copy in first + second + third:
                copy.wait_send()
            if k > 0:
                self.along_mp(c, k).wait_send()


def add_rows(target, target_index, source, source_index):
    lead, rows, lanes = target_index
    source_rows, source_lanes = source_index
    row_start, count = rows
    source_start = source_rows
    size = 32
    while count % size:
        size //= 2

    def body(i, carry):
        here = pl.ds(pl.multiple_of(row_start + i * size, size), size)
        there = pl.ds(pl.multiple_of(source_start + i * size, size), size)
        for part in range(lead):
            target[part, here, lanes] = target[part, here, lanes] + source[part, there, source_lanes]
        return carry

    lax.fori_loop(0, count // size, body, 0)


class Scatter:
    def __init__(self, place, fulls, outs, scratch, items):
        self.place, self.fulls, self.outs, self.items = place, fulls, outs, items
        count = len(fulls)
        self.whole = [len(full.shape) == 3 for full in fulls]
        buffers = [scratch[i * count : (i + 1) * count] for i in range(5)]
        self.sums, self.from_first, self.from_second, self.from_mp, self.staged = buffers
        self.own_sem, self.send, self.recv = scratch[5 * count :]
        self.steps = len(items) + 5

    @staticmethod
    def scratch(shapes, whole, mp_size):
        out = []
        for blocks in (4, 2, 1, 1):
            for lead, n in shapes:
                out.append(pltpu.VMEM((mp_size, lead, n, blocks * LANES), BF16))
        for (lead, n), is_whole in zip(shapes, whole):
            out.append(pltpu.VMEM((lead, n, 4 * LANES) if is_whole else (1, 8, LANES), BF16))
        dma = pltpu.SemaphoreType.DMA
        count = len(shapes) * mp_size
        return out + [dma((count,)), dma((count, 7)), dma((count, 7))]

    def size(self, c):
        return self.sums[c].shape[1], self.sums[c].shape[2]

    def source(self, t):
        c, k = self.items[t]
        if not self.whole[c]:
            return self.fulls[c].at[(k + self.place.mp_size - 1) % self.place.mp_size % 2]
        lead, n = self.size(c)
        target = lax.rem(self.place.mp + k, self.place.mp_size)
        return self.fulls[c].at[:, pl.ds(pl.multiple_of(target * n, 16), n), :]

    def from_core(self, t):
        c, k = self.items[t]
        place = self.place
        return remote(
            self.source(t).at[:, :, lanes_at((1 - place.core) * 4, 4)], self.sums[c].at[k],
            self.send.at[t, 0], self.recv.at[t, 0], place.to_core,
        )

    def own(self, t):
        c, _ = self.items[t]
        return Copy(
            self.source(t).at[:, :, lanes_at(self.place.core * 4, 4)], self.staged[c], self.own_sem.at[t]
        )

    def copies(self, t):
        c, k = self.items[t]
        place = self.place
        lead, n = self.size(c)
        top, bottom = pl.ds(0, n // 2), pl.ds(n // 2, n // 2)
        every = pl.ds(0, lead)
        sums = self.sums[c].at[k]

        def copy(i, source, landing, partner):
            return remote(source, landing, self.send.at[t, i], self.recv.at[t, i], partner)

        landing = self.from_first[c].at[k]
        first = [
            copy(
                1, sums.at[every, top, lanes_at((1 - place.y) * 2, 2)],
                landing.at[every, top, pl.ds(0, 256)], place.to_y,
            ),
            copy(
                2, sums.at[every, bottom, lanes_at(1 - place.x, 1)],
                landing.at[every, bottom, pl.ds(0, 128)], place.to_x,
            ),
            copy(
                3, sums.at[every, bottom, lanes_at(3 - place.x, 1)],
                landing.at[every, bottom, pl.ds(128, 128)], place.to_x,
            ),
        ]
        landing = self.from_second[c].at[k]
        second = [
            copy(
                4, sums.at[every, top, lanes_at(place.y * 2 + 1 - place.x, 1)],
                landing.at[every, top, pl.ds(0, 128)], place.to_x,
            ),
            copy(
                5, sums.at[every, bottom, lanes_at((1 - place.y) * 2 + place.x, 1)],
                landing.at[every, bottom, pl.ds(0, 128)], place.to_y,
            ),
        ]
        third = None
        if k > 0:
            third = copy(
                6, sums.at[:, :, lanes_at(place.y * 2 + place.x, 1)], self.from_mp[c].at[k],
                place.to_mp(k),
            )
        return first, second, third

    def step(self, s):
        count = len(self.items)
        place = self.place
        if s < count:
            self.from_core(s).start()
        if 0 <= s - 1 < count:
            t = s - 1
            c, k = self.items[t]
            lead, n = self.size(c)
            first, *_ = self.copies(t)
            self.from_core(t).wait_recv()
            if self.whole[c]:
                self.own(t).wait()
                add_rows(self.sums[c].at[k], (lead, (0, n), pl.ds(0, 512)), self.staged[c], (0, pl.ds(0, 512)))
            else:
                add_rows(
                    self.sums[c].at[k], (lead, (0, n), pl.ds(0, 512)),
                    self.source(t), (0, lanes_at(place.core * 4, 4)),
                )
            for copy in first:
                copy.start()
        if s < count and self.whole[self.items[s][0]]:
            self.own(s).start()
        if 0 <= s - 2 < count:
            t = s - 2
            c, k = self.items[t]
            lead, n = self.size(c)
            first, second, _ = self.copies(t)
            for copy in first:
                copy.wait_recv()
            sums, landing = self.sums[c].at[k], self.from_first[c].at[k]
            half = n // 2
            add_rows(sums, (lead, (0, half), lanes_at(place.y * 2, 2)), landing, (0, pl.ds(0, 256)))
            add_rows(sums, (lead, (half, half), lanes_at(place.x, 1)), landing, (half, pl.ds(0, 128)))
            add_rows(
                sums, (lead, (half, half), lanes_at(2 + place.x, 1)), landing, (half, pl.ds(128, 128))
            )
            for copy in second:
                copy.start()
        if 0 <= s - 3 < count:
            t = s - 3
            c, k = self.items[t]
            lead, n = self.size(c)
            _, second, third = self.copies(t)
            for copy in second:
                copy.wait_recv()
            sums, landing = self.sums[c].at[k], self.from_second[c].at[k]
            mine = lanes_at(place.y * 2 + place.x, 1)
            add_rows(sums, (lead, (0, n), mine), landing, (0, pl.ds(0, 128)))
            if third is not None:
                third.start()
        if 0 <= s - 5 < count:
            t = s - 5
            c, k = self.items[t]
            third = self.copies(t)[2]
            if third is not None:
                third.wait_recv()
            else:
                self.finish(c)

    def left(self, t):
        self.from_core(t).wait_send()

    def close(self):
        for t, (c, k) in enumerate(self.items):
            first, second, third = self.copies(t)
            if self.whole[c] or k in (0, self.place.mp_size - 1):
                self.from_core(t).wait_send()
            for copy in first + second:
                copy.wait_send()
            if third is not None:
                third.wait_send()

    def finish(self, c):
        place = self.place
        lead, n = self.size(c)
        mine = lanes_at(place.y * 2 + place.x, 1)
        sums, landing, out = self.sums[c], self.from_mp[c], self.outs[c]
        size = 32
        while n % size:
            size //= 2

        def body(i, carry):
            here = pl.ds(pl.multiple_of(i * size, size), size)
            for part in range(lead):
                total = sums[0, part, here, mine].astype(F32)
                for k in range(1, place.mp_size):
                    total = total + landing[k, part, here, :].astype(F32)
                out[part, here, :] = total
            return carry

        lax.fori_loop(0, n // size, body, 0)


def attention_shapes(head_count, head_size, rows, keys, width):
    whole = lambda shape: pl.BlockSpec(shape, lambda head: (0,) * len(shape))
    column = lambda size: pl.BlockSpec((head_size, size), lambda head: (head, 0))
    page = lambda a, b: pl.BlockSpec((1, a, b), lambda head: (head, 0, 0))
    return whole, column, page


def attend(queries, keys_t, values_t, layout, line, key_extra, query_bins):
    inner, rows = queries.shape
    keys = keys_t.shape[1]
    head_count, _, width = line.shape
    head_size = inner // head_count
    whole, column, page = attention_shapes(head_count, head_size, rows, keys, width)
    return pl.pallas_call(
        attend_kernel,
        grid=(head_count,),
        out_shape=(
            jax.ShapeDtypeStruct((inner, rows), BF16),
            jax.ShapeDtypeStruct((head_count, 1, rows), F32),
        ),
        in_specs=[
            column(rows), column(keys), column(keys), page(128, 128), page(1, width),
            whole((keys, 256)), whole((128, rows)),
        ],
        out_specs=(column(rows), page(1, rows)),
        scratch_shapes=[
            pltpu.VMEM((keys, 256), BF16),
            pltpu.VMEM((256, rows), BF16),
            pltpu.VMEM((LANES, width), F32),
            pltpu.VMEM((keys, rows), F32),
            pltpu.VMEM((keys, rows), BF16),
        ],
        compiler_params=pltpu.CompilerParams(
            dimension_semantics=("arbitrary",), vmem_limit_bytes=32 << 20
        ),
        name="attend",
    )(queries, keys_t, values_t, layout, line, key_extra, query_bins)


def attend_back(
    queries, keys_t, values_t, heads_out, heads_grad, lse, layout, line,
    key_extra, key_extra_t, query_bins, query_bins_t,
):
    inner, rows = queries.shape
    keys = keys_t.shape[1]
    head_count, _, width = line.shape
    head_size = inner // head_count
    whole, column, page = attention_shapes(head_count, head_size, rows, keys, width)
    return pl.pallas_call(
        attend_back_kernel,
        grid=(head_count,),
        out_shape=(
            jax.ShapeDtypeStruct((inner, rows), BF16),
            jax.ShapeDtypeStruct((inner, keys), BF16),
            jax.ShapeDtypeStruct((inner, keys), BF16),
            jax.ShapeDtypeStruct((head_count, 1, width), F32),
            jax.ShapeDtypeStruct((head_count, 128, 128), F32),
        ),
        in_specs=[
            column(rows), column(keys), column(keys), column(rows), column(rows),
            page(1, rows), page(128, 128), page(1, width),
            whole((keys, 256)), whole((128, keys)), whole((128, rows)), whole((rows, 128)),
        ],
        out_specs=(column(rows), column(keys), column(keys), page(1, width), page(128, 128)),
        scratch_shapes=[
            pltpu.VMEM((keys, 256), BF16),
            pltpu.VMEM((192, keys), BF16),
            pltpu.VMEM((256, rows), BF16),
            pltpu.VMEM((keys, 128), BF16),
            pltpu.VMEM((128, rows), BF16),
            pltpu.VMEM((LANES, width), F32),
            pltpu.VMEM((LANES, width), F32),
            pltpu.VMEM((keys, rows), BF16),
        ],
        compiler_params=pltpu.CompilerParams(
            dimension_semantics=("arbitrary",), vmem_limit_bytes=32 << 20
        ),
        name="attend_back",
    )(
        queries, keys_t, values_t, heads_out, heads_grad, lse, layout, line,
        key_extra, key_extra_t, query_bins, query_bins_t,
    )


def forward_items(mp_size):
    items = [(0, 0), (1, 0), (2, 0)] + [(0, k) for k in range(1, mp_size)]
    for k in range(1, mp_size):
        items += [(1, k), (2, k)]
    return items


def forward_kernel(
    mp_size, group,
    first_ref, gate_up_ref, down_ref, normed_t_ref, table_ref, key_info_ref, line_hot_ref,
    bin_hot_ref, input_ref, gain_ref, cotangent_ref,
    w_first, queries, keys_t, values_t, heads_out, lse, layout, line, key_extra, key_extra_t,
    slot_owner, residual, layer_output, second_grad, gate_up_full, down_full, tables,
    slot_t, w_gate_up, w_down, first_here, key_aug, query_aug, strip, scores, probs,
    second_t, second_owner, out_owner, out_t,
    hidden_a, hidden_b, hidden_c, act_t, low_t, stage_gate_up, stage_down,
    row_send, row_recv, row_own, table_send, table_recv, table_own, load_sem, store_sem, *sems,
):
    place = Place(mp_size)
    rows, model_width = input_ref.shape
    keys = keys_t.shape[1]
    blocks = keys // LANES
    width = strip.shape[1]
    inner_here = first_ref.shape[1]
    heads_here = inner_here // 64
    hidden = gate_up_ref.shape[1]
    member = lax.rem(place.mp, group)
    first_peer = place.mp - member
    own_lanes = pl.ds(pl.multiple_of(member * rows, LANES), rows)

    items = forward_items(mp_size)
    gather = Gather(
        place, [first_ref, gate_up_ref, down_ref], [w_first, w_gate_up, w_down], sems, items
    )
    at = {item: t for t, item in enumerate(items)}

    row_copies = [
        remote(
            normed_t_ref, slot_t.at[:, own_lanes], row_send.at[k], row_recv.at[k],
            (place.dp, first_peer + lax.rem(member + k, group)),
        )
        for k in range(1, group)
    ]
    table_copies = [
        remote(table_ref, tables.at[place.mp], table_send.at[k], table_recv.at[k], place.to_mp(k))
        for k in range(1, mp_size)
    ]
    row_here = Copy(normed_t_ref, slot_t.at[:, own_lanes], row_own.at[0])
    table_here = Copy(table_ref, tables.at[place.mp], table_own.at[0])

    row_here.start()
    table_here.start()
    meet(place)
    gather.start_chunk(0)
    for copy in table_copies + row_copies:
        copy.start()
    gather.start_chunk(1)
    gather.start_chunk(2)
    gather.step(0)

    key_rows = row_ids((64, keys)).astype(F32)
    x_place = jnp.where(key_rows == key_info_ref[0:1, :], 1.0, 0.0).astype(BF16)
    y_place = jnp.where(key_rows == key_info_ref[1:2, :], 1.0, 0.0).astype(BF16)
    key_extra_t[0:64, :] = x_place
    key_extra_t[64:128, :] = y_place
    tail = jnp.where(
        key_rows == 0.0, key_info_ref[2:3, :], jnp.where(key_rows < 4.0, 1.0, 0.0)
    ).astype(BF16)
    turned = jnp.concatenate([jnp.zeros((64, keys), BF16), x_place, y_place, tail], axis=0).T
    key_extra[...] = turned
    key_aug[...] = turned
    query_aug[pl.ds(192, 64), :] = jnp.where(row_ids((64, rows)) == 0, 1.0, 0.0).astype(BF16)
    gather.step(1)
    for block in range(model_width // LANES):
        owner = block_owner(block)
        out_owner[:, owner * LANES : (owner + 1) * LANES] = cotangent_ref[
            :, block * LANES : (block + 1) * LANES
        ].astype(BF16)
    out_t[...] = cotangent_ref[...].astype(BF16).T
    residual[...] = input_ref[...]
    layer_output[...] = jnp.zeros_like(layer_output)
    second_grad[...] = jnp.zeros_like(second_grad)
    row_here.wait()
    table_here.wait()
    gather.step(2)

    head_units = mp_size * heads_here
    plan = {}
    total = gather.steps
    for k in range(1, mp_size):
        need = at[(0, k)] + 2
        plan.setdefault((k * heads_here, 0), []).append(need)
    for k in range(mp_size):
        need = at[(2, k)] + 2
        plan.setdefault((head_units + k, 0), []).append(need)
    table = {}
    done = 2
    order = sorted(plan.items())
    for (unit, point), needs in order:
        need = max(needs)
        if need <= done:
            continue
        missing = list(range(done + 1, need + 1))
        spots = [(unit, 0)]
        if unit >= head_units:
            before = [(unit - 1, p) for p in (3, 2, 1)] if unit > head_units else []
            if unit == head_units:
                before = [(unit - 1, 0), (unit - 2, 0), (unit - 3, 0)]
        else:
            before = [(unit - 1, 0), (unit - 2, 0), (unit - 3, 0)]
        spots = spots + before
        for i, s in enumerate(reversed(missing)):
            table.setdefault(spots[min(i, len(spots) - 1)], []).append(s)
        done = need
    for spot in table:
        table[spot].sort()
    rest = list(range(done + 1, total))

    def communicate(unit, point):
        for (at_unit, at_point), steps in table.items():
            if at_point == point:

                @pl.when(unit == at_unit)
                def _(steps=steps):
                    for s in steps:
                        gather.step(s)

    def head_unit(unit, carry):
        communicate(unit, 0)
        step = lax.div(unit, heads_here)
        inside = lax.rem(unit, heads_here)
        source = place.from_mp(step)
        base = pl.multiple_of(source * inner_here, 16)
        head = source * heads_here + inside

        @pl.when(inside == 0)
        def _():
            for k in range(mp_size):

                @pl.when(step == k)
                def _(k=k):
                    gather.done(at[(0, k)])
                    if k == 0:
                        for copy in row_copies:
                            copy.wait_recv()
                    else:
                        table_copies[k - 1].wait_recv()

            load = Copy(w_first.at[:, pl.ds(base, inner_here), :], first_here, load_sem.at[0])
            load.start()
            hot = tables[source].astype(BF16)
            line[source] = jnp.dot(hot[0:8], line_hot_ref[...], preferred_element_type=F32)
            bins = jnp.dot(hot[8:24], bin_hot_ref[...], preferred_element_type=F32)
            for i in range(heads_here):
                x_line = jnp.broadcast_to(bins[i : i + 1], (64, LANES))
                y_line = jnp.broadcast_to(bins[8 + i : 9 + i], (64, LANES))
                left = lane_ids((64, LANES)) < 64
                x_part = pltpu.roll(x_line, 0, 1, stride=1, stride_axis=0)
                y_part = pltpu.roll(y_line, 64, 1, stride=1, stride_axis=0)
                layout[source * heads_here + i] = jnp.concatenate(
                    [jnp.where(left, x_part, 0.0), jnp.where(left, 0.0, y_part)], axis=0
                ).astype(BF16)
            load.wait()
            here = pl.ds(base, inner_here)
            queries[here, :] = jnp.dot(
                first_here[0], normed_t_ref[...], preferred_element_type=F32
            ).astype(BF16)
            keys_t[here, :] = jnp.dot(
                first_here[1], slot_t[...], preferred_element_type=F32
            ).astype(BF16)
            values_t[here, :] = jnp.dot(
                first_here[2], slot_t[...], preferred_element_type=F32
            ).astype(BF16)

        here = pl.ds(pl.multiple_of(head * 64, 16), 64)
        both = jnp.concatenate([keys_t[here, :], values_t[here, :]], axis=0).T
        low_lanes = lane_ids((keys, LANES)) < 64
        key_aug[:, 0:LANES] = jnp.where(low_lanes, both, key_extra[:, 0:LANES])
        query_aug[pl.ds(0, 64), :] = queries[here, :]
        query_aug[pl.ds(64, 128), :] = jnp.dot(
            layout[head], key_extra_t[:, own_lanes], preferred_element_type=F32
        ).astype(BF16)
        strip[...] = pltpu.roll(
            jnp.broadcast_to(line[source, pl.ds(inside, 1), :], (LANES, width)), 0, 1,
            stride=1, stride_axis=0,
        )
        query_all = query_aug[...]
        top = jnp.full((1, rows), -jnp.inf, F32)
        for block in range(blocks):
            some = pl.ds(block * LANES, LANES)
            part = jnp.dot(key_aug[some, :], query_all, preferred_element_type=F32)
            part = part + strip[:, pl.ds((blocks - 1 - block) * LANES, rows)]
            scores[some, :] = part
            top = jnp.maximum(top, jnp.max(part, axis=0, keepdims=True))
        sums = jnp.zeros((1, rows), F32)
        for block in range(blocks):
            some = pl.ds(block * LANES, LANES)
            part = jnp.exp(scores[some, :] - top)
            sums = sums + jnp.sum(part, axis=0, keepdims=True)
            probs[some, :] = part.astype(BF16)
        mixed = jnp.dot(values_t[here, :], probs[...], preferred_element_type=F32)
        heads_out[here, :] = (mixed / sums).astype(BF16)
        lse[head] = top + jnp.log(sums)

        @pl.when(inside == heads_here - 1)
        def _():
            part = heads_out[pl.ds(base, inner_here), :].T
            residual[...] = residual[...] + jnp.dot(
                part, first_here[3], preferred_element_type=F32
            )

        return carry

    lax.fori_loop(0, head_units, head_unit, 0)
    for block in range(model_width // LANES):
        owner = block_owner(block)
        slot_owner[:, owner * LANES : (owner + 1) * LANES] = slot_t[
            block * LANES : (block + 1) * LANES, :
        ].T

    def norm_rows(i, carry):
        here = pl.ds(pl.multiple_of(i * 16, 16), 16)
        values = residual[here, :]
        scale = lax.rsqrt(jnp.mean(values * values, axis=1, keepdims=True) + EPSILON)
        normed = (values * scale * gain_ref[...]).astype(BF16)
        second_owner[here, :] = normed
        return carry

    lax.fori_loop(0, rows // 16, norm_rows, 0)
    second_t[...] = second_owner[...].T
    turned_blocks = [second_owner[:, b * LANES : (b + 1) * LANES] for b in range(model_width // LANES)]
    for block, values in enumerate(turned_blocks):
        owner = block_owner(block)
        second_owner[:, owner * LANES : (owner + 1) * LANES] = values

    def store(step):
        source = place.from_mp(step)
        here = pl.ds(pl.multiple_of(source * hidden, 16), hidden)
        return [
            Copy(stage_gate_up, gate_up_full.at[:, here, :], store_sem.at[0]),
            Copy(stage_down, down_full.at[:, here, :], store_sem.at[1]),
        ]

    def hidden_unit(step, carry):
        unit = step + head_units
        communicate(unit, 0)
        source = place.from_mp(step)
        here = pl.ds(pl.multiple_of(source * hidden, 16), hidden)
        for k in range(mp_size):

            @pl.when(step == k)
            def _(k=k):
                gather.done(at[(1, k)])
                gather.done(at[(2, k)])

        hidden_a[...] = jnp.dot(w_gate_up[0, here, :], second_t[...], preferred_element_type=F32)
        hidden_b[...] = jnp.dot(w_gate_up[1, here, :], second_t[...], preferred_element_type=F32)
        communicate(unit, 1)
        hidden_c[...] = jnp.dot(w_down[0, here, :], out_t[...], preferred_element_type=F32)

        def activate(i, inner_carry):
            some = pl.ds(pl.multiple_of(i * 16, 16), 16)
            gate, up, slope = hidden_a[some, :], hidden_b[some, :], hidden_c[some, :]
            square = gate * gate
            factor = 0.7978845608028654
            bent = jnp.tanh(factor * gate * (1.0 + 0.044715 * square))
            half = 0.5 * (1.0 + bent)
            value = gate * half
            change = half + 0.5 * gate * (1.0 - bent * bent) * (
                factor * (1.0 + 3.0 * 0.044715 * square)
            )
            act_t[some, :] = (value * up).astype(BF16)
            low_t[some, :] = (slope * up * change).astype(BF16)
            low_t[pl.ds(pl.multiple_of(hidden + i * 16, 16), 16), :] = (slope * value).astype(BF16)
            return inner_carry

        lax.fori_loop(0, hidden // 16, activate, 0)
        communicate(unit, 2)

        @pl.when(step > 0)
        def _():
            for copy in store(step):
                copy.wait()

        stage_down[0] = jnp.dot(act_t[...], out_owner[...], preferred_element_type=F32).astype(BF16)
        stage_gate_up[0] = jnp.dot(
            low_t[0:hidden], second_owner[...], preferred_element_type=F32
        ).astype(BF16)
        stage_gate_up[1] = jnp.dot(
            low_t[hidden:], second_owner[...], preferred_element_type=F32
        ).astype(BF16)
        for copy in store(step):
            copy.start()
        communicate(unit, 3)
        layer_output[...] = layer_output[...] + dot_f32(act_t[...].T, w_down[0, here, :], 1, 0)
        second_grad[...] = (
            second_grad[...]
            + dot_f32(low_t[0:hidden].T, w_gate_up[0, here, :], 1, 0)
            + dot_f32(low_t[hidden:].T, w_gate_up[1, here, :], 1, 0)
        )
        return carry

    lax.fori_loop(0, mp_size, hidden_unit, 0)
    layer_output[...] = layer_output[...] + residual[...]
    for s in rest:
        gather.step(s)
    for copy in store(mp_size - 1):
        copy.wait()
    gather.close()
    for copy in row_copies + table_copies:
        copy.wait_send()


def block_owner(block):
    return (block % 2) * 4 + block // 2


def forward(mp_size, group, pieces, normed_t, table, key_info, line_hot, bin_hot, layer_input, gain, cotangent):
    first, gate_up, down = pieces
    rows, model_width = layer_input.shape
    keys = key_info.shape[1]
    width = line_hot.shape[1]
    inner_here, hidden = first.shape[1], gate_up.shape[1]
    inner, total_hidden = inner_here * mp_size, hidden * mp_size
    head_count = inner // 64
    dma = pltpu.SemaphoreType.DMA
    hbm = pl.BlockSpec(memory_space=HBM)
    vmem = pl.BlockSpec(memory_space=pltpu.VMEM)
    shape = jax.ShapeDtypeStruct
    out = [
        (shape((4, inner, model_width), BF16), hbm),
        (shape((inner, rows), BF16), vmem),
        (shape((inner, keys), BF16), vmem),
        (shape((inner, keys), BF16), vmem),
        (shape((inner, rows), BF16), vmem),
        (shape((head_count, 1, rows), F32), vmem),
        (shape((head_count, 128, 128), BF16), vmem),
        (shape((mp_size, 8, width), F32), vmem),
        (shape((keys, 256), BF16), vmem),
        (shape((128, keys), BF16), vmem),
        (shape((keys, model_width), BF16), vmem),
        (shape((rows, model_width), F32), vmem),
        (shape((rows, model_width), F32), vmem),
        (shape((rows, model_width), F32), vmem),
        (shape((2, total_hidden, model_width), BF16), hbm),
        (shape((1, total_hidden, model_width), BF16), hbm),
        (shape((mp_size, 24, LANES), F32), vmem),
    ]
    return pl.pallas_call(
        partial(forward_kernel, mp_size, group),
        out_shape=tuple(o[0] for o in out),
        in_specs=[hbm] * 3 + [vmem] * 8,
        out_specs=tuple(o[1] for o in out),
        scratch_shapes=[
            pltpu.VMEM((model_width, keys), BF16),
            pltpu.VMEM((2, total_hidden, model_width), BF16),
            pltpu.VMEM((1, total_hidden, model_width), BF16),
            pltpu.VMEM((4, inner_here, model_width), BF16),
            pltpu.VMEM((keys, 256), BF16),
            pltpu.VMEM((256, rows), BF16),
            pltpu.VMEM((LANES, width), F32),
            pltpu.VMEM((keys, rows), F32),
            pltpu.VMEM((keys, rows), BF16),
            pltpu.VMEM((model_width, rows), BF16),
            pltpu.VMEM((rows, model_width), BF16),
            pltpu.VMEM((rows, model_width), BF16),
            pltpu.VMEM((model_width, rows), BF16),
            pltpu.VMEM((hidden, rows), F32),
            pltpu.VMEM((hidden, rows), F32),
            pltpu.VMEM((hidden, rows), F32),
            pltpu.VMEM((hidden, rows), BF16),
            pltpu.VMEM((2 * hidden, rows), BF16),
            pltpu.VMEM((2, hidden, model_width), BF16),
            pltpu.VMEM((1, hidden, model_width), BF16),
            dma((group,)), dma((group,)), dma((1,)),
            dma((mp_size,)), dma((mp_size,)), dma((1,)), dma((1,)), dma((2,)),
        ]
        + Gather.semaphores(3, mp_size),
        compiler_params=pltpu.CompilerParams(
            collective_id=0, has_side_effects=True, vmem_limit_bytes=62 << 20
        ),
        name="forward",
    )(first, gate_up, down, normed_t, table, key_info, line_hot, bin_hot, layer_input, gain, cotangent)


def backward_items(mp_size):
    order = list(range(1, mp_size)) + [0]
    items = [(c, order[0]) for c in (0, 1)]
    for last, k in zip(order, order[1:]):
        items += [(0, k), (1, k), (2, last)]
    return items + [(2, order[-1])]


def unskewed(values, first, count, shift):
    width = values.shape[1]
    folded = None
    for group in range(count // 8):
        part = values[pl.ds(first + group * 8, 8), :]
        back = (-(group * 8 + shift)) % width
        part = pltpu.roll(part, back, 1) if back else part
        folded = part if folded is None else folded + part
    total = folded[0:1]
    for row in range(1, 8):
        total = total + pltpu.roll(folded[row : row + 1], width - row, 1)
    return total


def exact_dot(left, right):
    parts = three_parts(left)
    return sum(dot_f32(part, right, 1, 1) for part in parts)


def backward_kernel(mp_size, group, *refs):
    (
        gate_up_full, down_full, w_first, queries, keys_t, values_t, heads_out,
        residual_in, second_in, cotangent_in,
        lse, layout, line, key_extra, key_extra_t, slot_owner, layer_input, gains, line_hot, bin_hot,
        input_grad, small_out, gate_up_sum, down_sum, first_sum,
        *refs,
    ) = refs
    (
        slot_grad, own_grad, residual_grad, branch_owner, branch_t, w_query, w_output, w_kv,
        q_here, k_here, v_here, out_here, grad_here, dq_here, dk_here, dv_here, kv_here,
        key_aug, key_aug_t, query_aug, value_aug, grad_aug, strip, strip_grad, probs_grad,
        layout_grad, line_sums, bin_sums, gain_part, rows_out, peers, stage, stage_in, full_here,
        load_sem, value_sem, row_send, row_recv, stage_send, stage_recv,
        *refs,
    ) = refs
    place = Place(mp_size)
    rows, model_width = layer_input.shape
    keys = slot_owner.shape[0]
    blocks = keys // LANES
    inner_here = q_here.shape[0]
    heads_here = inner_here // 64
    member = lax.rem(place.mp, group)
    first_peer = place.mp - member
    own_start = pl.multiple_of(member * rows, LANES)
    own_lanes = pl.ds(own_start, rows)

    items = backward_items(mp_size)
    fulls = [gate_up_full, down_full, full_here]
    scatter = Scatter(place, fulls, [gate_up_sum, down_sum, first_sum], refs, items)

    loads = [
        Copy(second_in, slot_grad.at[pl.ds(0, rows), :], value_sem.at[0]),
        Copy(residual_in, slot_grad.at[pl.ds(rows, rows), :], value_sem.at[1]),
        Copy(cotangent_in, input_grad, value_sem.at[2]),
    ]
    for copy in loads:
        copy.start()
    meet(place)
    scatter.step(0)
    key_aug[...] = key_extra[...]
    key_aug_t[pl.ds(64, 128), :] = key_extra_t[...]
    for copy in loads:
        copy.wait()

    def norm_back(i, total):
        here = pl.ds(pl.multiple_of(i * 16, 16), 16)
        grad = slot_grad[here, :]
        values = slot_grad[pl.ds(pl.multiple_of(rows + i * 16, 16), 16), :]
        scale = lax.rsqrt(jnp.mean(values * values, axis=1, keepdims=True) + EPSILON)
        scaled = gains[1:2, :] * grad
        mean = jnp.mean(scaled * values, axis=1, keepdims=True)
        result = input_grad[here, :] + scale * scaled - values * (scale * scale * scale * mean)
        residual_grad[here, :] = result
        branch_owner[here, :] = result.astype(BF16)
        product = grad * values * scale
        return total + product[0:8] + product[8:16]

    total = lax.fori_loop(0, rows // 16, norm_back, jnp.zeros((8, model_width), F32))
    gain_part[1:2, :] = jnp.sum(total, axis=0, keepdims=True)
    scatter.step(1)
    branch_t[...] = branch_owner[...].T
    parts = [branch_owner[:, b * LANES : (b + 1) * LANES] for b in range(model_width // LANES)]
    for block, values in enumerate(parts):
        owner = block_owner(block)
        branch_owner[:, owner * LANES : (owner + 1) * LANES] = values
    slot_grad[...] = jnp.zeros_like(slot_grad)
    own_grad[...] = jnp.zeros_like(own_grad)
    scatter.step(2)

    plan = {}
    for block in range(mp_size - 1):
        plan[(block, 1)] = [3 * block + 3]
        plan[(block, 2)] = [3 * block + 4]
        if block + 2 < mp_size:
            plan[(block + 1, 0)] = [3 * block + 5]
    done = 3 * mp_size - 1
    plan[(mp_size - 1, 2)] = [done]

    def communicate(block, point):
        for (at_block, at_point), steps in plan.items():
            if at_point == point:

                @pl.when(block == at_block)
                def _(steps=steps):
                    for s in steps:
                        scatter.step(s)

    def block_unit(block, carry):
        communicate(block, 0)
        step = lax.rem(block + 1, mp_size)
        target = lax.rem(place.mp + step, mp_size)
        base = pl.multiple_of(target * inner_here, 16)
        here = pl.ds(base, inner_here)
        slot = lax.rem(block, 2)
        copies = [
            Copy(w_first.at[0, here, :], w_query, load_sem.at[0]),
            Copy(w_first.at[3, here, :], w_output, load_sem.at[1]),
            Copy(queries.at[here, :], q_here, load_sem.at[2]),
            Copy(keys_t.at[here, :], k_here, load_sem.at[3]),
            Copy(values_t.at[here, :], v_here, load_sem.at[4]),
            Copy(heads_out.at[here, :], out_here, load_sem.at[5]),
        ]
        for i in range(heads_here):
            for part in range(2):
                copies.append(
                    Copy(
                        w_first.at[1 + part, pl.ds(pl.multiple_of(base + i * 64, 16), 64), :],
                        w_kv.at[pl.ds(i * 128 + part * 64, 64), :],
                        load_sem.at[6 + 2 * i + part],
                    )
                )
        for copy in copies:
            copy.start()
        for copy in copies:
            copy.wait()

        for b in range(2, mp_size):

            @pl.when(block == b)
            def _(b=b):
                scatter.left(items.index((2, (b - 1) % mp_size)))

        grad_here[...] = jnp.dot(w_output[...], branch_t[...], preferred_element_type=F32).astype(BF16)
        full_here[slot, 3] = jnp.dot(
            out_here[...], branch_owner[...], preferred_element_type=F32
        ).astype(BF16)

        def head_unit(inside, inner_carry):
            head = target * heads_here + inside
            some = pl.ds(pl.multiple_of(inside * 64, 16), 64)
            q_head, k_head, v_head = q_here[some, :], k_here[some, :], v_here[some, :]
            grad_head = grad_here[some, :]
            both = jnp.concatenate([k_head, v_head], axis=0).T
            lanes = lane_ids((keys, LANES))
            key_aug[:, 0:LANES] = jnp.where(lanes < 64, both, key_extra[:, 0:LANES])
            ones = jnp.where(lanes < 3, 1.0, 0.0).astype(BF16)
            value_aug[...] = jnp.where(lanes < 64, ones, both)
            key_aug_t[pl.ds(0, 64), :] = k_head
            query_aug[pl.ds(0, 64), :] = q_head
            query_aug[pl.ds(64, 128), :] = jnp.dot(
                layout[head], key_extra_t[:, own_lanes], preferred_element_type=F32
            ).astype(BF16)
            high, middle, low = three_parts(-lse[head])
            tail = row_ids((64, rows))
            rows_of = lambda part: jnp.broadcast_to(part.astype(F32), (64, rows))
            query_aug[pl.ds(192, 64), :] = jnp.where(
                tail == 0, 1.0,
                jnp.where(
                    tail == 1, rows_of(high),
                    jnp.where(tail == 2, rows_of(middle), jnp.where(tail == 3, rows_of(low), 0.0)),
                ),
            ).astype(BF16)
            row_dot = jnp.sum(
                grad_head.astype(F32) * out_here[some, :].astype(F32), axis=0, keepdims=True
            )
            high, middle, low = three_parts(-row_dot)
            grad_aug[pl.ds(0, 64), :] = jnp.where(
                tail == 0, rows_of(high),
                jnp.where(tail == 1, rows_of(middle), jnp.where(tail == 2, rows_of(low), 0.0)),
            ).astype(BF16)
            grad_aug[pl.ds(64, 64), :] = grad_head
            width = strip.shape[1]
            strip[...] = pltpu.roll(
                jnp.broadcast_to(line[target, pl.ds(inside, 1), :], (LANES, width)), 0, 1,
                stride=1, stride_axis=0,
            )
            strip_grad[...] = jnp.zeros_like(strip_grad)
            query_and_grad = jnp.concatenate([q_head, grad_head], axis=0).T
            query_all = query_aug[...]
            grad_all = grad_aug[...]
            half = lane_ids((LANES, LANES)) < 64
            kv_lanes = pl.ds(pl.multiple_of(inside * LANES, LANES), LANES)
            for part_index in range(blocks):
                these = pl.ds(part_index * LANES, LANES)
                band = pl.ds((blocks - 1 - part_index) * LANES, rows)
                part = jnp.dot(key_aug[these, :], query_all, preferred_element_type=F32)
                part = jnp.exp(part + strip[:, band])
                slope = part * jnp.dot(value_aug[these, :], grad_all, preferred_element_type=F32)
                strip_grad[:, band] = strip_grad[:, band] + slope
                slope = slope.astype(BF16)
                probs_grad[these, :] = slope
                key_part = jnp.dot(slope, query_and_grad, preferred_element_type=F32)
                value_part = jnp.dot(part.astype(BF16), query_and_grad, preferred_element_type=F32)
                joined = jnp.where(half, key_part, value_part)
                kv_here[these, kv_lanes] = joined.astype(BF16)
                turned = joined.T.astype(BF16)
                dk_here[some, these] = turned[0:64]
                dv_here[some, these] = turned[64:128]
            query_part = jnp.dot(key_aug_t[...], probs_grad[...], preferred_element_type=F32)
            dq_here[some, :] = query_part[0:64].astype(BF16)
            bins = dot_f32(query_part[64:192].astype(BF16), key_extra_t[:, own_lanes], 1, 1)
            left = lane_ids((LANES, LANES)) < 64
            upper = row_ids((LANES, LANES)) < 64
            layout_grad[...] = jnp.where(left == upper, bins, 0.0)
            bin_sums[0, pl.ds(head, 1), :] = unskewed(layout_grad, 0, 64, 0)
            bin_sums[1, pl.ds(head, 1), :] = unskewed(layout_grad, 64, 64, 64)
            line_sums[pl.ds(head, 1), :] = unskewed(strip_grad, 0, LANES, 0)
            return inner_carry

        half_heads = heads_here // 2
        lax.fori_loop(0, half_heads, head_unit, 0)
        communicate(block, 1)
        lax.fori_loop(half_heads, heads_here, head_unit, 0)
        full_here[slot, 0] = jnp.dot(
            dq_here[...], slot_owner[pl.ds(own_start, rows), :], preferred_element_type=F32
        ).astype(BF16)
        full_here[slot, 1] = jnp.dot(
            dk_here[...], slot_owner[...], preferred_element_type=F32
        ).astype(BF16)
        full_here[slot, 2] = jnp.dot(
            dv_here[...], slot_owner[...], preferred_element_type=F32
        ).astype(BF16)
        slot_grad[...] = slot_grad[...] + jnp.dot(
            kv_here[...], w_kv[...], preferred_element_type=F32
        )
        own_grad[...] = own_grad[...] + jnp.dot(
            dq_here[...].T, w_query[...], preferred_element_type=F32
        )
        communicate(block, 2)
        return carry

    lax.fori_loop(0, mp_size, block_unit, 0)

    copies = []
    for k in range(1, group):
        other = lax.rem(member + k, group)
        rows_out[k - 1] = slot_grad[pl.ds(pl.multiple_of(other * rows, 16), rows), :].astype(BF16)
        copies.append(
            remote(
                rows_out.at[k - 1], peers.at[k - 1], row_send.at[k], row_recv.at[k],
                (place.dp, first_peer + other),
            )
        )
    for copy in copies:
        copy.start()
    steps = list(range(done + 1, scatter.steps))
    for s in steps[:1]:
        scatter.step(s)

    gain_rows = model_width // LANES
    head_count = bin_sums.shape[1]
    stage[0, 2 * gain_rows : 2 * gain_rows + head_count, :] = exact_dot(line_sums[...], line_hot[...])
    for i in range(2):
        start = 2 * gain_rows + (1 + i) * head_count
        stage[0, start : start + head_count, :] = exact_dot(bin_sums[i], bin_hot[...])
    for s in steps[1:2]:
        scatter.step(s)
    for copy in copies:
        copy.wait_recv()

    def input_back(i, total):
        here = pl.ds(pl.multiple_of(i * 16, 16), 16)
        grad = own_grad[here, :] + slot_grad[pl.ds(pl.multiple_of(own_start + i * 16, 16), 16), :]
        for k in range(group - 1):
            grad = grad + peers[k, here, :].astype(F32)
        values = layer_input[here, :]
        scale = lax.rsqrt(jnp.mean(values * values, axis=1, keepdims=True) + EPSILON)
        scaled = gains[0:1, :] * grad
        mean = jnp.mean(scaled * values, axis=1, keepdims=True)
        input_grad[here, :] = (
            residual_grad[here, :] + scale * scaled - values * (scale * scale * scale * mean)
        )
        product = grad * values * scale
        return total + product[0:8] + product[8:16]

    total = lax.fori_loop(0, rows // 16, input_back, jnp.zeros((8, model_width), F32))
    gain_part[0:1, :] = jnp.sum(total, axis=0, keepdims=True)
    for which in range(2):
        for i in range(gain_rows):
            row = which * gain_rows + i
            stage[0, row : row + 1, :] = gain_part[which : which + 1, i * LANES : (i + 1) * LANES]

    partners = [place.to_core, place.to_x, place.to_y]
    bit = 1
    while bit < mp_size:
        flipped = place.mp + bit - 2 * bit * lax.rem(lax.div(place.mp, bit), 2)
        partners.append((place.dp, flipped))
        bit *= 2
    sums = [
        remote(stage.at[i], stage_in.at[i], stage_send.at[i], stage_recv.at[i], partner)
        for i, partner in enumerate(partners)
    ]
    sums[0].start()
    steps = steps[2:]
    for i, copy in enumerate(sums):
        for s in steps[:1]:
            scatter.step(s)
        steps = steps[1:]
        copy.wait_recv()
        if i + 1 < len(sums):
            stage[i + 1] = stage[i] + stage_in[i]
            sums[i + 1].start()
        else:
            small_out[...] = stage[i] + stage_in[i]
    for s in steps:
        scatter.step(s)
    scatter.close()
    for copy in copies + sums:
        copy.wait_send()


def backward(
    mp_size, group, gate_up_full, down_full, w_first, queries, keys_t, values_t, heads_out,
    residual, second_grad, cotangent, lse, layout, line, key_extra, key_extra_t, slot_owner,
    layer_input, gains, line_hot, bin_hot,
):
    rows, model_width = layer_input.shape
    keys = slot_owner.shape[0]
    width = line.shape[2]
    inner_here = queries.shape[0] // mp_size
    heads_here = inner_here // 64
    head_count = heads_here * mp_size
    hidden = down_full.shape[1] // mp_size
    sizes = [(2, hidden), (1, hidden), (4, inner_here)]
    count = 3 + (mp_size - 1).bit_length()
    small_rows = 2 * model_width // LANES + 3 * head_count
    others = max(group - 1, 1)
    dma = pltpu.SemaphoreType.DMA
    hbm = pl.BlockSpec(memory_space=HBM)
    vmem = pl.BlockSpec(memory_space=pltpu.VMEM)
    shape = jax.ShapeDtypeStruct
    return pl.pallas_call(
        partial(backward_kernel, mp_size, group),
        out_shape=(
            shape((rows, model_width), F32),
            shape((small_rows, LANES), F32),
            *[shape((lead, n, LANES), F32) for lead, n in sizes],
        ),
        in_specs=[hbm] * 10 + [vmem] * 10,
        out_specs=(vmem,) * 5,
        scratch_shapes=[
            pltpu.VMEM((keys, model_width), F32),
            pltpu.VMEM((rows, model_width), F32),
            pltpu.VMEM((rows, model_width), F32),
            pltpu.VMEM((rows, model_width), BF16),
            pltpu.VMEM((model_width, rows), BF16),
            pltpu.VMEM((inner_here, model_width), BF16),
            pltpu.VMEM((inner_here, model_width), BF16),
            pltpu.VMEM((2 * inner_here, model_width), BF16),
            pltpu.VMEM((inner_here, rows), BF16),
            pltpu.VMEM((inner_here, keys), BF16),
            pltpu.VMEM((inner_here, keys), BF16),
            pltpu.VMEM((inner_here, rows), BF16),
            pltpu.VMEM((inner_here, rows), BF16),
            pltpu.VMEM((inner_here, rows), BF16),
            pltpu.VMEM((inner_here, keys), BF16),
            pltpu.VMEM((inner_here, keys), BF16),
            pltpu.VMEM((keys, heads_here * LANES), BF16),
            pltpu.VMEM((keys, 256), BF16),
            pltpu.VMEM((192, keys), BF16),
            pltpu.VMEM((256, rows), BF16),
            pltpu.VMEM((keys, LANES), BF16),
            pltpu.VMEM((LANES, rows), BF16),
            pltpu.VMEM((LANES, width), F32),
            pltpu.VMEM((LANES, width), F32),
            pltpu.VMEM((keys, rows), BF16),
            pltpu.VMEM((LANES, LANES), F32),
            pltpu.VMEM((head_count, width), F32),
            pltpu.VMEM((2, head_count, LANES), F32),
            pltpu.VMEM((2, model_width), F32),
            pltpu.VMEM((others, rows, model_width), BF16),
            pltpu.VMEM((others, rows, model_width), BF16),
            pltpu.VMEM((count, small_rows, LANES), F32),
            pltpu.VMEM((count, small_rows, LANES), F32),
            pltpu.VMEM((2, 4, inner_here, model_width), BF16),
            dma((6 + 2 * heads_here,)), dma((3,)), dma((group,)), dma((group,)),
            dma((count,)), dma((count,)),
        ]
        + Scatter.scratch(sizes, (True, True, False), mp_size),
        compiler_params=pltpu.CompilerParams(
            collective_id=1, has_side_effects=True, vmem_limit_bytes=63 << 20
        ),
        name="backward",
    )(
        gate_up_full, down_full, w_first, queries, keys_t, values_t, heads_out, residual,
        second_grad, cotangent, lse, layout, line, key_extra, key_extra_t, slot_owner, layer_input,
        gains, line_hot, bin_hot,
    )


def line_onehot(first_row, width, key_blocks):
    place = jnp.arange(width, dtype=jnp.int32)
    place = jnp.where(place >= width - LANES, place - width, place)
    offset = LANES * (key_blocks - 1) - place - first_row
    return (bucket_of(offset)[:, None] == jnp.arange(32, dtype=jnp.int32)[None, :]).astype(F32)


def bin_onehot():
    bins = np.arange(NBIN)
    offset = bins[:, None] - bins[None, :]
    distance = np.abs(offset)
    bucket = np.minimum(distance, 7) + sum((distance >= t).astype(np.int64) for t in THRESHOLDS)
    bucket = bucket + 16 * (offset > 0)
    return jnp.asarray(bucket[:, :, None] == np.arange(32), F32)


def gather_rows(local, axis_name):
    return lax.all_gather(local, axis_name, axis=0, tiled=True)


def scatter_grad(full):
    summed = lax.psum_scatter(full, "dp", scatter_dimension=1, tiled=True)
    return lax.psum_scatter(summed, "mp", scatter_dimension=0, tiled=True)


def per_device_plain(
    dp_size, mp_size,
    layer_input, norm_gains, query_weight, key_value_weight, output_weight,
    gate_up_weight, down_weight, bias_tables, doc_lengths, box_bins, cotangent,
):
    rows, model_width = layer_input.shape
    doc_count = doc_lengths.shape[0]
    slot_span = box_bins.shape[1] // doc_count
    group = mp_size // doc_count
    mp_index = lax.axis_index("mp")
    doc = mp_index // group
    first_row = (mp_index % group) * rows
    key_blocks = slot_span // LANES
    width = LANES * (key_blocks + (rows + LANES - 1) // LANES)
    groups = [[d * group + i for i in range(group)] for d in range(doc_count)]
    gain_first = norm_gains[0].astype(F32)
    gain_second = norm_gains[1].astype(F32)

    w_query = gather_rows(query_weight.T, "mp")
    inner_here = query_weight.shape[1]
    inner = inner_here * mp_size
    w_key = gather_rows(key_value_weight[:, 0].T, "mp")
    w_value = gather_rows(key_value_weight[:, 1].T, "mp")
    w_output = gather_rows(output_weight, "mp")
    w_gate = gather_rows(gate_up_weight[:, 0].T, "mp")
    w_up = gather_rows(gate_up_weight[:, 1].T, "mp")
    w_down = gather_rows(down_weight, "mp")
    tables = lax.all_gather(bias_tables, "mp", axis=2, tiled=True).astype(F32)
    head_count = tables.shape[2]

    onehot_line = line_onehot(first_row, width, key_blocks)
    line = jnp.dot(onehot_line, tables[0], precision=lax.Precision.HIGHEST)
    line = line.T.reshape(head_count, 1, width)
    onehot_bin = bin_onehot()
    x_part = jnp.einsum("ban,nh->hba", onehot_bin, tables[1], precision=lax.Precision.HIGHEST)
    y_part = jnp.einsum("ban,nh->hba", onehot_bin, tables[2], precision=lax.Precision.HIGHEST)
    empty = jnp.zeros_like(x_part)
    layout = jnp.concatenate(
        [jnp.concatenate([x_part, empty], axis=2), jnp.concatenate([empty, y_part], axis=2)], axis=1
    ).astype(BF16)
    key_bins = lax.dynamic_slice(box_bins, (0, doc * slot_span), (2, slot_span))
    own_bins = lax.dynamic_slice(key_bins, (0, first_row), (2, rows))
    bin_ids = jnp.arange(NBIN, dtype=jnp.int32)

    def placed_rows(bins):
        return jnp.concatenate(
            [bins[0][:, None] == bin_ids, bins[1][:, None] == bin_ids], axis=1
        ).astype(BF16)

    def placed_lanes(bins):
        return jnp.concatenate(
            [bin_ids[:, None] == bins[0][None], bin_ids[:, None] == bins[1][None]], axis=0
        ).astype(BF16)

    length = lax.dynamic_index_in_dim(doc_lengths, doc, keepdims=False)
    masked = jnp.arange(slot_span, dtype=jnp.int32)[:, None] >= length
    key_placed = placed_rows(key_bins)
    key_extra = jnp.concatenate(
        [
            jnp.zeros((slot_span, 64), BF16),
            key_placed,
            jnp.where(masked, NEG_FILL, 0.0).astype(BF16),
            jnp.ones((slot_span, 3), BF16),
            jnp.zeros((slot_span, 60), BF16),
        ],
        axis=1,
    )
    key_extra_t = placed_lanes(key_bins)
    query_bins_t = placed_rows(own_bins)
    query_bins = placed_lanes(own_bins)

    scale_first = inverse_rms(layer_input)
    normed = (layer_input * scale_first * gain_first).astype(BF16)
    slot_normed = lax.all_gather(normed, "mp", axis=0, tiled=True, axis_index_groups=groups)
    queries = dot_f32(w_query, normed, 1, 1).astype(BF16)
    keys_t = dot_f32(w_key, slot_normed, 1, 1).astype(BF16)
    values_t = dot_f32(w_value, slot_normed, 1, 1).astype(BF16)
    heads_out, lse = attend(queries, keys_t, values_t, layout, line, key_extra, query_bins)
    residual = layer_input + dot_f32(heads_out, w_output, 0, 0)
    scale_second = inverse_rms(residual)
    normed_second = (residual * scale_second * gain_second).astype(BF16)
    gate = dot_f32(normed_second, w_gate, 1, 1)
    up = dot_f32(normed_second, w_up, 1, 1)
    gelu_value, gelu_pull = jax.vjp(lambda v: jax.nn.gelu(v, approximate=True), gate)
    activated = (gelu_value * up).astype(BF16)
    layer_output = residual + dot_f32(activated, w_down, 1, 0)

    out_low = cotangent.astype(BF16)
    down_full = dot_f32(activated, out_low, 0, 0).astype(BF16)
    act_grad = dot_f32(out_low, w_down, 1, 1)
    gate_low = gelu_pull(act_grad * up)[0].astype(BF16)
    up_low = (act_grad * gelu_value).astype(BF16)
    gate_full = dot_f32(gate_low, normed_second, 0, 0).astype(BF16)
    up_full = dot_f32(up_low, normed_second, 0, 0).astype(BF16)
    second_grad = dot_f32(gate_low, w_gate, 1, 0) + dot_f32(up_low, w_up, 1, 0)
    gain_second_grad = jnp.sum(second_grad * residual * scale_second, axis=0)
    scaled = gain_second * second_grad
    residual_grad = (
        cotangent
        + scale_second * scaled
        - residual * scale_second**3 * jnp.mean(scaled * residual, axis=-1, keepdims=True)
    )

    branch_low = residual_grad.astype(BF16)
    output_full = dot_f32(heads_out, branch_low, 1, 0).astype(BF16)
    heads_grad = dot_f32(w_output, branch_low, 1, 1).astype(BF16)
    dq, dk, dv, line_grad, layout_grad = attend_back(
        queries, keys_t, values_t, heads_out, heads_grad, lse, layout, line,
        key_extra, key_extra_t, query_bins, query_bins_t,
    )
    query_full = dot_f32(dq, normed, 1, 0).astype(BF16)
    key_full = dot_f32(dk, slot_normed, 1, 0).astype(BF16)
    value_full = dot_f32(dv, slot_normed, 1, 0).astype(BF16)
    slot_grad = dot_f32(dk, w_key, 0, 0) + dot_f32(dv, w_value, 0, 0)
    first_grad = lax.psum_scatter(
        slot_grad.astype(BF16), "mp", scatter_dimension=0, tiled=True, axis_index_groups=groups
    ).astype(F32) + dot_f32(dq, w_query, 0, 0)
    gain_first_grad = jnp.sum(first_grad * layer_input * scale_first, axis=0)
    scaled = gain_first * first_grad
    input_grad = (
        residual_grad
        + scale_first * scaled
        - layer_input * scale_first**3 * jnp.mean(scaled * layer_input, axis=-1, keepdims=True)
    )

    gain_grad = lax.psum_scatter(
        jnp.stack([gain_first_grad, gain_second_grad]), ("dp", "mp"), scatter_dimension=1, tiled=True
    )
    line_part = jnp.dot(
        onehot_line.T, line_grad[:, 0].T, precision=lax.Precision.HIGHEST
    )
    x_part = jnp.einsum(
        "ban,hba->nh", onehot_bin, layout_grad[:, :64, :64], precision=lax.Precision.HIGHEST
    )
    y_part = jnp.einsum(
        "ban,hba->nh", onehot_bin, layout_grad[:, 64:, 64:], precision=lax.Precision.HIGHEST
    )
    table_full = jnp.stack([line_part, x_part, y_part])
    table_grad = lax.psum_scatter(
        lax.psum_scatter(table_full, "mp", scatter_dimension=2, tiled=True),
        "dp", scatter_dimension=1, tiled=True,
    )

    query_grad = scatter_grad(query_full).T.astype(F32)
    key_value_grad = jnp.stack(
        [scatter_grad(key_full).T, scatter_grad(value_full).T], axis=1
    ).astype(F32)
    output_grad = scatter_grad(output_full).astype(F32)
    gate_up_grad = jnp.stack(
        [scatter_grad(gate_full).T, scatter_grad(up_full).T], axis=1
    ).astype(F32)
    down_grad = scatter_grad(down_full).astype(F32)
    return (
        layer_output, input_grad, gain_grad, query_grad, key_value_grad,
        output_grad, gate_up_grad, down_grad, table_grad,
    )


def per_device_linked(
    dp_size, mp_size,
    layer_input, norm_gains, query_weight, key_value_weight, output_weight,
    gate_up_weight, down_weight, bias_tables, doc_lengths, box_bins, cotangent,
):
    rows, model_width = layer_input.shape
    doc_count = doc_lengths.shape[0]
    slot_span = box_bins.shape[1] // doc_count
    group = mp_size // doc_count
    dp_index, mp_index = lax.axis_index("dp"), lax.axis_index("mp")
    doc = mp_index // group
    first_row = (mp_index % group) * rows
    key_blocks = slot_span // LANES
    width = LANES * (key_blocks + rows // LANES)
    heads_here = bias_tables.shape[2]
    head_count = heads_here * mp_size
    gain_second = norm_gains[1:2].astype(F32)

    column = ((dp_index % 2) * 4 + dp_index // 2) * LANES
    piece = lambda weight, axis: lax.dynamic_slice_in_dim(weight, column, LANES, axis)
    key_value_piece = jnp.transpose(piece(key_value_weight, 0), (1, 2, 0))
    pieces = [
        jnp.stack(
            [
                piece(query_weight, 0).T, key_value_piece[0], key_value_piece[1], piece(output_weight, 1)
            ]
        ),
        jnp.transpose(piece(gate_up_weight, 0), (1, 2, 0)),
        piece(down_weight, 1)[None],
    ]
    table = jnp.swapaxes(bias_tables.astype(F32), 1, 2)
    table = jnp.pad(table, ((0, 0), (0, 8 - heads_here), (0, LANES - 32))).reshape(24, LANES)

    onehot_line = line_onehot(first_row, width, key_blocks)
    line_hot = jnp.pad(onehot_line.T, ((0, LANES - 32), (0, 0))).astype(BF16)
    place = jnp.arange(LANES, dtype=jnp.int32)
    place = jnp.where(place < NBIN, place, place - LANES)
    bin_hot = (bucket_of(-place)[None, :] == jnp.arange(LANES, dtype=jnp.int32)[:, None]).astype(BF16)
    key_bins = lax.dynamic_slice(box_bins, (0, doc * slot_span), (2, slot_span))
    length = lax.dynamic_index_in_dim(doc_lengths, doc, keepdims=False)
    masked = jnp.arange(slot_span, dtype=jnp.int32)[None, :] >= length
    key_info = jnp.concatenate(
        [key_bins.astype(F32), jnp.where(masked, NEG_FILL, 0.0), jnp.zeros((5, slot_span), F32)]
    )

    scale_first = inverse_rms(layer_input)
    normed_t = (layer_input * scale_first * norm_gains[0].astype(F32)).astype(BF16).T
    (
        w_first, queries, keys_t, values_t, heads_out, lse, layout, line, key_extra, key_extra_t,
        slot_owner, residual, layer_output, second_grad, gate_up_full, down_full, _,
    ) = forward(
        mp_size, group, pieces, normed_t, table, key_info, line_hot, bin_hot, layer_input,
        gain_second, cotangent,
    )
    input_grad, small, gate_up_sum, down_sum, summed = backward(
        mp_size, group, gate_up_full, down_full, w_first, queries, keys_t, values_t, heads_out,
        residual, second_grad, cotangent, lse, layout, line, key_extra, key_extra_t, slot_owner,
        layer_input, norm_gains.astype(F32), line_hot, bin_hot,
    )
    gain_rows = model_width // LANES
    gains = small[: 2 * gain_rows].reshape(2, model_width)
    share = model_width // (dp_size * mp_size)
    at = (dp_index * mp_size + mp_index) * share
    gain_grad = lax.dynamic_slice(gains, (0, at), (2, share))
    tables = small[2 * gain_rows :].reshape(3, head_count, LANES)
    table_grad = lax.dynamic_slice(
        tables,
        (0, mp_index * heads_here, dp_index * (32 // dp_size)),
        (3, heads_here, 32 // dp_size),
    )
    table_grad = jnp.swapaxes(table_grad, 1, 2)
    query_grad = summed[0].T
    key_value_grad = jnp.transpose(summed[1:3], (2, 0, 1))
    gate_up_grad = jnp.transpose(gate_up_sum, (2, 0, 1))
    return (
        layer_output, input_grad, gain_grad, query_grad, key_value_grad,
        summed[3], gate_up_grad, down_sum[0], table_grad,
    )


def per_device(dp_size, mp_size, *args):
    rows, model_width = args[0].shape
    heads_here = args[7].shape[2]
    fits = dp_size == 8 and model_width == 8 * LANES and mp_size == 4
    fits = fits and heads_here <= 8 and rows % LANES == 0
    body = per_device_linked if fits else per_device_plain
    return body(dp_size, mp_size, *args)


def solution(mesh):
    return jax.shard_map(
        partial(per_device, mesh.shape["dp"], mesh.shape["mp"]),
        mesh=mesh,
        in_specs=(
            P(("dp", "mp"), None),
            P(),
            P(None, "mp"),
            P(None, None, "mp"),
            P("mp", None),
            P(None, None, "mp"),
            P("mp", None),
            P(None, None, "mp"),
            P("dp"),
            P(None, "dp"),
            P(("dp", "mp"), None),
        ),
        out_specs=(
            P(("dp", "mp"), None),
            P(("dp", "mp"), None),
            P(None, ("dp", "mp")),
            P("dp", "mp"),
            P("dp", None, "mp"),
            P("mp", "dp"),
            P("dp", None, "mp"),
            P("mp", "dp"),
            P(None, "dp", "mp"),
        ),
        check_vma=False,
    )
```

time: 510 us -> 353 us (0.69); the launches traced: 503 us -> 353 us
  matrix products: 89.2 us -> 0 us
  local copies, waits for them, and re-layouts: 44.7 us -> 21 us
  other arithmetic: 25.1 us -> 6.59 us
  Pallas kernels: 342 us -> 324 us
    dot_general x27 -> x0, matrix products: 89.2 us -> none  [the longest x21 82.2 us: dot_f32(): lax.dot_general(left, right, (((left_dim,), (right_dim,)), ((), ())), pre...]
    pallas_call x4 -> x2, Pallas kernels: 342 us -> 324 us  [the longest x1 181 us: forward(): pl.pallas_call(partial(forward_kernel, mp_size, group), out_shape=tuple((...]
    another operation x4 -> x1, other arithmetic: 13.5 us -> 0.74 us  [per_device_linked(): jnp.stack([piece(query_weight, 0).T, key_value_piece[0], key_value_piece[...]
    unnamed x108 -> x34, local copies, waits for them, and re-layouts: 21.1 us -> 10.9 us
    reshape x14 -> x1, local copies, waits for them, and re-layouts: 8.86 us -> 0.01 us  [per_device_linked(): gains = small[:2 * gain_rows].reshape(2, model_width)]
where the time goes in v2:
time: 353 us
  Pallas kernels  324 us (92%)
  local copies, waits for them, and re-layouts  21 us (6%)
  other arithmetic  6.59 us (2%)
    pallas_call x1, Pallas kernels, forward(): pl.pallas_call(partial(forward_kernel, mp_size, group), out_shape=tuple((...  181 us
    pallas_call x1, Pallas kernels, backward(): pl.pallas_call(partial(backward_kernel, mp_size, group), out_shape=(shape...  144 us
    unnamed x34, local copies, waits for them, and re-layouts  10.9 us

profile of v2, /device:TPU:0, one launch (start us, length us, event | category | flops | bytes accessed | tf_op | source)
XLA Modules:
  0.0 352.8 jit_solution(9437469955549437666)
XLA Ops:
  0.6 0.0 copy-start
  0.7 0.0 copy-start.1
  0.7 1.0 copy-done
  1.7 1.0 constant_dynamic-slice_fusion.2
  2.7 0.1 copy.27
  2.9 0.9 constant_dynamic-slice_fusion.3
  3.7 0.1 copy.26
  3.8 0.7 pad_maximum_fusion.first_ref
  4.6 1.7 dynamic-slice_bitcast_fusion.gate_up_ref
  6.3 1.6 dynamic-slice_bitcast_fusion.1.down_ref
  7.9 0.0 copy-done.1
  7.9 0.0 copy-start.7
  7.9 1.6 copy.22
  9.5 0.0 copy-done.7
  9.5 0.0 copy-start.2
  9.5 0.6 slice_convert_fusion
  10.1 0.2 multiply_reduce_fusion
  10.3 0.0 copy-start.10
  10.3 0.0 copy-start.11
  10.3 0.0 copy-start.9
  10.4 0.6 copy-done.2
  11.0 1.1 fusion.normed_t_ref
  12.0 0.0 copy-done.10
  12.0 0.6 bitcast_convert_fusion.table_ref
  12.7 0.0 copy-done.11
  12.7 0.6 dynamic_slice.34
  13.2 0.7 compare_select_fusion.1
  13.9 0.0 copy-done.9
  13.9 0.1 pad.17.clone
  14.0 0.7 maximum_maximum_fusion.key_info_ref
  14.8 0.7 convert_convert_fusion.line_hot_ref.refs_18_
  15.5 0.6 fusion.1.bin_hot_ref.refs_19_
  16.1 180.8 %forward.1 = (bf16[4,1024,1024]{2,1,0:T(8,128)(2,1)}, bf16[1024,384]{1,0:T(8,128)(2,1)}, bf16[1024,768]{1,0:T(8,128)(2,1)}, bf16[1024,768]{1,0:T(8,128)(2,1)}, b...) custom-call(bf16[4,256,128]{2,1,0:T(8,128)(2,1)} %pad_maximum_fusion, ...), custom_call_target="tpu_custom_call" | custom-call | tf_op jit(solution)/shard_map/forward/pallas_call | solution.py:987
  196.9 0.6 convert_element_type.180.refs_17_
  197.5 143.6 %backward.1 = (f32[384,1024]{1,0:T(8,128)}, f32[64,128]{1,0:T(8,128)}, f32[2,704,128]{2,1,0:T(8,128)}, f32[1,704,128]{2,1,0:T(8,128)}, f32[4,256,128]{2,1,0:T(8,128)}) custom-call(bf16[2,2816,1024]{2,1,0:T(8,128)(2,1)} %get-tuple-element.31.refs_0_, bf16[1,2816,1024]{2,1,0:T(8,128)(2,1)} %get-tuple-element.32.refs_1_, ...), custom_call_target="tpu_custom_call" | custom-call | tf_op jit(solution)/shard_map/backward/pallas_call | solution.py:1373
  341.2 0.0 copy-start.8
  341.2 0.0 copy-start.3
  341.2 0.8 slice.26
  342.0 0.6 constant_dynamic-slice_fusion.1
  342.6 1.6 slice_bitcast_fusion.1
  344.3 0.8 copy.24
  345.0 1.0 slice_bitcast_fusion
  346.0 0.8 copy.25
  346.9 0.0 copy-done.8
  346.9 0.1 constant_dynamic-slice_fusion
  346.9 0.7 copy.28
  347.6 0.0 copy-done.3
  347.6 0.0 copy-start.4
  347.6 1.1 copy.33
  348.8 0.8 copy-done.4
  349.6 0.0 copy-start.5
  349.6 0.0 copy-start.6
  349.6 1.1 copy.34
  350.8 0.5 copy-done.5
  351.2 0.9 copy.35
  352.1 0.0 copy-done.6
  352.1 0.7 copy.36
  (9 shorter events, 0.1 us)
Async XLA Ops:
  0.6 1.0 copy-start
  0.7 7.3 %copy-start.1 = (f32[384,1024]{1,0:T(8,128)S(1)}, f32[384,1024]{1,0:T(8,128)}, u32[]{:S(2)}) copy-start(f32[384,1024]{1,0:T(8,128)} %refs_16_.1) | copy-start | bytes 4718596
  7.9 1.6 copy-start.7
  9.5 1.4 copy-start.2
  10.3 1.7 copy-start.10
  10.3 2.3 copy-start.11
  10.3 3.6 %copy-start.9 = (s32[2,1536]{1,0:T(2,128)S(1)}, s32[2,1536]{1,0:T(2,128)}, u32[]{:S(2)}) copy-start(s32[2,1536]{1,0:T(2,128)} %param.20) | copy-start | bytes 36868
  341.2 5.7 %copy-start.8 = (f32[64,128]{1,0:T(8,128)S(1)}, f32[64,128]{1,0:T(8,128)}, u32[]{:S(2)}) copy-start(f32[64,128]{1,0:T(8,128)} %get-tuple-element.47) | copy-start | bytes 98308
  341.2 6.5 %copy-start.3 = (f32[384,1024]{1,0:T(8,128)S(1)}, f32[384,1024]{1,0:T(8,128)}, u32[]{:S(2)}) copy-start(f32[384,1024]{1,0:T(8,128)} %get-tuple-element.73) | copy-start | bytes 4718596
  347.6 2.0 copy-start.4
  349.6 1.6 copy-start.5
  349.6 2.5 copy-start.6

commit v3 on v2

--- a/solution.py
+++ b/solution.py
@@ -192,6 +192,7 @@
         self.to_core = (self.dp + 1 - 2 * self.core, self.mp)
         self.to_x = (self.dp + 2 - 4 * self.x, self.mp)
         self.to_y = (self.dp + 4 - 8 * self.y, self.mp)
+        self.to_corner = (self.dp + 6 - 4 * self.x - 8 * self.y, self.mp)
 
     def to_mp(self, step):
         return (self.dp, lax.rem(self.mp + step, self.mp_size))
@@ -201,7 +202,7 @@
 
     def partners(self):
         others = [self.to_mp(step) for step in range(1, self.mp_size)]
-        return [self.to_core, self.to_x, self.to_y] + others
+        return [self.to_core, self.to_x, self.to_y, self.to_corner] + others
 
 
 def meet(place):
@@ -313,27 +314,32 @@
         third = [copy(5, None, base, 4, place.to_core)]
         return first, second, third
 
+    def first(self, t):
+        c, k = self.items[t]
+        if k == 0:
+            self.own(c).wait()
+        else:
+            self.along_mp(c, k).wait_recv()
+        for copy in self.copies(t)[0]:
+            copy.start()
+
     def step(self, s):
         count = len(self.items)
-        if 0 <= s - 2 < count:
-            _, second, third = self.copies(s - 2)
-            for copy in second:
-                copy.wait_recv()
-            third[0].start()
+        if s == 0:
+            self.first(0)
         if 0 <= s - 1 < count:
             first, second, _ = self.copies(s - 1)
             for copy in first:
                 copy.wait_recv()
             for copy in second:
                 copy.start()
-        if s < count:
-            c, k = self.items[s]
-            if k == 0:
-                self.own(c).wait()
-            else:
-                self.along_mp(c, k).wait_recv()
-            for copy in self.copies(s)[0]:
-                copy.start()
+        if s + 1 < count:
+            self.first(s + 1)
+        if 0 <= s - 2 < count:
+            _, second, third = self.copies(s - 2)
+            for copy in second:
+                copy.wait_recv()
+            third[0].start()
 
     def done(self, t):
         self.copies(t)[2][0].wait_recv()
@@ -723,36 +729,10 @@
     gather.step(2)
 
     head_units = mp_size * heads_here
-    plan = {}
-    total = gather.steps
-    for k in range(1, mp_size):
-        need = at[(0, k)] + 2
-        plan.setdefault((k * heads_here, 0), []).append(need)
-    for k in range(mp_size):
-        need = at[(2, k)] + 2
-        plan.setdefault((head_units + k, 0), []).append(need)
-    table = {}
-    done = 2
-    order = sorted(plan.items())
-    for (unit, point), needs in order:
-        need = max(needs)
-        if need <= done:
-            continue
-        missing = list(range(done + 1, need + 1))
-        spots = [(unit, 0)]
-        if unit >= head_units:
-            before = [(unit - 1, p) for p in (3, 2, 1)] if unit > head_units else []
-            if unit == head_units:
-                before = [(unit - 1, 0), (unit - 2, 0), (unit - 3, 0)]
-        else:
-            before = [(unit - 1, 0), (unit - 2, 0), (unit - 3, 0)]
-        spots = spots + before
-        for i, s in enumerate(reversed(missing)):
-            table.setdefault(spots[min(i, len(spots) - 1)], []).append(s)
-        done = need
-    for spot in table:
-        table[spot].sort()
-    rest = list(range(done + 1, total))
+    table = {
+        (2, 0): [3], (4, 0): [4, 5], (6, 0): [6], (8, 0): [7], (12, 0): [8], (14, 0): [9],
+        (16, 2): [10], (17, 1): [11], (18, 2): [12], (19, 0): [13],
+    }
 
     def communicate(unit, point):
         for (at_unit, at_point), steps in table.items():
@@ -940,8 +920,6 @@
 
     lax.fori_loop(0, mp_size, hidden_unit, 0)
     layer_output[...] = layer_output[...] + residual[...]
-    for s in rest:
-        gather.step(s)
     for copy in store(mp_size - 1):
         copy.wait()
     gather.close()
@@ -1107,7 +1085,7 @@
         return total + product[0:8] + product[8:16]
 
     total = lax.fori_loop(0, rows // 16, norm_back, jnp.zeros((8, model_width), F32))
-    gain_part[1:2, :] = jnp.sum(total, axis=0, keepdims=True)
+    gain_part[...] = jnp.sum(total, axis=0, keepdims=True)
     scatter.step(1)
     branch_t[...] = branch_owner[...].T
     parts = [branch_owner[:, b * LANES : (b + 1) * LANES] for b in range(model_width // LANES)]
@@ -1118,14 +1096,11 @@
     own_grad[...] = jnp.zeros_like(own_grad)
     scatter.step(2)
 
-    plan = {}
-    for block in range(mp_size - 1):
-        plan[(block, 1)] = [3 * block + 3]
-        plan[(block, 2)] = [3 * block + 4]
-        if block + 2 < mp_size:
-            plan[(block + 1, 0)] = [3 * block + 5]
-    done = 3 * mp_size - 1
-    plan[(mp_size - 1, 2)] = [done]
+    plan = {
+        (0, 2): [3], (0, 4): [4], (1, 2): [5], (1, 4): [6], (2, 2): [7], (2, 3): [8], (2, 4): [9],
+        (3, 2): [10], (3, 4): [11],
+    }
+    done = 11
 
     def communicate(block, point):
         for (at_block, at_point), steps in plan.items():
@@ -1177,6 +1152,12 @@
         ).astype(BF16)
 
         def head_unit(inside, inner_carry):
+            for point in range(1, heads_here):
+
+                @pl.when(inside == point)
+                def _(point=point):
+                    communicate(block, point)
+
             head = target * heads_here + inside
             some = pl.ds(pl.multiple_of(inside * 64, 16), 64)
             q_head, k_head, v_head = q_here[some, :], k_here[some, :], v_here[some, :]
@@ -1248,10 +1229,7 @@
             line_sums[pl.ds(head, 1), :] = unskewed(strip_grad, 0, LANES, 0)
             return inner_carry
 
-        half_heads = heads_here // 2
-        lax.fori_loop(0, half_heads, head_unit, 0)
-        communicate(block, 1)
-        lax.fori_loop(half_heads, heads_here, head_unit, 0)
+        lax.fori_loop(0, heads_here, head_unit, 0)
         full_here[slot, 0] = jnp.dot(
             dq_here[...], slot_owner[pl.ds(own_start, rows), :], preferred_element_type=F32
         ).astype(BF16)
@@ -1267,7 +1245,7 @@
         own_grad[...] = own_grad[...] + jnp.dot(
             dq_here[...].T, w_query[...], preferred_element_type=F32
         )
-        communicate(block, 2)
+        communicate(block, heads_here)
         return carry
 
     lax.fori_loop(0, mp_size, block_unit, 0)
@@ -1294,12 +1272,65 @@
     for i in range(2):
         start = 2 * gain_rows + (1 + i) * head_count
         stage[0, start : start + head_count, :] = exact_dot(bin_sums[i], bin_hot[...])
-    for s in steps[1:2]:
-        scatter.step(s)
+    for block in range(gain_rows):
+        these = slice(block * LANES, (block + 1) * LANES)
+        owner = block_owner(block)
+        those = slice(owner * LANES, (owner + 1) * LANES)
+
+        def gain_sum(i, total, these=these, those=those):
+            here = pl.ds(pl.multiple_of(i * 64, 64), 64)
+            product = slot_grad[here, these] * slot_owner[here, those].astype(F32)
+            return total + jnp.sum(product.reshape(8, 8, LANES), axis=0)
+
+        def own_sum(i, total, these=these, those=those):
+            here = pl.ds(pl.multiple_of(i * 64, 64), 64)
+            there = pl.ds(pl.multiple_of(own_start + i * 64, 64), 64)
+            product = own_grad[here, these] * slot_owner[there, those].astype(F32)
+            return total + jnp.sum(product.reshape(8, 8, LANES), axis=0)
+
+        total = lax.fori_loop(0, keys // 64, gain_sum, jnp.zeros((8, LANES), F32))
+        total = lax.fori_loop(0, rows // 64, own_sum, total)
+        stage[0, block : block + 1, :] = (
+            jnp.sum(total, axis=0, keepdims=True) / gains[0:1, these]
+        )
+        stage[0, gain_rows + block : gain_rows + block + 1, :] = gain_part[:, these]
+
+    rounds = [[place.to_core], [place.to_x, place.to_y, place.to_corner]]
+    rounds.append([place.to_mp(k) for k in range(1, mp_size)])
+    at, sums = 0, []
+    for i, partners in enumerate(rounds):
+        sums.append(
+            [
+                remote(
+                    stage.at[i], stage_in.at[at + j], stage_send.at[at + j], stage_recv.at[at + j], partner
+                )
+                for j, partner in enumerate(partners)
+            ]
+        )
+        at += len(partners)
+    at = 0
+    steps = steps[1:]
+    for i, group_sums in enumerate(sums):
+        for copy in group_sums:
+            copy.start()
+        for s in steps[:1]:
+            scatter.step(s)
+        steps = steps[1:]
+        for copy in group_sums:
+            copy.wait_recv()
+        value = stage[i]
+        for j in range(len(group_sums)):
+            value = value + stage_in[at + j]
+        at += len(group_sums)
+        if i + 1 < len(sums):
+            stage[i + 1] = value
+        else:
+            small_out[...] = value
+    sums = sum(sums, [])
     for copy in copies:
         copy.wait_recv()
 
-    def input_back(i, total):
+    def input_back(i, carry):
         here = pl.ds(pl.multiple_of(i * 16, 16), 16)
         grad = own_grad[here, :] + slot_grad[pl.ds(pl.multiple_of(own_start + i * 16, 16), 16), :]
         for k in range(group - 1):
@@ -1311,38 +1342,9 @@
         input_grad[here, :] = (
             residual_grad[here, :] + scale * scaled - values * (scale * scale * scale * mean)
         )
-        product = grad * values * scale
-        return total + product[0:8] + product[8:16]
-
-    total = lax.fori_loop(0, rows // 16, input_back, jnp.zeros((8, model_width), F32))
-    gain_part[0:1, :] = jnp.sum(total, axis=0, keepdims=True)
-    for which in range(2):
-        for i in range(gain_rows):
-            row = which * gain_rows + i
-            stage[0, row : row + 1, :] = gain_part[which : which + 1, i * LANES : (i + 1) * LANES]
-
-    partners = [place.to_core, place.to_x, place.to_y]
-    bit = 1
-    while bit < mp_size:
-        flipped = place.mp + bit - 2 * bit * lax.rem(lax.div(place.mp, bit), 2)
-        partners.append((place.dp, flipped))
-        bit *= 2
-    sums = [
-        remote(stage.at[i], stage_in.at[i], stage_send.at[i], stage_recv.at[i], partner)
-        for i, partner in enumerate(partners)
-    ]
-    sums[0].start()
-    steps = steps[2:]
-    for i, copy in enumerate(sums):
-        for s in steps[:1]:
-            scatter.step(s)
-        steps = steps[1:]
-        copy.wait_recv()
-        if i + 1 < len(sums):
-            stage[i + 1] = stage[i] + stage_in[i]
-            sums[i + 1].start()
-        else:
-            small_out[...] = stage[i] + stage_in[i]
+        return carry
+
+    lax.fori_loop(0, rows // 16, input_back, 0)
     for s in steps:
         scatter.step(s)
     scatter.close()
@@ -1363,7 +1365,7 @@
     head_count = heads_here * mp_size
     hidden = down_full.shape[1] // mp_size
     sizes = [(2, hidden), (1, hidden), (4, inner_here)]
-    count = 3 + (mp_size - 1).bit_length()
+    count = 4 + mp_size - 1
     small_rows = 2 * model_width // LANES + 3 * head_count
     others = max(group - 1, 1)
     dma = pltpu.SemaphoreType.DMA
@@ -1408,10 +1410,10 @@
             pltpu.VMEM((LANES, LANES), F32),
             pltpu.VMEM((head_count, width), F32),
             pltpu.VMEM((2, head_count, LANES), F32),
-            pltpu.VMEM((2, model_width), F32),
+            pltpu.VMEM((1, model_width), F32),
             pltpu.VMEM((others, rows, model_width), BF16),
             pltpu.VMEM((others, rows, model_width), BF16),
-            pltpu.VMEM((count, small_rows, LANES), F32),
+            pltpu.VMEM((3, small_rows, LANES), F32),
             pltpu.VMEM((count, small_rows, LANES), F32),
             pltpu.VMEM((2, 4, inner_here, model_width), BF16),
             dma((6 + 2 * heads_here,)), dma((3,)), dma((group,)), dma((group,)),
@@ -1696,7 +1698,7 @@
     rows, model_width = args[0].shape
     heads_here = args[7].shape[2]
     fits = dp_size == 8 and model_width == 8 * LANES and mp_size == 4
-    fits = fits and heads_here <= 8 and rows % LANES == 0
+    fits = fits and heads_here == 4 and rows % LANES == 0
     body = per_device_linked if fits else per_device_plain
     return body(dp_size, mp_size, *args)
 

time: 353 us -> 322 us (0.912)
  Pallas kernels: 324 us -> 293 us
    pallas_call x1, Pallas kernels: 181 us -> 163 us  [forward(): pl.pallas_call(partial(forward_kernel, mp_size, group), out_shape=tuple((...]
    pallas_call x1, Pallas kernels: 144 us -> 130 us  [backward(): pl.pallas_call(partial(backward_kernel, mp_size, group), out_shape=(shape...]
where the time goes in v3:
time: 322 us
  Pallas kernels  293 us (91%)
  local copies, waits for them, and re-layouts  21 us (7%)
  other arithmetic  6.59 us (2%)
    pallas_call x1, Pallas kernels, forward(): pl.pallas_call(partial(forward_kernel, mp_size, group), out_shape=tuple((...  163 us
    pallas_call x1, Pallas kernels, backward(): pl.pallas_call(partial(backward_kernel, mp_size, group), out_shape=(shape...  130 us
    unnamed x34, local copies, waits for them, and re-layouts  10.9 us

profile of v3, /device:TPU:0, one launch (start us, length us, event | category | flops | bytes accessed | tf_op | source)
XLA Modules:
  0.0 321.7 jit_solution(4246073011794535508)
XLA Ops:
  0.6 0.0 copy-start
  0.7 0.0 copy-start.1
  0.7 1.0 copy-done
  1.7 1.0 constant_dynamic-slice_fusion.2
  2.7 0.1 copy.27
  2.9 0.9 constant_dynamic-slice_fusion.3
  3.7 0.1 copy.26
  3.8 0.7 pad_maximum_fusion.first_ref
  4.6 1.7 dynamic-slice_bitcast_fusion.gate_up_ref
  6.3 1.6 dynamic-slice_bitcast_fusion.1.down_ref
  7.9 0.0 copy-done.1
  7.9 0.0 copy-start.7
  7.9 1.6 copy.22
  9.5 0.0 copy-done.7
  9.5 0.0 copy-start.2
  9.5 0.6 slice_convert_fusion
  10.1 0.2 multiply_reduce_fusion
  10.3 0.0 copy-start.10
  10.3 0.0 copy-start.11
  10.3 0.0 copy-start.9
  10.4 0.6 copy-done.2
  11.0 1.1 fusion.normed_t_ref
  12.0 0.0 copy-done.10
  12.0 0.6 bitcast_convert_fusion.table_ref
  12.7 0.0 copy-done.11
  12.7 0.6 dynamic_slice.34
  13.2 0.7 compare_select_fusion.1
  13.9 0.0 copy-done.9
  13.9 0.1 pad.17.clone
  14.0 0.7 maximum_maximum_fusion.key_info_ref
  14.8 0.7 convert_convert_fusion.line_hot_ref.refs_18_
  15.5 0.6 fusion.1.bin_hot_ref.refs_19_
  16.1 163.1 %forward.1 = (bf16[4,1024,1024]{2,1,0:T(8,128)(2,1)}, bf16[1024,384]{1,0:T(8,128)(2,1)}, bf16[1024,768]{1,0:T(8,128)(2,1)}, bf16[1024,768]{1,0:T(8,128)(2,1)}, b...) custom-call(bf16[4,256,128]{2,1,0:T(8,128)(2,1)} %pad_maximum_fusion, ...), custom_call_target="tpu_custom_call" | custom-call | tf_op jit(solution)/shard_map/forward/pallas_call | solution.py:965
  179.2 0.6 convert_element_type.180.refs_17_
  179.8 130.2 %backward.1 = (f32[384,1024]{1,0:T(8,128)}, f32[64,128]{1,0:T(8,128)}, f32[2,704,128]{2,1,0:T(8,128)}, f32[1,704,128]{2,1,0:T(8,128)}, f32[4,256,128]{2,1,0:T(8,128)}) custom-call(bf16[2,2816,1024]{2,1,0:T(8,128)(2,1)} %get-tuple-element.31.refs_0_, bf16[1,2816,1024]{2,1,0:T(8,128)(2,1)} %get-tuple-element.32.refs_1_, ...), custom_call_target="tpu_custom_call" | custom-call | tf_op jit(solution)/shard_map/backward/pallas_call | solution.py:1375
  310.0 0.0 copy-start.8
  310.0 0.0 copy-start.3
  310.0 0.8 slice.26
  310.9 0.6 constant_dynamic-slice_fusion.1
  311.5 1.6 slice_bitcast_fusion.1
  313.1 0.8 copy.24
  313.9 1.0 slice_bitcast_fusion
  314.9 0.8 copy.25
  315.7 0.0 copy-done.8
  315.7 0.1 constant_dynamic-slice_fusion
  315.8 0.7 copy.28
  316.5 0.0 copy-done.3
  316.5 0.0 copy-start.4
  316.5 1.1 copy.33
  317.6 0.8 copy-done.4
  318.5 0.0 copy-start.5
  318.5 0.0 copy-start.6
  318.5 1.1 copy.34
  319.6 0.5 copy-done.5
  320.1 0.9 copy.35
  320.9 0.0 copy-done.6
  320.9 0.7 copy.36
  (9 shorter events, 0.1 us)
Async XLA Ops:
  0.6 1.0 copy-start
  0.7 7.3 %copy-start.1 = (f32[384,1024]{1,0:T(8,128)S(1)}, f32[384,1024]{1,0:T(8,128)}, u32[]{:S(2)}) copy-start(f32[384,1024]{1,0:T(8,128)} %refs_16_.1) | copy-start | bytes 4718596
  7.9 1.6 copy-start.7
  9.5 1.4 copy-start.2
  10.3 1.7 copy-start.10
  10.3 2.3 copy-start.11
  10.3 3.6 %copy-start.9 = (s32[2,1536]{1,0:T(2,128)S(1)}, s32[2,1536]{1,0:T(2,128)}, u32[]{:S(2)}) copy-start(s32[2,1536]{1,0:T(2,128)} %param.20) | copy-start | bytes 36868
  310.0 5.7 %copy-start.8 = (f32[64,128]{1,0:T(8,128)S(1)}, f32[64,128]{1,0:T(8,128)}, u32[]{:S(2)}) copy-start(f32[64,128]{1,0:T(8,128)} %get-tuple-element.47) | copy-start | bytes 98308
  310.0 6.5 %copy-start.3 = (f32[384,1024]{1,0:T(8,128)S(1)}, f32[384,1024]{1,0:T(8,128)}, u32[]{:S(2)}) copy-start(f32[384,1024]{1,0:T(8,128)} %get-tuple-element.73) | copy-start | bytes 4718596
  316.5 2.0 copy-start.4
  318.5 1.6 copy-start.5
  318.5 2.5 copy-start.6

commit v4 on v3

--- a/solution.py
+++ b/solution.py
@@ -194,23 +194,27 @@
         self.to_y = (self.dp + 4 - 8 * self.y, self.mp)
         self.to_corner = (self.dp + 6 - 4 * self.x - 8 * self.y, self.mp)
 
+    def across(self, step):
+        low = lax.rem(lax.rem(self.mp, 2) + step % 2, 2)
+        high = lax.rem(lax.div(self.mp, 2) + step // 2, 2)
+        return low + 2 * high
+
     def to_mp(self, step):
-        return (self.dp, lax.rem(self.mp + step, self.mp_size))
-
-    def from_mp(self, step):
-        return lax.rem(self.mp + self.mp_size - step, self.mp_size)
+        return (self.dp, self.across(step))
 
     def partners(self):
         others = [self.to_mp(step) for step in range(1, self.mp_size)]
         return [self.to_core, self.to_x, self.to_y, self.to_corner] + others
 
 
+def greet(place):
+    barrier = pltpu.get_barrier_semaphore()
+    for partner in place.partners():
+        pl.semaphore_signal(barrier, inc=1, device_id=partner, device_id_type=MESH)
+
+
 def meet(place):
-    barrier = pltpu.get_barrier_semaphore()
-    partners = place.partners()
-    for partner in partners:
-        pl.semaphore_signal(barrier, inc=1, device_id=partner, device_id_type=MESH)
-    pl.semaphore_wait(barrier, len(partners))
+    pl.semaphore_wait(pltpu.get_barrier_semaphore(), len(place.partners()))
 
 
 class Copy:
@@ -248,13 +252,10 @@
 
 
 class Gather:
-    LAGS = 2
-
-    def __init__(self, place, pieces, outs, sems, items=None):
+    def __init__(self, place, pieces, outs, sems, items):
         self.place, self.pieces, self.outs = place, pieces, outs
         self.z_send, self.z_recv, self.own_sem, self.send, self.recv = sems
-        self.items = items or [(c, k) for c in range(len(pieces)) for k in range(place.mp_size)]
-        self.steps = len(self.items) + self.LAGS
+        self.items = items
 
     @staticmethod
     def semaphores(count, mp_size):
@@ -283,20 +284,17 @@
     def along_mp(self, c, step):
         place = self.place
         block = place.core * 4 + place.y * 2 + place.x
+        source = place.across(2) if step == 3 else place.mp
+        window = self.window(c, source, None, block, 1)
         return remote(
-            self.pieces[c], self.window(c, place.mp, None, block, 1),
-            self.z_send.at[c, step], self.z_recv.at[c, step], place.to_mp(step),
+            window if step == 3 else self.pieces[c], window,
+            self.z_send.at[c, step], self.z_recv.at[c, step], place.to_mp(2 if step == 2 else 1),
         )
-
-    def start_chunk(self, c):
-        self.own(c).start()
-        for step in range(1, self.place.mp_size):
-            self.along_mp(c, step).start()
 
     def copies(self, t):
         c, k = self.items[t]
         place = self.place
-        source = place.from_mp(k)
+        source = place.across(k)
         base = place.core * 4
         mine = base + place.y * 2 + place.x
         turned = base + (1 - place.y) * 2 + place.x
@@ -320,26 +318,31 @@
             self.own(c).wait()
         else:
             self.along_mp(c, k).wait_recv()
+        if k == 2:
+            self.along_mp(c, 3).start()
         for copy in self.copies(t)[0]:
             copy.start()
 
-    def step(self, s):
-        count = len(self.items)
-        if s == 0:
-            self.first(0)
-        if 0 <= s - 1 < count:
-            first, second, _ = self.copies(s - 1)
-            for copy in first:
-                copy.wait_recv()
-            for copy in second:
-                copy.start()
-        if s + 1 < count:
-            self.first(s + 1)
-        if 0 <= s - 2 < count:
-            _, second, third = self.copies(s - 2)
-            for copy in second:
-                copy.wait_recv()
-            third[0].start()
+    def second(self, t):
+        first, second, _ = self.copies(t)
+        for copy in first:
+            copy.wait_recv()
+        for copy in second:
+            copy.start()
+
+    def third(self, t):
+        _, second, third = self.copies(t)
+        for copy in second:
+            copy.wait_recv()
+        third[0].start()
+
+    def run(self, ops):
+        for op in ops.split():
+            which, t = op[0], int(op[1:])
+            if which == "z":
+                self.along_mp(*self.items[t]).start()
+            else:
+                {"f": self.first, "s": self.second, "t": self.third}[which](t)
 
     def done(self, t):
         self.copies(t)[2][0].wait_recv()
@@ -380,7 +383,7 @@
         buffers = [scratch[i * count : (i + 1) * count] for i in range(5)]
         self.sums, self.from_first, self.from_second, self.from_mp, self.staged = buffers
         self.own_sem, self.send, self.recv = scratch[5 * count :]
-        self.steps = len(items) + 5
+        self.steps = len(items) + 8
 
     @staticmethod
     def scratch(shapes, whole, mp_size):
@@ -400,9 +403,9 @@
     def source(self, t):
         c, k = self.items[t]
         if not self.whole[c]:
-            return self.fulls[c].at[(k + self.place.mp_size - 1) % self.place.mp_size % 2]
+            return self.fulls[c].at[(k + 1) % 2]
         lead, n = self.size(c)
-        target = lax.rem(self.place.mp + k, self.place.mp_size)
+        target = self.place.across(k)
         return self.fulls[c].at[:, pl.ds(pl.multiple_of(target * n, 16), n), :]
 
     def from_core(self, t):
@@ -459,8 +462,8 @@
         third = None
         if k > 0:
             third = copy(
-                6, sums.at[:, :, lanes_at(place.y * 2 + place.x, 1)], self.from_mp[c].at[k],
-                place.to_mp(k),
+                6, sums.at[:, :, lanes_at(place.y * 2 + place.x, 1)], self.from_mp[c].at[k - 1],
+                place.to_mp(1 if k % 2 else 2),
             )
         return first, second, third
 
@@ -487,8 +490,8 @@
                 copy.start()
         if s < count and self.whole[self.items[s][0]]:
             self.own(s).start()
-        if 0 <= s - 2 < count:
-            t = s - 2
+        if 0 <= s - 3 < count:
+            t = s - 3
             c, k = self.items[t]
             lead, n = self.size(c)
             first, second, _ = self.copies(t)
@@ -503,8 +506,8 @@
             )
             for copy in second:
                 copy.start()
-        if 0 <= s - 3 < count:
-            t = s - 3
+        if 0 <= s - 5 < count:
+            t = s - 5
             c, k = self.items[t]
             lead, n = self.size(c)
             _, second, third = self.copies(t)
@@ -513,15 +516,24 @@
             sums, landing = self.sums[c].at[k], self.from_second[c].at[k]
             mine = lanes_at(place.y * 2 + place.x, 1)
             add_rows(sums, (lead, (0, n), mine), landing, (0, pl.ds(0, 128)))
-            if third is not None:
+            if k % 2:
                 third.start()
-        if 0 <= s - 5 < count:
-            t = s - 5
-            c, k = self.items[t]
-            third = self.copies(t)[2]
-            if third is not None:
-                third.wait_recv()
-            else:
+        if 0 <= s - 6 < count and self.items[s - 6][1] == 2:
+            c, k = self.items[s - 6]
+            lead, n = self.size(c)
+            self.copies(self.items.index((c, 3)))[2].wait_recv()
+            mine = lanes_at(place.y * 2 + place.x, 1)
+            add_rows(
+                self.sums[c].at[k], (lead, (0, n), mine), self.from_mp[c].at[2], (0, pl.ds(0, 128))
+            )
+            self.copies(s - 6)[2].start()
+        if 0 <= s - 8 < count:
+            c = self.items[s - 8][0]
+            steps = [k for which, k in self.items if which == c]
+            if self.items[s - 8][1] == steps[-1]:
+                for k in steps:
+                    if k in (1, 2):
+                        self.copies(self.items.index((c, k)))[2].wait_recv()
                 self.finish(c)
 
     def left(self, t):
@@ -530,7 +542,7 @@
     def close(self):
         for t, (c, k) in enumerate(self.items):
             first, second, third = self.copies(t)
-            if self.whole[c] or k in (0, self.place.mp_size - 1):
+            if self.whole[c] or k < 2:
                 self.from_core(t).wait_send()
             for copy in first + second:
                 copy.wait_send()
@@ -550,8 +562,8 @@
             here = pl.ds(pl.multiple_of(i * size, size), size)
             for part in range(lead):
                 total = sums[0, part, here, mine].astype(F32)
-                for k in range(1, place.mp_size):
-                    total = total + landing[k, part, here, :].astype(F32)
+                for k in (1, 2):
+                    total = total + landing[k - 1, part, here, :].astype(F32)
                 out[part, here, :] = total
             return carry
 
@@ -642,23 +654,20 @@
     )
 
 
-def forward_items(mp_size):
-    items = [(0, 0), (1, 0), (2, 0)] + [(0, k) for k in range(1, mp_size)]
-    for k in range(1, mp_size):
-        items += [(1, k), (2, k)]
-    return items
+FORWARD_ITEMS = [(0, 0), (1, 0), (2, 0), (0, 1), (0, 2), (0, 3), (1, 1), (2, 1), (1, 2), (2, 2), (1, 3), (2, 3)]
 
 
 def forward_kernel(
     mp_size, group,
-    first_ref, gate_up_ref, down_ref, normed_t_ref, table_ref, key_info_ref, line_hot_ref,
-    bin_hot_ref, input_ref, gain_ref, cotangent_ref,
-    w_first, queries, keys_t, values_t, heads_out, lse, layout, line, key_extra, key_extra_t,
-    slot_owner, residual, layer_output, second_grad, gate_up_full, down_full, tables,
-    slot_t, w_gate_up, w_down, first_here, key_aug, query_aug, strip, scores, probs,
+    query_ref, output_ref, gate_up_ref, down_ref, key_value_ref, table_ref, boxes_ref, lengths_ref,
+    input_ref, gain_ref, cotangent_ref,
+    w_first, queries_out, keys_out, values_out, heads_out_out, lse, layout, line, key_extra, key_extra_t,
+    slot_owner_out, residual_out, layer_output, second_grad, gate_up_full, down_full, tables,
+    line_hot, bin_hot, queries, keys_t, values_t, heads_out, slot_owner, residual,
+    first_ref, query_piece, normed_t, slot_t, w_gate_up, w_down, first_here, key_aug, query_aug, strip, scores, probs,
     second_t, second_owner, out_owner, out_t,
     hidden_a, hidden_b, hidden_c, act_t, low_t, stage_gate_up, stage_down,
-    row_send, row_recv, row_own, table_send, table_recv, table_own, load_sem, store_sem, *sems,
+    row_send, row_recv, row_own, table_send, table_recv, table_own, load_sem, store_sem, keep_sem, *sems,
 ):
     place = Place(mp_size)
     rows, model_width = input_ref.shape
@@ -668,19 +677,22 @@
     inner_here = first_ref.shape[1]
     heads_here = inner_here // 64
     hidden = gate_up_ref.shape[1]
+    doc = lax.div(place.mp, group)
     member = lax.rem(place.mp, group)
     first_peer = place.mp - member
     own_lanes = pl.ds(pl.multiple_of(member * rows, LANES), rows)
 
-    items = forward_items(mp_size)
+    items = FORWARD_ITEMS
+    column = lanes_at(place.core * 4 + place.y * 2 + place.x, 1)
     gather = Gather(
-        place, [first_ref, gate_up_ref, down_ref], [w_first, w_gate_up, w_down], sems, items
+        place, [first_ref, gate_up_ref.at[:, :, column], down_ref.at[:, :, column]],
+        [w_first, w_gate_up, w_down], sems, items
     )
     at = {item: t for t, item in enumerate(items)}
 
     row_copies = [
         remote(
-            normed_t_ref, slot_t.at[:, own_lanes], row_send.at[k], row_recv.at[k],
+            normed_t, slot_t.at[:, own_lanes], row_send.at[k], row_recv.at[k],
             (place.dp, first_peer + lax.rem(member + k, group)),
         )
         for k in range(1, group)
@@ -689,32 +701,67 @@
         remote(table_ref, tables.at[place.mp], table_send.at[k], table_recv.at[k], place.to_mp(k))
         for k in range(1, mp_size)
     ]
-    row_here = Copy(normed_t_ref, slot_t.at[:, own_lanes], row_own.at[0])
+    row_here = Copy(normed_t, slot_t.at[:, own_lanes], row_own.at[0])
     table_here = Copy(table_ref, tables.at[place.mp], table_own.at[0])
 
+    greet(place)
+    loads = [
+        Copy(query_ref.at[column, :], query_piece, load_sem.at[0]),
+        Copy(output_ref.at[:, column], first_ref.at[3], load_sem.at[1]),
+    ]
+    for copy in loads:
+        copy.start()
+    for c in range(1, 3):
+        gather.own(c).start()
+    table_here.start()
+    turned = key_value_ref[...].T
+    first_ref[1] = turned[0:inner_here]
+    first_ref[2] = turned[inner_here : 2 * inner_here]
+
+    def norm_into(values_ref, gain):
+        def body(i, carry):
+            here = pl.ds(pl.multiple_of(i * 16, 16), 16)
+            values = values_ref[here, :]
+            scale = lax.rsqrt(jnp.mean(values * values, axis=1, keepdims=True) + EPSILON)
+            second_owner[here, :] = (values * scale * gain).astype(BF16)
+            return carry
+
+        lax.fori_loop(0, rows // 16, body, 0)
+
+    norm_into(input_ref, gain_ref[0:1, :])
+    normed_t[...] = second_owner[...].T
     row_here.start()
-    table_here.start()
+    for copy in loads:
+        copy.wait()
+    first_ref[0] = query_piece[...].T
+    gather.own(0).start()
     meet(place)
-    gather.start_chunk(0)
-    for copy in table_copies + row_copies:
+    gather.run("f0 f1")
+    for copy in row_copies + table_copies:
         copy.start()
-    gather.start_chunk(1)
-    gather.start_chunk(2)
-    gather.step(0)
-
-    key_rows = row_ids((64, keys)).astype(F32)
-    x_place = jnp.where(key_rows == key_info_ref[0:1, :], 1.0, 0.0).astype(BF16)
-    y_place = jnp.where(key_rows == key_info_ref[1:2, :], 1.0, 0.0).astype(BF16)
+    gather.along_mp(0, 1).start()
+
+    key_rows = row_ids((64, keys))
+    key_bins = boxes_ref[:, pl.ds(pl.multiple_of(doc * keys, LANES), keys)]
+    x_place = jnp.where(key_rows == key_bins[0:1], 1.0, 0.0).astype(BF16)
+    y_place = jnp.where(key_rows == key_bins[1:2], 1.0, 0.0).astype(BF16)
     key_extra_t[0:64, :] = x_place
     key_extra_t[64:128, :] = y_place
-    tail = jnp.where(
-        key_rows == 0.0, key_info_ref[2:3, :], jnp.where(key_rows < 4.0, 1.0, 0.0)
-    ).astype(BF16)
+    mask = jnp.where(lane_ids((64, keys)) >= lengths_ref[doc], NEG_FILL, 0.0)
+    first_row = member * rows
+    spot = lane_ids((8, width))
+    spot = jnp.where(spot >= width - LANES, spot - width, spot)
+    bucket = bucket_of(LANES * (blocks - 1) - spot - first_row)[0:1]
+    line_hot[...] = jnp.where(row_ids((LANES, width)) == bucket, 1.0, 0.0).astype(BF16)
+    spot = lane_ids((8, LANES))
+    bucket = bucket_of(jnp.where(spot < NBIN, -spot, LANES - spot))[0:1]
+    bin_hot[...] = jnp.where(row_ids((LANES, LANES)) == bucket, 1.0, 0.0).astype(BF16)
+    tail = jnp.where(key_rows == 0, mask, jnp.where(key_rows < 4, 1.0, 0.0)).astype(BF16)
     turned = jnp.concatenate([jnp.zeros((64, keys), BF16), x_place, y_place, tail], axis=0).T
     key_extra[...] = turned
     key_aug[...] = turned
     query_aug[pl.ds(192, 64), :] = jnp.where(row_ids((64, rows)) == 0, 1.0, 0.0).astype(BF16)
-    gather.step(1)
+    gather.run("s0 f2")
     for block in range(model_width // LANES):
         owner = block_owner(block)
         out_owner[:, owner * LANES : (owner + 1) * LANES] = cotangent_ref[
@@ -726,28 +773,29 @@
     second_grad[...] = jnp.zeros_like(second_grad)
     row_here.wait()
     table_here.wait()
-    gather.step(2)
+    gather.run("s1 t0")
 
     head_units = mp_size * heads_here
     table = {
-        (2, 0): [3], (4, 0): [4, 5], (6, 0): [6], (8, 0): [7], (12, 0): [8], (14, 0): [9],
-        (16, 2): [10], (17, 1): [11], (18, 2): [12], (19, 0): [13],
+        (1, 0): "f3 z4 z6", (2, 0): "s3 s2 t1", (4, 0): "t3 f4 z7", (5, 0): "s4 t2", (6, 0): "f5 z8",
+        (7, 0): "t4 f6", (8, 0): "s5 z9", (9, 0): "f7 s6", (11, 0): "t5", (12, 0): "f8 s7", (13, 0): "t6",
+        (14, 0): "f9 s8", (16, 0): "f10 t7", (16, 2): "s9", (17, 0): "f11 t8", (17, 1): "s10",
+        (17, 3): "t9", (18, 0): "s11", (18, 3): "t10", (19, 0): "t11",
     }
 
     def communicate(unit, point):
-        for (at_unit, at_point), steps in table.items():
+        for (at_unit, at_point), ops in table.items():
             if at_point == point:
 
                 @pl.when(unit == at_unit)
-                def _(steps=steps):
-                    for s in steps:
-                        gather.step(s)
+                def _(ops=ops):
+                    gather.run(ops)
 
     def head_unit(unit, carry):
         communicate(unit, 0)
         step = lax.div(unit, heads_here)
         inside = lax.rem(unit, heads_here)
-        source = place.from_mp(step)
+        source = place.across(step)
         base = pl.multiple_of(source * inner_here, 16)
         head = source * heads_here + inside
 
@@ -767,8 +815,8 @@
             load = Copy(w_first.at[:, pl.ds(base, inner_here), :], first_here, load_sem.at[0])
             load.start()
             hot = tables[source].astype(BF16)
-            line[source] = jnp.dot(hot[0:8], line_hot_ref[...], preferred_element_type=F32)
-            bins = jnp.dot(hot[8:24], bin_hot_ref[...], preferred_element_type=F32)
+            line[source] = jnp.dot(hot[0:8], line_hot[...], preferred_element_type=F32)
+            bins = jnp.dot(hot[8:24], bin_hot[...], preferred_element_type=F32)
             for i in range(heads_here):
                 x_line = jnp.broadcast_to(bins[i : i + 1], (64, LANES))
                 y_line = jnp.broadcast_to(bins[8 + i : 9 + i], (64, LANES))
@@ -781,7 +829,7 @@
             load.wait()
             here = pl.ds(base, inner_here)
             queries[here, :] = jnp.dot(
-                first_here[0], normed_t_ref[...], preferred_element_type=F32
+                first_here[0], normed_t[...], preferred_element_type=F32
             ).astype(BF16)
             keys_t[here, :] = jnp.dot(
                 first_here[1], slot_t[...], preferred_element_type=F32
@@ -836,15 +884,18 @@
             block * LANES : (block + 1) * LANES, :
         ].T
 
-    def norm_rows(i, carry):
-        here = pl.ds(pl.multiple_of(i * 16, 16), 16)
-        values = residual[here, :]
-        scale = lax.rsqrt(jnp.mean(values * values, axis=1, keepdims=True) + EPSILON)
-        normed = (values * scale * gain_ref[...]).astype(BF16)
-        second_owner[here, :] = normed
-        return carry
-
-    lax.fori_loop(0, rows // 16, norm_rows, 0)
+    kept = [
+        Copy(here, there, keep_sem.at[i])
+        for i, (here, there) in enumerate(
+            [
+                (queries, queries_out), (keys_t, keys_out), (values_t, values_out),
+                (heads_out, heads_out_out), (slot_owner, slot_owner_out), (residual, residual_out),
+            ]
+        )
+    ]
+    for copy in kept:
+        copy.start()
+    norm_into(residual, gain_ref[1:2, :])
     second_t[...] = second_owner[...].T
     turned_blocks = [second_owner[:, b * LANES : (b + 1) * LANES] for b in range(model_width // LANES)]
     for block, values in enumerate(turned_blocks):
@@ -852,7 +903,7 @@
         second_owner[:, owner * LANES : (owner + 1) * LANES] = values
 
     def store(step):
-        source = place.from_mp(step)
+        source = place.across(step)
         here = pl.ds(pl.multiple_of(source * hidden, 16), hidden)
         return [
             Copy(stage_gate_up, gate_up_full.at[:, here, :], store_sem.at[0]),
@@ -862,7 +913,7 @@
     def hidden_unit(step, carry):
         unit = step + head_units
         communicate(unit, 0)
-        source = place.from_mp(step)
+        source = place.across(step)
         here = pl.ds(pl.multiple_of(source * hidden, 16), hidden)
         for k in range(mp_size):
 
@@ -925,18 +976,22 @@
     gather.close()
     for copy in row_copies + table_copies:
         copy.wait_send()
+    for copy in kept:
+        copy.wait()
 
 
 def block_owner(block):
     return (block % 2) * 4 + block // 2
 
 
-def forward(mp_size, group, pieces, normed_t, table, key_info, line_hot, bin_hot, layer_input, gain, cotangent):
-    first, gate_up, down = pieces
+def forward(
+    mp_size, group, query, output, gate_up, down, key_value, table, boxes, lengths, layer_input,
+    gains, cotangent,
+):
     rows, model_width = layer_input.shape
-    keys = key_info.shape[1]
-    width = line_hot.shape[1]
-    inner_here, hidden = first.shape[1], gate_up.shape[1]
+    keys = boxes.shape[1] // lengths.shape[0]
+    width = LANES * (keys // LANES + rows // LANES)
+    inner_here, hidden = query.shape[1], gate_up.shape[1]
     inner, total_hidden = inner_here * mp_size, hidden * mp_size
     head_count = inner // 64
     dma = pltpu.SemaphoreType.DMA
@@ -945,29 +1000,40 @@
     shape = jax.ShapeDtypeStruct
     out = [
         (shape((4, inner, model_width), BF16), hbm),
-        (shape((inner, rows), BF16), vmem),
-        (shape((inner, keys), BF16), vmem),
-        (shape((inner, keys), BF16), vmem),
-        (shape((inner, rows), BF16), vmem),
+        (shape((inner, rows), BF16), hbm),
+        (shape((inner, keys), BF16), hbm),
+        (shape((inner, keys), BF16), hbm),
+        (shape((inner, rows), BF16), hbm),
         (shape((head_count, 1, rows), F32), vmem),
         (shape((head_count, 128, 128), BF16), vmem),
         (shape((mp_size, 8, width), F32), vmem),
         (shape((keys, 256), BF16), vmem),
         (shape((128, keys), BF16), vmem),
-        (shape((keys, model_width), BF16), vmem),
-        (shape((rows, model_width), F32), vmem),
+        (shape((keys, model_width), BF16), hbm),
+        (shape((rows, model_width), F32), hbm),
         (shape((rows, model_width), F32), vmem),
         (shape((rows, model_width), F32), vmem),
         (shape((2, total_hidden, model_width), BF16), hbm),
         (shape((1, total_hidden, model_width), BF16), hbm),
         (shape((mp_size, 24, LANES), F32), vmem),
+        (shape((LANES, width), BF16), vmem),
+        (shape((LANES, LANES), BF16), vmem),
     ]
     return pl.pallas_call(
         partial(forward_kernel, mp_size, group),
         out_shape=tuple(o[0] for o in out),
-        in_specs=[hbm] * 3 + [vmem] * 8,
+        in_specs=[hbm] * 4 + [vmem] * 3 + [pl.BlockSpec(memory_space=pltpu.SMEM)] + [vmem] * 3,
         out_specs=tuple(o[1] for o in out),
         scratch_shapes=[
+            pltpu.VMEM((inner, rows), BF16),
+            pltpu.VMEM((inner, keys), BF16),
+            pltpu.VMEM((inner, keys), BF16),
+            pltpu.VMEM((inner, rows), BF16),
+            pltpu.VMEM((keys, model_width), BF16),
+            pltpu.VMEM((rows, model_width), F32),
+            pltpu.VMEM((4, inner_here, LANES), BF16),
+            pltpu.VMEM((LANES, inner_here), BF16),
+            pltpu.VMEM((model_width, rows), BF16),
             pltpu.VMEM((model_width, keys), BF16),
             pltpu.VMEM((2, total_hidden, model_width), BF16),
             pltpu.VMEM((1, total_hidden, model_width), BF16),
@@ -989,22 +1055,19 @@
             pltpu.VMEM((2, hidden, model_width), BF16),
             pltpu.VMEM((1, hidden, model_width), BF16),
             dma((group,)), dma((group,)), dma((1,)),
-            dma((mp_size,)), dma((mp_size,)), dma((1,)), dma((1,)), dma((2,)),
+            dma((mp_size,)), dma((mp_size,)), dma((1,)), dma((2,)), dma((2,)), dma((6,)),
         ]
         + Gather.semaphores(3, mp_size),
         compiler_params=pltpu.CompilerParams(
             collective_id=0, has_side_effects=True, vmem_limit_bytes=62 << 20
         ),
         name="forward",
-    )(first, gate_up, down, normed_t, table, key_info, line_hot, bin_hot, layer_input, gain, cotangent)
-
-
-def backward_items(mp_size):
-    order = list(range(1, mp_size)) + [0]
-    items = [(c, order[0]) for c in (0, 1)]
-    for last, k in zip(order, order[1:]):
-        items += [(0, k), (1, k), (2, last)]
-    return items + [(2, order[-1])]
+    )(
+        query, output, gate_up, down, key_value, table, boxes, lengths, layer_input, gains, cotangent,
+    )
+
+
+BACKWARD_ITEMS = [(0, 3), (1, 3), (0, 2), (1, 2), (2, 3), (0, 1), (2, 2), (1, 1), (0, 0), (1, 0), (2, 1), (2, 0)]
 
 
 def unskewed(values, first, count, shift):
@@ -1053,7 +1116,7 @@
     own_start = pl.multiple_of(member * rows, LANES)
     own_lanes = pl.ds(own_start, rows)
 
-    items = backward_items(mp_size)
+    items = BACKWARD_ITEMS
     fulls = [gate_up_full, down_full, full_here]
     scatter = Scatter(place, fulls, [gate_up_sum, down_sum, first_sum], refs, items)
 
@@ -1064,6 +1127,7 @@
     ]
     for copy in loads:
         copy.start()
+    greet(place)
     meet(place)
     scatter.step(0)
     key_aug[...] = key_extra[...]
@@ -1097,10 +1161,9 @@
     scatter.step(2)
 
     plan = {
-        (0, 2): [3], (0, 4): [4], (1, 2): [5], (1, 4): [6], (2, 2): [7], (2, 3): [8], (2, 4): [9],
-        (3, 2): [10], (3, 4): [11],
+        (0, 2): [3], (0, 4): [4], (1, 2): [5], (1, 4): [6], (2, 2): [7], (2, 4): [8], (3, 4): [9],
     }
-    done = 11
+    done = 9
 
     def communicate(block, point):
         for (at_block, at_point), steps in plan.items():
@@ -1113,8 +1176,8 @@
 
     def block_unit(block, carry):
         communicate(block, 0)
-        step = lax.rem(block + 1, mp_size)
-        target = lax.rem(place.mp + step, mp_size)
+        step = mp_size - 1 - block
+        target = place.across(step)
         base = pl.multiple_of(target * inner_here, 16)
         here = pl.ds(base, inner_here)
         slot = lax.rem(block, 2)
@@ -1137,19 +1200,21 @@
                 )
         for copy in copies:
             copy.start()
-        for copy in copies:
+        for copy in (copies[1], copies[5]):
             copy.wait()
 
         for b in range(2, mp_size):
 
             @pl.when(block == b)
             def _(b=b):
-                scatter.left(items.index((2, (b - 1) % mp_size)))
+                scatter.left(items.index((2, mp_size + 1 - b)))
 
         grad_here[...] = jnp.dot(w_output[...], branch_t[...], preferred_element_type=F32).astype(BF16)
         full_here[slot, 3] = jnp.dot(
             out_here[...], branch_owner[...], preferred_element_type=F32
         ).astype(BF16)
+        for copy in [copies[0]] + copies[2:5] + copies[6:]:
+            copy.wait()
 
         def head_unit(inside, inner_carry):
             for point in range(1, heads_here):
@@ -1308,25 +1373,29 @@
             ]
         )
         at += len(partners)
-    at = 0
     steps = steps[1:]
-    for i, group_sums in enumerate(sums):
-        for copy in group_sums:
-            copy.start()
-        for s in steps[:1]:
+
+    def advance(count):
+        nonlocal steps
+        for s in steps[:count]:
             scatter.step(s)
-        steps = steps[1:]
-        for copy in group_sums:
+        steps = steps[count:]
+
+    def round_done(i):
+        at = sum(len(partners) for partners in rounds[:i])
+        value = stage[i]
+        for j, copy in enumerate(sums[i]):
             copy.wait_recv()
-        value = stage[i]
-        for j in range(len(group_sums)):
             value = value + stage_in[at + j]
-        at += len(group_sums)
-        if i + 1 < len(sums):
-            stage[i + 1] = value
-        else:
-            small_out[...] = value
-    sums = sum(sums, [])
+        return value
+
+    for copy in sums[0]:
+        copy.start()
+    advance(2)
+    stage[1] = round_done(0)
+    for copy in sums[1]:
+        copy.start()
+    advance(2)
     for copy in copies:
         copy.wait_recv()
 
@@ -1345,6 +1414,13 @@
         return carry
 
     lax.fori_loop(0, rows // 16, input_back, 0)
+    advance(1)
+    stage[2] = round_done(1)
+    for copy in sums[2]:
+        copy.start()
+    advance(len(steps))
+    small_out[...] = round_done(2)
+    sums = sum(sums, [])
     for s in steps:
         scatter.step(s)
     scatter.close()
@@ -1621,57 +1697,28 @@
 ):
     rows, model_width = layer_input.shape
     doc_count = doc_lengths.shape[0]
-    slot_span = box_bins.shape[1] // doc_count
     group = mp_size // doc_count
     dp_index, mp_index = lax.axis_index("dp"), lax.axis_index("mp")
-    doc = mp_index // group
-    first_row = (mp_index % group) * rows
-    key_blocks = slot_span // LANES
-    width = LANES * (key_blocks + rows // LANES)
     heads_here = bias_tables.shape[2]
     head_count = heads_here * mp_size
-    gain_second = norm_gains[1:2].astype(F32)
-
+    inner_here = query_weight.shape[1]
+    gains = norm_gains.astype(F32)
     column = ((dp_index % 2) * 4 + dp_index // 2) * LANES
-    piece = lambda weight, axis: lax.dynamic_slice_in_dim(weight, column, LANES, axis)
-    key_value_piece = jnp.transpose(piece(key_value_weight, 0), (1, 2, 0))
-    pieces = [
-        jnp.stack(
-            [
-                piece(query_weight, 0).T, key_value_piece[0], key_value_piece[1], piece(output_weight, 1)
-            ]
-        ),
-        jnp.transpose(piece(gate_up_weight, 0), (1, 2, 0)),
-        piece(down_weight, 1)[None],
-    ]
+    key_value = lax.dynamic_slice_in_dim(key_value_weight, column, LANES, 0)
     table = jnp.swapaxes(bias_tables.astype(F32), 1, 2)
     table = jnp.pad(table, ((0, 0), (0, 8 - heads_here), (0, LANES - 32))).reshape(24, LANES)
-
-    onehot_line = line_onehot(first_row, width, key_blocks)
-    line_hot = jnp.pad(onehot_line.T, ((0, LANES - 32), (0, 0))).astype(BF16)
-    place = jnp.arange(LANES, dtype=jnp.int32)
-    place = jnp.where(place < NBIN, place, place - LANES)
-    bin_hot = (bucket_of(-place)[None, :] == jnp.arange(LANES, dtype=jnp.int32)[:, None]).astype(BF16)
-    key_bins = lax.dynamic_slice(box_bins, (0, doc * slot_span), (2, slot_span))
-    length = lax.dynamic_index_in_dim(doc_lengths, doc, keepdims=False)
-    masked = jnp.arange(slot_span, dtype=jnp.int32)[None, :] >= length
-    key_info = jnp.concatenate(
-        [key_bins.astype(F32), jnp.where(masked, NEG_FILL, 0.0), jnp.zeros((5, slot_span), F32)]
-    )
-
-    scale_first = inverse_rms(layer_input)
-    normed_t = (layer_input * scale_first * norm_gains[0].astype(F32)).astype(BF16).T
     (
         w_first, queries, keys_t, values_t, heads_out, lse, layout, line, key_extra, key_extra_t,
-        slot_owner, residual, layer_output, second_grad, gate_up_full, down_full, _,
+        slot_owner, residual, layer_output, second_grad, gate_up_full, down_full, _, line_hot, bin_hot,
     ) = forward(
-        mp_size, group, pieces, normed_t, table, key_info, line_hot, bin_hot, layer_input,
-        gain_second, cotangent,
+        mp_size, group, query_weight, output_weight, jnp.transpose(gate_up_weight, (1, 2, 0)),
+        down_weight[None], key_value.reshape(LANES, 2 * inner_here), table, box_bins, doc_lengths,
+        layer_input, gains, cotangent,
     )
     input_grad, small, gate_up_sum, down_sum, summed = backward(
         mp_size, group, gate_up_full, down_full, w_first, queries, keys_t, values_t, heads_out,
         residual, second_grad, cotangent, lse, layout, line, key_extra, key_extra_t, slot_owner,
-        layer_input, norm_gains.astype(F32), line_hot, bin_hot,
+        layer_input, gains, line_hot, bin_hot,
     )
     gain_rows = model_width // LANES
     gains = small[: 2 * gain_rows].reshape(2, model_width)

time: 322 us -> 282 us (0.88)
  Pallas kernels: 293 us -> 265 us
  local copies, waits for them, and re-layouts: 21 us -> 13.3 us
  other arithmetic: 6.59 us -> 2.57 us
    pallas_call x1, Pallas kernels: 163 us -> 135 us  [forward(): pl.pallas_call(partial(forward_kernel, mp_size, group), out_shape=tuple((...]
    unnamed x34 -> x18, local copies, waits for them, and re-layouts: 10.9 us -> 8.14 us
where the time goes in v4:
time: 282 us
  Pallas kernels  265 us (94%)
  local copies, waits for them, and re-layouts  13.3 us (5%)
    pallas_call x1, Pallas kernels, forward(): pl.pallas_call(partial(forward_kernel, mp_size, group), out_shape=tuple((...  135 us
    pallas_call x1, Pallas kernels, backward(): pl.pallas_call(partial(backward_kernel, mp_size, group), out_shape=(shape...  130 us
    unnamed x18, local copies, waits for them, and re-layouts  8.14 us

profile of v4, /device:TPU:0, one launch (start us, length us, event | category | flops | bytes accessed | tf_op | source)
XLA Modules:
  0.0 281.9 jit_solution(193169227240419198)
XLA Ops:
  0.7 1.0 constant_dynamic-slice_fusion.2
  1.7 0.7 copy.24
  2.3 1.3 bitcast_convert_fusion.table_ref
  3.6 1.3 convert_element_type.6.gain_ref.refs_17_
  4.9 135.4 %forward.1 = (bf16[4,1024,1024]{2,1,0:T(8,128)(2,1)}, bf16[1024,384]{1,0:T(8,128)(2,1)}, bf16[1024,768]{1,0:T(8,128)(2,1)}, bf16[1024,768]{1,0:T(8,128)(2,1)}, b...) custom-call(bf16[1024,256]{1,0:T(8,128)(2,1)} %query_ref.1, ...), custom_call_target="tpu_custom_call" | custom-call | tf_op jit(solution)/shard_map/forward/pallas_call | solution.py:1022
  140.3 129.9 %backward.1 = (f32[384,1024]{1,0:T(8,128)}, f32[64,128]{1,0:T(8,128)}, f32[2,704,128]{2,1,0:T(8,128)}, f32[1,704,128]{2,1,0:T(8,128)}, f32[4,256,128]{2,1,0:T(8,128)}) custom-call(bf16[2,2816,1024]{2,1,0:T(8,128)(2,1)} %get-tuple-element.33.refs_0_, bf16[1,2816,1024]{2,1,0:T(8,128)(2,1)} %get-tuple-element.34.refs_1_, ...), custom_call_target="tpu_custom_call" | custom-call | tf_op jit(solution)/shard_map/backward/pallas_call | solution.py:1451
  270.2 0.0 copy-start.4
  270.2 0.0 copy-start
  270.2 0.8 slice.15
  271.1 0.6 constant_dynamic-slice_fusion.1
  271.7 1.6 slice_bitcast_fusion.1
  273.3 0.8 copy.21
  274.1 1.0 slice_bitcast_fusion
  275.1 0.8 copy.22
  275.9 0.0 copy-done.4
  275.9 0.1 constant_dynamic-slice_fusion
  276.0 0.7 copy.23
  276.7 0.0 copy-done
  276.7 0.0 copy-start.1
  276.7 1.1 copy.29
  277.8 0.8 copy-done.1
  278.7 0.0 copy-start.2
  278.7 0.0 copy-start.3
  278.7 1.1 copy.30
  279.8 0.5 copy-done.2
  280.3 0.9 copy.31
  281.1 0.0 copy-done.3
  281.1 0.7 copy.32
  (2 shorter events, 0.0 us)
Async XLA Ops:
  270.2 5.7 %copy-start.4 = (f32[64,128]{1,0:T(8,128)S(1)}, f32[64,128]{1,0:T(8,128)}, u32[]{:S(2)}) copy-start(f32[64,128]{1,0:T(8,128)} %get-tuple-element.51) | copy-start | bytes 98308
  270.2 6.5 %copy-start = (f32[384,1024]{1,0:T(8,128)S(1)}, f32[384,1024]{1,0:T(8,128)}, u32[]{:S(2)}) copy-start(f32[384,1024]{1,0:T(8,128)} %get-tuple-element.75) | copy-start | bytes 4718596
  276.7 2.0 copy-start.1
  278.7 1.6 copy-start.2
  278.7 2.5 copy-start.3

commit v5 on v4

--- a/solution.py
+++ b/solution.py
@@ -376,26 +376,35 @@
 
 
 class Scatter:
-    def __init__(self, place, fulls, outs, scratch, items):
+    def __init__(self, place, fulls, outs, scratch, items, shares=None, inside=False):
+        self.inside = inside
         self.place, self.fulls, self.outs, self.items = place, fulls, outs, items
         count = len(fulls)
+        self.shares = shares or [None] * count
+        self.held = [sorted(k for c, k in items if c == which) for which in range(count)]
         self.whole = [len(full.shape) == 3 for full in fulls]
         buffers = [scratch[i * count : (i + 1) * count] for i in range(5)]
         self.sums, self.from_first, self.from_second, self.from_mp, self.staged = buffers
-        self.own_sem, self.send, self.recv = scratch[5 * count :]
-        self.steps = len(items) + 8
+        self.own_sem, self.send, self.recv, self.share_send, self.share_recv = scratch[5 * count :]
 
     @staticmethod
-    def scratch(shapes, whole, mp_size):
+    def scratch(shapes, whole, items):
         out = []
-        for blocks in (4, 2, 1, 1):
-            for lead, n in shapes:
-                out.append(pltpu.VMEM((mp_size, lead, n, blocks * LANES), BF16))
+        for part, blocks in enumerate((4, 2, 1, 1)):
+            for c, (lead, n) in enumerate(shapes):
+                slots = sum(which == c for which, _ in items)
+                if part == 3:
+                    slots, lead, n = (3, lead, n) if slots > 1 else (1, 1, 16)
+                out.append(pltpu.VMEM((slots, lead, n, blocks * LANES), BF16))
         for (lead, n), is_whole in zip(shapes, whole):
-            out.append(pltpu.VMEM((lead, n, 4 * LANES) if is_whole else (1, 8, LANES), BF16))
+            out.append(pltpu.VMEM((lead, n, 4 * LANES) if is_whole else (1, 16, LANES), BF16))
         dma = pltpu.SemaphoreType.DMA
-        count = len(shapes) * mp_size
-        return out + [dma((count,)), dma((count, 7)), dma((count, 7))]
+        count = len(items)
+        out += [dma((count,)), dma((count, 7)), dma((count, 7))]
+        return out + [dma((len(shapes),)), dma((len(shapes),))]
+
+    def slot(self, c, k):
+        return self.held[c].index(k)
 
     def size(self, c):
         return self.sums[c].shape[1], self.sums[c].shape[2]
@@ -412,7 +421,7 @@
         c, k = self.items[t]
         place = self.place
         return remote(
-            self.source(t).at[:, :, lanes_at((1 - place.core) * 4, 4)], self.sums[c].at[k],
+            self.source(t).at[:, :, lanes_at((1 - place.core) * 4, 4)], self.sums[c].at[self.slot(c, k)],
             self.send.at[t, 0], self.recv.at[t, 0], place.to_core,
         )
 
@@ -428,12 +437,12 @@
         lead, n = self.size(c)
         top, bottom = pl.ds(0, n // 2), pl.ds(n // 2, n // 2)
         every = pl.ds(0, lead)
-        sums = self.sums[c].at[k]
+        sums = self.sums[c].at[self.slot(c, k)]
 
         def copy(i, source, landing, partner):
             return remote(source, landing, self.send.at[t, i], self.recv.at[t, i], partner)
 
-        landing = self.from_first[c].at[k]
+        landing = self.from_first[c].at[self.slot(c, k)]
         first = [
             copy(
                 1, sums.at[every, top, lanes_at((1 - place.y) * 2, 2)],
@@ -448,7 +457,7 @@
                 landing.at[every, bottom, pl.ds(128, 128)], place.to_x,
             ),
         ]
-        landing = self.from_second[c].at[k]
+        landing = self.from_second[c].at[self.slot(c, k)]
         second = [
             copy(
                 4, sums.at[every, top, lanes_at(place.y * 2 + 1 - place.x, 1)],
@@ -467,74 +476,81 @@
             )
         return first, second, third
 
-    def step(self, s):
-        count = len(self.items)
+    def core(self, t):
+        self.from_core(t).start()
+        if self.whole[self.items[t][0]]:
+            self.own(t).start()
+
+    def first(self, t):
+        c, k = self.items[t]
+        lead, n = self.size(c)
+        sums = self.sums[c].at[self.slot(c, k)]
+        self.from_core(t).wait_recv()
+        if self.whole[c]:
+            self.own(t).wait()
+            add_rows(sums, (lead, (0, n), pl.ds(0, 512)), self.staged[c], (0, pl.ds(0, 512)))
+        else:
+            mine = lanes_at(self.place.core * 4, 4)
+            add_rows(sums, (lead, (0, n), pl.ds(0, 512)), self.source(t), (0, mine))
+        for copy in self.copies(t)[0]:
+            copy.start()
+
+    def second(self, t):
+        c, k = self.items[t]
         place = self.place
-        if s < count:
-            self.from_core(s).start()
-        if 0 <= s - 1 < count:
-            t = s - 1
-            c, k = self.items[t]
-            lead, n = self.size(c)
-            first, *_ = self.copies(t)
-            self.from_core(t).wait_recv()
-            if self.whole[c]:
-                self.own(t).wait()
-                add_rows(self.sums[c].at[k], (lead, (0, n), pl.ds(0, 512)), self.staged[c], (0, pl.ds(0, 512)))
-            else:
-                add_rows(
-                    self.sums[c].at[k], (lead, (0, n), pl.ds(0, 512)),
-                    self.source(t), (0, lanes_at(place.core * 4, 4)),
-                )
-            for copy in first:
-                copy.start()
-        if s < count and self.whole[self.items[s][0]]:
-            self.own(s).start()
-        if 0 <= s - 3 < count:
-            t = s - 3
-            c, k = self.items[t]
-            lead, n = self.size(c)
-            first, second, _ = self.copies(t)
-            for copy in first:
-                copy.wait_recv()
-            sums, landing = self.sums[c].at[k], self.from_first[c].at[k]
-            half = n // 2
-            add_rows(sums, (lead, (0, half), lanes_at(place.y * 2, 2)), landing, (0, pl.ds(0, 256)))
-            add_rows(sums, (lead, (half, half), lanes_at(place.x, 1)), landing, (half, pl.ds(0, 128)))
+        lead, n = self.size(c)
+        first, second, _ = self.copies(t)
+        for copy in first:
+            copy.wait_recv()
+        slot = self.slot(c, k)
+        sums, landing = self.sums[c].at[slot], self.from_first[c].at[slot]
+        half = n // 2
+        add_rows(sums, (lead, (0, half), lanes_at(place.y * 2, 2)), landing, (0, pl.ds(0, 256)))
+        add_rows(sums, (lead, (half, half), lanes_at(place.x, 1)), landing, (half, pl.ds(0, 128)))
+        add_rows(sums, (lead, (half, half), lanes_at(2 + place.x, 1)), landing, (half, pl.ds(128, 128)))
+        for copy in second:
+            copy.start()
+
+    def third(self, t):
+        c, k = self.items[t]
+        lead, n = self.size(c)
+        _, second, third = self.copies(t)
+        for copy in second:
+            copy.wait_recv()
+        slot = self.slot(c, k)
+        mine = lanes_at(self.place.y * 2 + self.place.x, 1)
+        add_rows(
+            self.sums[c].at[slot], (lead, (0, n), mine), self.from_second[c].at[slot], (0, pl.ds(0, 128))
+        )
+        if k == 2:
+            self.copies(self.items.index((c, 3)))[2].wait_recv()
             add_rows(
-                sums, (lead, (half, half), lanes_at(2 + place.x, 1)), landing, (half, pl.ds(128, 128))
+                self.sums[c].at[slot], (lead, (0, n), mine), self.from_mp[c].at[2], (0, pl.ds(0, 128))
             )
-            for copy in second:
-                copy.start()
-        if 0 <= s - 5 < count:
-            t = s - 5
-            c, k = self.items[t]
-            lead, n = self.size(c)
-            _, second, third = self.copies(t)
-            for copy in second:
-                copy.wait_recv()
-            sums, landing = self.sums[c].at[k], self.from_second[c].at[k]
-            mine = lanes_at(place.y * 2 + place.x, 1)
-            add_rows(sums, (lead, (0, n), mine), landing, (0, pl.ds(0, 128)))
-            if k % 2:
-                third.start()
-        if 0 <= s - 6 < count and self.items[s - 6][1] == 2:
-            c, k = self.items[s - 6]
-            lead, n = self.size(c)
-            self.copies(self.items.index((c, 3)))[2].wait_recv()
-            mine = lanes_at(place.y * 2 + place.x, 1)
-            add_rows(
-                self.sums[c].at[k], (lead, (0, n), mine), self.from_mp[c].at[2], (0, pl.ds(0, 128))
-            )
-            self.copies(s - 6)[2].start()
-        if 0 <= s - 8 < count:
-            c = self.items[s - 8][0]
-            steps = [k for which, k in self.items if which == c]
-            if self.items[s - 8][1] == steps[-1]:
-                for k in steps:
-                    if k in (1, 2):
-                        self.copies(self.items.index((c, k)))[2].wait_recv()
-                self.finish(c)
+        if k > 0 and not self.inside:
+            third.start()
+
+    def share(self, c):
+        return remote(
+            self.shares[c], self.from_mp[c].at[0], self.share_send.at[c], self.share_recv.at[c],
+            self.place.to_mp(1),
+        )
+
+    def end(self, c):
+        if self.inside:
+            self.finish(c)
+            return
+        if self.shares[c] is not None:
+            self.share(c).wait_recv()
+        for k in (1, 2):
+            if (c, k) in self.items:
+                self.copies(self.items.index((c, k)))[2].wait_recv()
+        self.finish(c)
+
+    def run(self, ops):
+        for op in ops.split():
+            table = {"c": self.core, "f": self.first, "s": self.second, "t": self.third, "e": self.end}
+            table[op[0]](int(op[1:]))
 
     def left(self, t):
         self.from_core(t).wait_send()
@@ -546,14 +562,19 @@
                 self.from_core(t).wait_send()
             for copy in first + second:
                 copy.wait_send()
-            if third is not None:
+            if third is not None and not self.inside:
                 third.wait_send()
+        for c, share in enumerate(self.shares):
+            if share is not None:
+                self.share(c).wait_send()
 
     def finish(self, c):
         place = self.place
         lead, n = self.size(c)
         mine = lanes_at(place.y * 2 + place.x, 1)
         sums, landing, out = self.sums[c], self.from_mp[c], self.outs[c]
+        steps = () if self.inside else (1, 2)
+        slot = self.slot(c, 1 if self.inside else 0)
         size = 32
         while n % size:
             size //= 2
@@ -561,10 +582,10 @@
         def body(i, carry):
             here = pl.ds(pl.multiple_of(i * size, size), size)
             for part in range(lead):
-                total = sums[0, part, here, mine].astype(F32)
-                for k in (1, 2):
+                total = sums[slot, part, here, mine].astype(F32)
+                for k in steps:
                     total = total + landing[k - 1, part, here, :].astype(F32)
-                out[part, here, :] = total
+                out[part, here, :] = total.astype(out.dtype)
             return carry
 
         lax.fori_loop(0, n // size, body, 0)
@@ -657,13 +678,16 @@
 FORWARD_ITEMS = [(0, 0), (1, 0), (2, 0), (0, 1), (0, 2), (0, 3), (1, 1), (2, 1), (1, 2), (2, 2), (1, 3), (2, 3)]
 
 
+FORWARD_SUMS = [(0, 1), (1, 1)]
+
+
 def forward_kernel(
     mp_size, group,
     query_ref, output_ref, gate_up_ref, down_ref, key_value_ref, table_ref, boxes_ref, lengths_ref,
     input_ref, gain_ref, cotangent_ref,
     w_first, queries_out, keys_out, values_out, heads_out_out, lse, layout, line, key_extra, key_extra_t,
     slot_owner_out, residual_out, layer_output, second_grad, gate_up_full, down_full, tables,
-    line_hot, bin_hot, queries, keys_t, values_t, heads_out, slot_owner, residual,
+    line_hot, bin_hot, gate_up_share, down_share, queries, keys_t, values_t, heads_out, slot_owner, residual,
     first_ref, query_piece, normed_t, slot_t, w_gate_up, w_down, first_here, key_aug, query_aug, strip, scores, probs,
     second_t, second_owner, out_owner, out_t,
     hidden_a, hidden_b, hidden_c, act_t, low_t, stage_gate_up, stage_down,
@@ -686,7 +710,7 @@
     column = lanes_at(place.core * 4 + place.y * 2 + place.x, 1)
     gather = Gather(
         place, [first_ref, gate_up_ref.at[:, :, column], down_ref.at[:, :, column]],
-        [w_first, w_gate_up, w_down], sems, items
+        [w_first, w_gate_up, w_down], sems[:5], items
     )
     at = {item: t for t, item in enumerate(items)}
 
@@ -782,6 +806,11 @@
         (14, 0): "f9 s8", (16, 0): "f10 t7", (16, 2): "s9", (17, 0): "f11 t8", (17, 1): "s10",
         (17, 3): "t9", (18, 0): "s11", (18, 3): "t10", (19, 0): "t11",
     }
+    scatter = Scatter(
+        place, [gate_up_full, down_full], [gate_up_share, down_share], sems[5:], FORWARD_SUMS,
+        inside=True,
+    )
+    sum_table = {(18, 3): "c0 c1", (19, 0): "f0 f1", (19, 2): "s0", (19, 3): "s1"}
 
     def communicate(unit, point):
         for (at_unit, at_point), ops in table.items():
@@ -790,6 +819,13 @@
                 @pl.when(unit == at_unit)
                 def _(ops=ops):
                     gather.run(ops)
+
+        for (at_unit, at_point), ops in sum_table.items():
+            if at_point == point:
+
+                @pl.when(unit == at_unit)
+                def _(ops=ops):
+                    scatter.run(ops)
 
     def head_unit(unit, carry):
         communicate(unit, 0)
@@ -971,9 +1007,11 @@
 
     lax.fori_loop(0, mp_size, hidden_unit, 0)
     layer_output[...] = layer_output[...] + residual[...]
+    scatter.run("t0 t1 e0 e1")
     for copy in store(mp_size - 1):
         copy.wait()
     gather.close()
+    scatter.close()
     for copy in row_copies + table_copies:
         copy.wait_send()
     for copy in kept:
@@ -1018,6 +1056,8 @@
         (shape((mp_size, 24, LANES), F32), vmem),
         (shape((LANES, width), BF16), vmem),
         (shape((LANES, LANES), BF16), vmem),
+        (shape((2, hidden, LANES), BF16), vmem),
+        (shape((1, hidden, LANES), BF16), vmem),
     ]
     return pl.pallas_call(
         partial(forward_kernel, mp_size, group),
@@ -1057,7 +1097,8 @@
             dma((group,)), dma((group,)), dma((1,)),
             dma((mp_size,)), dma((mp_size,)), dma((1,)), dma((2,)), dma((2,)), dma((6,)),
         ]
-        + Gather.semaphores(3, mp_size),
+        + Gather.semaphores(3, mp_size)
+        + Scatter.scratch([(2, hidden), (1, hidden)], (True, True), FORWARD_SUMS),
         compiler_params=pltpu.CompilerParams(
             collective_id=0, has_side_effects=True, vmem_limit_bytes=62 << 20
         ),
@@ -1067,7 +1108,7 @@
     )
 
 
-BACKWARD_ITEMS = [(0, 3), (1, 3), (0, 2), (1, 2), (2, 3), (0, 1), (2, 2), (1, 1), (0, 0), (1, 0), (2, 1), (2, 0)]
+BACKWARD_ITEMS = [(0, 3), (1, 3), (0, 2), (1, 2), (2, 3), (2, 2), (0, 0), (2, 1), (1, 0), (2, 0)]
 
 
 def unskewed(values, first, count, shift):
@@ -1094,7 +1135,7 @@
         gate_up_full, down_full, w_first, queries, keys_t, values_t, heads_out,
         residual_in, second_in, cotangent_in,
         lse, layout, line, key_extra, key_extra_t, slot_owner, layer_input, gains, line_hot, bin_hot,
-        input_grad, small_out, gate_up_sum, down_sum, first_sum,
+        gate_up_share, down_share, input_grad, small_out, gate_up_sum, down_sum, first_sum,
         *refs,
     ) = refs
     (
@@ -1118,7 +1159,9 @@
 
     items = BACKWARD_ITEMS
     fulls = [gate_up_full, down_full, full_here]
-    scatter = Scatter(place, fulls, [gate_up_sum, down_sum, first_sum], refs, items)
+    scatter = Scatter(
+        place, fulls, [gate_up_sum, down_sum, first_sum], refs, items, [gate_up_share, down_share, None]
+    )
 
     loads = [
         Copy(second_in, slot_grad.at[pl.ds(0, rows), :], value_sem.at[0]),
@@ -1129,7 +1172,9 @@
         copy.start()
     greet(place)
     meet(place)
-    scatter.step(0)
+    scatter.run("c0 c1")
+    for c in range(2):
+        scatter.share(c).start()
     key_aug[...] = key_extra[...]
     key_aug_t[pl.ds(64, 128), :] = key_extra_t[...]
     for copy in loads:
@@ -1150,7 +1195,7 @@
 
     total = lax.fori_loop(0, rows // 16, norm_back, jnp.zeros((8, model_width), F32))
     gain_part[...] = jnp.sum(total, axis=0, keepdims=True)
-    scatter.step(1)
+    scatter.run("f0 c2")
     branch_t[...] = branch_owner[...].T
     parts = [branch_owner[:, b * LANES : (b + 1) * LANES] for b in range(model_width // LANES)]
     for block, values in enumerate(parts):
@@ -1158,21 +1203,29 @@
         branch_owner[:, owner * LANES : (owner + 1) * LANES] = values
     slot_grad[...] = jnp.zeros_like(slot_grad)
     own_grad[...] = jnp.zeros_like(own_grad)
-    scatter.step(2)
+    scatter.run("f1 c3")
 
     plan = {
-        (0, 2): [3], (0, 4): [4], (1, 2): [5], (1, 4): [6], (2, 2): [7], (2, 4): [8], (3, 4): [9],
+        (0, 2): "s0 f2", (0, 3): "s1 f3", (0, 4): "t0 c4", (1, 1): "s2", (1, 2): "t1 f4", (1, 3): "s3 c6",
+        (2, 0): "t2 c5", (2, 1): "s4 f5", (2, 2): "t3", (2, 3): "f6 c8", (2, 4): "t4 c7", (3, 1): "s5",
+        (3, 2): "s6 f7", (3, 4): "t5 f8 c9",
     }
-    done = 9
 
     def communicate(block, point):
-        for (at_block, at_point), steps in plan.items():
+        for (at_block, at_point), ops in plan.items():
             if at_point == point:
 
                 @pl.when(block == at_block)
-                def _(steps=steps):
-                    for s in steps:
-                        scatter.step(s)
+                def _(ops=ops):
+                    scatter.run(ops)
+
+    row_copies = [
+        remote(
+            rows_out.at[k - 1], peers.at[k - 1], row_send.at[k], row_recv.at[k],
+            (place.dp, first_peer + lax.rem(member + k, group)),
+        )
+        for k in range(1, group)
+    ]
 
     def block_unit(block, carry):
         communicate(block, 0)
@@ -1295,6 +1348,20 @@
             return inner_carry
 
         lax.fori_loop(0, heads_here, head_unit, 0)
+        slot_grad[...] = slot_grad[...] + jnp.dot(
+            kv_here[...], w_kv[...], preferred_element_type=F32
+        )
+        own_grad[...] = own_grad[...] + jnp.dot(
+            dq_here[...].T, w_query[...], preferred_element_type=F32
+        )
+
+        @pl.when(block == mp_size - 1)
+        def _():
+            for k, copy in enumerate(row_copies):
+                other = lax.rem(member + k + 1, group)
+                rows_out[k] = slot_grad[pl.ds(pl.multiple_of(other * rows, 16), rows), :].astype(BF16)
+                copy.start()
+
         full_here[slot, 0] = jnp.dot(
             dq_here[...], slot_owner[pl.ds(own_start, rows), :], preferred_element_type=F32
         ).astype(BF16)
@@ -1304,32 +1371,12 @@
         full_here[slot, 2] = jnp.dot(
             dv_here[...], slot_owner[...], preferred_element_type=F32
         ).astype(BF16)
-        slot_grad[...] = slot_grad[...] + jnp.dot(
-            kv_here[...], w_kv[...], preferred_element_type=F32
-        )
-        own_grad[...] = own_grad[...] + jnp.dot(
-            dq_here[...].T, w_query[...], preferred_element_type=F32
-        )
         communicate(block, heads_here)
         return carry
 
     lax.fori_loop(0, mp_size, block_unit, 0)
 
-    copies = []
-    for k in range(1, group):
-        other = lax.rem(member + k, group)
-        rows_out[k - 1] = slot_grad[pl.ds(pl.multiple_of(other * rows, 16), rows), :].astype(BF16)
-        copies.append(
-            remote(
-                rows_out.at[k - 1], peers.at[k - 1], row_send.at[k], row_recv.at[k],
-                (place.dp, first_peer + other),
-            )
-        )
-    for copy in copies:
-        copy.start()
-    steps = list(range(done + 1, scatter.steps))
-    for s in steps[:1]:
-        scatter.step(s)
+    scatter.run("t6 f9")
 
     gain_rows = model_width // LANES
     head_count = bin_sums.shape[1]
@@ -1373,14 +1420,6 @@
             ]
         )
         at += len(partners)
-    steps = steps[1:]
-
-    def advance(count):
-        nonlocal steps
-        for s in steps[:count]:
-            scatter.step(s)
-        steps = steps[count:]
-
     def round_done(i):
         at = sum(len(partners) for partners in rounds[:i])
         value = stage[i]
@@ -1391,12 +1430,12 @@
 
     for copy in sums[0]:
         copy.start()
-    advance(2)
+    scatter.run("s7 s8")
     stage[1] = round_done(0)
     for copy in sums[1]:
         copy.start()
-    advance(2)
-    for copy in copies:
+    scatter.run("t7 s9")
+    for copy in row_copies:
         copy.wait_recv()
 
     def input_back(i, carry):
@@ -1414,24 +1453,21 @@
         return carry
 
     lax.fori_loop(0, rows // 16, input_back, 0)
-    advance(1)
     stage[2] = round_done(1)
     for copy in sums[2]:
         copy.start()
-    advance(len(steps))
+    scatter.run("t8 t9 e0 e1 e2")
     small_out[...] = round_done(2)
     sums = sum(sums, [])
-    for s in steps:
-        scatter.step(s)
     scatter.close()
-    for copy in copies + sums:
+    for copy in row_copies + sums:
         copy.wait_send()
 
 
 def backward(
     mp_size, group, gate_up_full, down_full, w_first, queries, keys_t, values_t, heads_out,
     residual, second_grad, cotangent, lse, layout, line, key_extra, key_extra_t, slot_owner,
-    layer_input, gains, line_hot, bin_hot,
+    layer_input, gains, line_hot, bin_hot, gate_up_share, down_share,
 ):
     rows, model_width = layer_input.shape
     keys = slot_owner.shape[0]
@@ -1455,7 +1491,7 @@
             shape((small_rows, LANES), F32),
             *[shape((lead, n, LANES), F32) for lead, n in sizes],
         ),
-        in_specs=[hbm] * 10 + [vmem] * 10,
+        in_specs=[hbm] * 10 + [vmem] * 12,
         out_specs=(vmem,) * 5,
         scratch_shapes=[
             pltpu.VMEM((keys, model_width), F32),
@@ -1495,7 +1531,7 @@
             dma((6 + 2 * heads_here,)), dma((3,)), dma((group,)), dma((group,)),
             dma((count,)), dma((count,)),
         ]
-        + Scatter.scratch(sizes, (True, True, False), mp_size),
+        + Scatter.scratch(sizes, (True, True, False), BACKWARD_ITEMS),
         compiler_params=pltpu.CompilerParams(
             collective_id=1, has_side_effects=True, vmem_limit_bytes=63 << 20
         ),
@@ -1503,7 +1539,7 @@
     )(
         gate_up_full, down_full, w_first, queries, keys_t, values_t, heads_out, residual,
         second_grad, cotangent, lse, layout, line, key_extra, key_extra_t, slot_owner, layer_input,
-        gains, line_hot, bin_hot,
+        gains, line_hot, bin_hot, gate_up_share, down_share,
     )
 
 
@@ -1710,6 +1746,7 @@
     (
         w_first, queries, keys_t, values_t, heads_out, lse, layout, line, key_extra, key_extra_t,
         slot_owner, residual, layer_output, second_grad, gate_up_full, down_full, _, line_hot, bin_hot,
+        gate_up_share, down_share,
     ) = forward(
         mp_size, group, query_weight, output_weight, jnp.transpose(gate_up_weight, (1, 2, 0)),
         down_weight[None], key_value.reshape(LANES, 2 * inner_here), table, box_bins, doc_lengths,
@@ -1718,7 +1755,7 @@
     input_grad, small, gate_up_sum, down_sum, summed = backward(
         mp_size, group, gate_up_full, down_full, w_first, queries, keys_t, values_t, heads_out,
         residual, second_grad, cotangent, lse, layout, line, key_extra, key_extra_t, slot_owner,
-        layer_input, gains, line_hot, bin_hot,
+        layer_input, gains, line_hot, bin_hot, gate_up_share, down_share,
     )
     gain_rows = model_width // LANES
     gains = small[: 2 * gain_rows].reshape(2, model_width)

time: 282 us -> 274 us (0.972)
  Pallas kernels: 265 us -> 257 us
    pallas_call x1, Pallas kernels: 130 us -> 110 us  [backward(): pl.pallas_call(partial(backward_kernel, mp_size, group), out_shape=(shape...]
    pallas_call x1, Pallas kernels: 135 us -> 147 us  [forward(): pl.pallas_call(partial(forward_kernel, mp_size, group), out_shape=tuple((...]
where the time goes in v5:
time: 274 us
  Pallas kernels  257 us (94%)
  local copies, waits for them, and re-layouts  13.3 us (5%)
    pallas_call x1, Pallas kernels, forward(): pl.pallas_call(partial(forward_kernel, mp_size, group), out_shape=tuple((...  147 us
    pallas_call x1, Pallas kernels, backward(): pl.pallas_call(partial(backward_kernel, mp_size, group), out_shape=(shape...  110 us
    unnamed x18, local copies, waits for them, and re-layouts  8.14 us

profile of v5, /device:TPU:0, one launch (start us, length us, event | category | flops | bytes accessed | tf_op | source)
XLA Modules:
  0.0 273.7 jit_solution(4209357765995451681)
XLA Ops:
  0.7 1.0 constant_dynamic-slice_fusion.2
  1.7 0.7 copy.24
  2.3 1.3 bitcast_convert_fusion.table_ref
  3.6 1.3 convert_element_type.6.gain_ref.refs_17_
  4.9 146.9 %forward.1 = (bf16[4,1024,1024]{2,1,0:T(8,128)(2,1)}, bf16[1024,384]{1,0:T(8,128)(2,1)}, bf16[1024,768]{1,0:T(8,128)(2,1)}, bf16[1024,768]{1,0:T(8,128)(2,1)}, b...) custom-call(bf16[1024,256]{1,0:T(8,128)(2,1)} %query_ref.1, ...), custom_call_target="tpu_custom_call" | custom-call | tf_op jit(solution)/shard_map/forward/pallas_call | solution.py:1062
  151.9 110.2 %backward.1 = (f32[384,1024]{1,0:T(8,128)}, f32[64,128]{1,0:T(8,128)}, f32[2,704,128]{2,1,0:T(8,128)}, f32[1,704,128]{2,1,0:T(8,128)}, f32[4,256,128]{2,1,0:T(8,128)}) custom-call(bf16[2,2816,1024]{2,1,0:T(8,128)(2,1)} %get-tuple-element.35.refs_0_, bf16[1,2816,1024]{2,1,0:T(8,128)(2,1)} %get-tuple-element.36.refs_1_, ...), custom_call_target="tpu_custom_call" | custom-call | tf_op jit(solution)/shard_map/backward/pallas_call | solution.py:1487
  262.0 0.0 copy-start.4
  262.0 0.0 copy-start
  262.1 0.8 slice.15
  262.9 0.6 constant_dynamic-slice_fusion.1
  263.5 1.6 slice_bitcast_fusion.1
  265.2 0.8 copy.21
  265.9 1.0 slice_bitcast_fusion
  266.9 0.8 copy.22
  267.7 0.0 copy-done.4
  267.7 0.1 constant_dynamic-slice_fusion
  267.8 0.7 copy.23
  268.5 0.0 copy-done
  268.5 0.0 copy-start.1
  268.5 1.1 copy.29
  269.6 0.8 copy-done.1
  270.5 0.0 copy-start.2
  270.5 0.0 copy-start.3
  270.5 1.1 copy.30
  271.6 0.5 copy-done.2
  272.1 0.9 copy.31
  272.9 0.0 copy-done.3
  272.9 0.7 copy.32
  (2 shorter events, 0.0 us)
Async XLA Ops:
  262.0 5.7 %copy-start.4 = (f32[64,128]{1,0:T(8,128)S(1)}, f32[64,128]{1,0:T(8,128)}, u32[]{:S(2)}) copy-start(f32[64,128]{1,0:T(8,128)} %get-tuple-element.55) | copy-start | bytes 98308
  262.0 6.5 %copy-start = (f32[384,1024]{1,0:T(8,128)S(1)}, f32[384,1024]{1,0:T(8,128)}, u32[]{:S(2)}) copy-start(f32[384,1024]{1,0:T(8,128)} %get-tuple-element.79) | copy-start | bytes 4718596
  268.5 2.0 copy-start.1
  270.5 1.6 copy-start.2
  270.5 2.5 copy-start.3

commit v6 on v5

--- a/solution.py
+++ b/solution.py
@@ -810,7 +810,7 @@
         place, [gate_up_full, down_full], [gate_up_share, down_share], sems[5:], FORWARD_SUMS,
         inside=True,
     )
-    sum_table = {(18, 3): "c0 c1", (19, 0): "f0 f1", (19, 2): "s0", (19, 3): "s1"}
+    sum_table = {(18, 0): "c0 c1", (18, 3): "f0 f1", (19, 3): "s0"}
 
     def communicate(unit, point):
         for (at_unit, at_point), ops in table.items():
@@ -948,6 +948,12 @@
 
     def hidden_unit(step, carry):
         unit = step + head_units
+
+        @pl.when(step > 0)
+        def _():
+            for copy in store(step):
+                copy.wait()
+
         communicate(unit, 0)
         source = place.across(step)
         here = pl.ds(pl.multiple_of(source * hidden, 16), hidden)
@@ -981,11 +987,6 @@
 
         lax.fori_loop(0, hidden // 16, activate, 0)
         communicate(unit, 2)
-
-        @pl.when(step > 0)
-        def _():
-            for copy in store(step):
-                copy.wait()
 
         stage_down[0] = jnp.dot(act_t[...], out_owner[...], preferred_element_type=F32).astype(BF16)
         stage_gate_up[0] = jnp.dot(
@@ -1007,7 +1008,8 @@
 
     lax.fori_loop(0, mp_size, hidden_unit, 0)
     layer_output[...] = layer_output[...] + residual[...]
-    scatter.run("t0 t1 e0 e1")
+    scatter.run("s1 t0 t1")
+    scatter.run("e0 e1")
     for copy in store(mp_size - 1):
         copy.wait()
     gather.close()
@@ -1135,11 +1137,11 @@
         gate_up_full, down_full, w_first, queries, keys_t, values_t, heads_out,
         residual_in, second_in, cotangent_in,
         lse, layout, line, key_extra, key_extra_t, slot_owner, layer_input, gains, line_hot, bin_hot,
-        gate_up_share, down_share, input_grad, small_out, gate_up_sum, down_sum, first_sum,
+        gate_up_share, down_share, input_out, small_out, gate_up_sum, down_sum, first_sum,
         *refs,
     ) = refs
     (
-        slot_grad, own_grad, residual_grad, branch_owner, branch_t, w_query, w_output, w_kv,
+        input_grad, slot_grad, own_grad, residual_grad, branch_owner, branch_t, w_query, w_output, w_kv,
         q_here, k_here, v_here, out_here, grad_here, dq_here, dk_here, dv_here, kv_here,
         key_aug, key_aug_t, query_aug, value_aug, grad_aug, strip, strip_grad, probs_grad,
         layout_grad, line_sums, bin_sums, gain_part, rows_out, peers, stage, stage_in, full_here,
@@ -1453,13 +1455,17 @@
         return carry
 
     lax.fori_loop(0, rows // 16, input_back, 0)
+    leave = Copy(input_grad, input_out, value_sem.at[0])
+    leave.start()
     stage[2] = round_done(1)
     for copy in sums[2]:
         copy.start()
-    scatter.run("t8 t9 e0 e1 e2")
+    scatter.run("t8 t9")
+    scatter.run("e0 e1 e2")
     small_out[...] = round_done(2)
     sums = sum(sums, [])
     scatter.close()
+    leave.wait()
     for copy in row_copies + sums:
         copy.wait_send()
 
@@ -1492,8 +1498,9 @@
             *[shape((lead, n, LANES), F32) for lead, n in sizes],
         ),
         in_specs=[hbm] * 10 + [vmem] * 12,
-        out_specs=(vmem,) * 5,
+        out_specs=(hbm,) + (vmem,) * 4,
         scratch_shapes=[
+            pltpu.VMEM((rows, model_width), F32),
             pltpu.VMEM((keys, model_width), F32),
             pltpu.VMEM((rows, model_width), F32),
             pltpu.VMEM((rows, model_width), F32),

time: 274 us -> 270 us (0.985)
  Pallas kernels: 257 us -> 253 us
    pallas_call x1, Pallas kernels: 147 us -> 144 us  [forward(): pl.pallas_call(partial(forward_kernel, mp_size, group), out_shape=tuple((...]
where the time goes in v6:
time: 270 us; the launch traced here: 269 us
  Pallas kernels  253 us (94%)
  local copies, waits for them, and re-layouts  13.3 us (5%)
    pallas_call x1, Pallas kernels, forward(): pl.pallas_call(partial(forward_kernel, mp_size, group), out_shape=tuple((...  144 us
    pallas_call x1, Pallas kernels, backward(): pl.pallas_call(partial(backward_kernel, mp_size, group), out_shape=(shape...  109 us
    unnamed x18, local copies, waits for them, and re-layouts  8.14 us

profile of v6, /device:TPU:0, one launch (start us, length us, event | category | flops | bytes accessed | tf_op | source)
XLA Modules:
  0.0 269.1 jit_solution(10139496847479860576)
XLA Ops:
  0.7 1.0 constant_dynamic-slice_fusion.2
  1.7 0.7 copy.24
  2.3 1.3 bitcast_convert_fusion.table_ref
  3.6 1.3 convert_element_type.6.gain_ref.refs_17_
  4.9 143.7 %forward.1 = (bf16[4,1024,1024]{2,1,0:T(8,128)(2,1)}, bf16[1024,384]{1,0:T(8,128)(2,1)}, bf16[1024,768]{1,0:T(8,128)(2,1)}, bf16[1024,768]{1,0:T(8,128)(2,1)}, b...) custom-call(bf16[1024,256]{1,0:T(8,128)(2,1)} %query_ref.1, ...), custom_call_target="tpu_custom_call" | custom-call | tf_op jit(solution)/shard_map/forward/pallas_call | solution.py:1064
  148.6 108.9 %backward.1 = (f32[384,1024]{1,0:T(8,128)}, f32[64,128]{1,0:T(8,128)}, f32[2,704,128]{2,1,0:T(8,128)}, f32[1,704,128]{2,1,0:T(8,128)}, f32[4,256,128]{2,1,0:T(8,128)}) custom-call(bf16[2,2816,1024]{2,1,0:T(8,128)(2,1)} %get-tuple-element.35.refs_0_, bf16[1,2816,1024]{2,1,0:T(8,128)(2,1)} %get-tuple-element.36.refs_1_, ...), custom_call_target="tpu_custom_call" | custom-call | tf_op jit(solution)/shard_map/backward/pallas_call | solution.py:1493
  257.5 0.0 copy-start.4
  257.5 0.0 copy-start
  257.5 0.8 slice.15
  258.3 0.6 constant_dynamic-slice_fusion.1
  259.0 1.6 slice_bitcast_fusion.1
  260.6 0.8 copy.21
  261.4 1.0 slice_bitcast_fusion
  262.3 0.8 copy.22
  263.2 0.0 copy-done.4
  263.2 0.1 constant_dynamic-slice_fusion
  263.2 0.7 copy.23
  263.9 0.0 copy-done
  263.9 0.0 copy-start.1
  263.9 1.1 copy.29
  265.1 0.8 copy-done.1
  265.9 0.0 copy-start.2
  265.9 0.0 copy-start.3
  265.9 1.1 copy.30
  267.1 0.5 copy-done.2
  267.5 0.9 copy.31
  268.4 0.0 copy-done.3
  268.4 0.7 copy.32
  (2 shorter events, 0.0 us)
Async XLA Ops:
  257.5 5.7 %copy-start.4 = (f32[64,128]{1,0:T(8,128)S(1)}, f32[64,128]{1,0:T(8,128)}, u32[]{:S(2)}) copy-start(f32[64,128]{1,0:T(8,128)} %get-tuple-element.55) | copy-start | bytes 98308
  257.5 6.5 %copy-start = (f32[384,1024]{1,0:T(8,128)S(1)}, f32[384,1024]{1,0:T(8,128)}, u32[]{:S(2)}) copy-start(f32[384,1024]{1,0:T(8,128)} %get-tuple-element.79) | copy-start | bytes 4718596
  263.9 2.0 copy-start.1
  265.9 1.6 copy-start.2
  265.9 2.5 copy-start.3

commit v7 on v6

--- a/solution.py
+++ b/solution.py
@@ -752,7 +752,7 @@
 
         lax.fori_loop(0, rows // 16, body, 0)
 
-    norm_into(input_ref, gain_ref[0:1, :])
+    norm_into(input_ref, gain_ref[0:1, :].astype(F32))
     normed_t[...] = second_owner[...].T
     row_here.start()
     for copy in loads:
@@ -804,7 +804,7 @@
         (1, 0): "f3 z4 z6", (2, 0): "s3 s2 t1", (4, 0): "t3 f4 z7", (5, 0): "s4 t2", (6, 0): "f5 z8",
         (7, 0): "t4 f6", (8, 0): "s5 z9", (9, 0): "f7 s6", (11, 0): "t5", (12, 0): "f8 s7", (13, 0): "t6",
         (14, 0): "f9 s8", (16, 0): "f10 t7", (16, 2): "s9", (17, 0): "f11 t8", (17, 1): "s10",
-        (17, 3): "t9", (18, 0): "s11", (18, 3): "t10", (19, 0): "t11",
+        (17, 3): "t9", (18, 0): "s11", (18, 3): "t10", (19, 1): "t11",
     }
     scatter = Scatter(
         place, [gate_up_full, down_full], [gate_up_share, down_share], sems[5:], FORWARD_SUMS,
@@ -931,7 +931,7 @@
     ]
     for copy in kept:
         copy.start()
-    norm_into(residual, gain_ref[1:2, :])
+    norm_into(residual, gain_ref[1:2, :].astype(F32))
     second_t[...] = second_owner[...].T
     turned_blocks = [second_owner[:, b * LANES : (b + 1) * LANES] for b in range(model_width // LANES)]
     for block, values in enumerate(turned_blocks):
@@ -962,11 +962,16 @@
             @pl.when(step == k)
             def _(k=k):
                 gather.done(at[(1, k)])
-                gather.done(at[(2, k)])
 
         hidden_a[...] = jnp.dot(w_gate_up[0, here, :], second_t[...], preferred_element_type=F32)
         hidden_b[...] = jnp.dot(w_gate_up[1, here, :], second_t[...], preferred_element_type=F32)
         communicate(unit, 1)
+        for k in range(mp_size):
+
+            @pl.when(step == k)
+            def _(k=k):
+                gather.done(at[(2, k)])
+
         hidden_c[...] = jnp.dot(w_down[0, here, :], out_t[...], preferred_element_type=F32)
 
         def activate(i, inner_carry):
@@ -1187,7 +1192,7 @@
         grad = slot_grad[here, :]
         values = slot_grad[pl.ds(pl.multiple_of(rows + i * 16, 16), 16), :]
         scale = lax.rsqrt(jnp.mean(values * values, axis=1, keepdims=True) + EPSILON)
-        scaled = gains[1:2, :] * grad
+        scaled = gains[1:2, :].astype(F32) * grad
         mean = jnp.mean(scaled * values, axis=1, keepdims=True)
         result = input_grad[here, :] + scale * scaled - values * (scale * scale * scale * mean)
         residual_grad[here, :] = result
@@ -1405,7 +1410,7 @@
         total = lax.fori_loop(0, keys // 64, gain_sum, jnp.zeros((8, LANES), F32))
         total = lax.fori_loop(0, rows // 64, own_sum, total)
         stage[0, block : block + 1, :] = (
-            jnp.sum(total, axis=0, keepdims=True) / gains[0:1, these]
+            jnp.sum(total, axis=0, keepdims=True) / gains[0:1, these].astype(F32)
         )
         stage[0, gain_rows + block : gain_rows + block + 1, :] = gain_part[:, these]
 
@@ -1432,7 +1437,7 @@
 
     for copy in sums[0]:
         copy.start()
-    scatter.run("s7 s8")
+    scatter.run("s7 s8 e0")
     stage[1] = round_done(0)
     for copy in sums[1]:
         copy.start()
@@ -1447,7 +1452,7 @@
             grad = grad + peers[k, here, :].astype(F32)
         values = layer_input[here, :]
         scale = lax.rsqrt(jnp.mean(values * values, axis=1, keepdims=True) + EPSILON)
-        scaled = gains[0:1, :] * grad
+        scaled = gains[0:1, :].astype(F32) * grad
         mean = jnp.mean(scaled * values, axis=1, keepdims=True)
         input_grad[here, :] = (
             residual_grad[here, :] + scale * scaled - values * (scale * scale * scale * mean)
@@ -1461,7 +1466,7 @@
     for copy in sums[2]:
         copy.start()
     scatter.run("t8 t9")
-    scatter.run("e0 e1 e2")
+    scatter.run("e1 e2")
     small_out[...] = round_done(2)
     sums = sum(sums, [])
     scatter.close()
@@ -1745,7 +1750,6 @@
     heads_here = bias_tables.shape[2]
     head_count = heads_here * mp_size
     inner_here = query_weight.shape[1]
-    gains = norm_gains.astype(F32)
     column = ((dp_index % 2) * 4 + dp_index // 2) * LANES
     key_value = lax.dynamic_slice_in_dim(key_value_weight, column, LANES, 0)
     table = jnp.swapaxes(bias_tables.astype(F32), 1, 2)
@@ -1757,12 +1761,12 @@
     ) = forward(
         mp_size, group, query_weight, output_weight, jnp.transpose(gate_up_weight, (1, 2, 0)),
         down_weight[None], key_value.reshape(LANES, 2 * inner_here), table, box_bins, doc_lengths,
-        layer_input, gains, cotangent,
+        layer_input, norm_gains, cotangent,
     )
     input_grad, small, gate_up_sum, down_sum, summed = backward(
         mp_size, group, gate_up_full, down_full, w_first, queries, keys_t, values_t, heads_out,
         residual, second_grad, cotangent, lse, layout, line, key_extra, key_extra_t, slot_owner,
-        layer_input, gains, line_hot, bin_hot, gate_up_share, down_share,
+        layer_input, norm_gains, line_hot, bin_hot, gate_up_share, down_share,
     )
     gain_rows = model_width // LANES
     gains = small[: 2 * gain_rows].reshape(2, model_width)

time: 270 us -> 268 us (level)
  no operation moved by 1% of the time
where the time goes in v7:
time: 268 us
  Pallas kernels  253 us (94%)
  local copies, waits for them, and re-layouts  13.3 us (5%)
    pallas_call x1, Pallas kernels, forward(): pl.pallas_call(partial(forward_kernel, mp_size, group), out_shape=tuple((...  144 us
    pallas_call x1, Pallas kernels, backward(): pl.pallas_call(partial(backward_kernel, mp_size, group), out_shape=(shape...  109 us
    unnamed x18, local copies, waits for them, and re-layouts  8.14 us

profile of v7, /device:TPU:0, one launch (start us, length us, event | category | flops | bytes accessed | tf_op | source)
XLA Modules:
  0.0 267.9 jit_solution(924425501839553623)
XLA Ops:
  0.7 1.0 constant_dynamic-slice_fusion.2
  1.7 0.7 copy.24
  2.3 1.3 bitcast_convert_fusion.table_ref
  3.6 143.7 %forward.1 = (bf16[4,1024,1024]{2,1,0:T(8,128)(2,1)}, bf16[1024,384]{1,0:T(8,128)(2,1)}, bf16[1024,768]{1,0:T(8,128)(2,1)}, bf16[1024,768]{1,0:T(8,128)(2,1)}, b...) custom-call(bf16[1024,256]{1,0:T(8,128)(2,1)} %query_ref.1, ...), custom_call_target="tpu_custom_call" | custom-call | tf_op jit(solution)/shard_map/forward/pallas_call | solution.py:1069
  147.3 108.9 %backward.1 = (f32[384,1024]{1,0:T(8,128)}, f32[64,128]{1,0:T(8,128)}, f32[2,704,128]{2,1,0:T(8,128)}, f32[1,704,128]{2,1,0:T(8,128)}, f32[4,256,128]{2,1,0:T(8,128)}) custom-call(bf16[2,2816,1024]{2,1,0:T(8,128)(2,1)} %get-tuple-element.35.refs_0_, bf16[1,2816,1024]{2,1,0:T(8,128)(2,1)} %get-tuple-element.36.refs_1_, ...), custom_call_target="tpu_custom_call" | custom-call | tf_op jit(solution)/shard_map/backward/pallas_call | solution.py:1498
  256.2 0.0 copy-start.4
  256.2 0.0 copy-start
  256.2 0.8 slice.15
  257.1 0.6 constant_dynamic-slice_fusion.1
  257.7 1.6 slice_bitcast_fusion.1
  259.4 0.8 copy.21
  260.1 1.0 slice_bitcast_fusion
  261.1 0.8 copy.22
  261.9 0.0 copy-done.4
  261.9 0.1 constant_dynamic-slice_fusion
  262.0 0.7 copy.23
  262.7 0.0 copy-done
  262.7 0.0 copy-start.1
  262.7 1.1 copy.29
  263.8 0.8 copy-done.1
  264.7 0.0 copy-start.2
  264.7 0.0 copy-start.3
  264.7 1.1 copy.30
  265.8 0.5 copy-done.2
  266.3 0.9 copy.31
  267.1 0.0 copy-done.3
  267.1 0.7 copy.32
  (2 shorter events, 0.0 us)
Async XLA Ops:
  256.2 5.7 %copy-start.4 = (f32[64,128]{1,0:T(8,128)S(1)}, f32[64,128]{1,0:T(8,128)}, u32[]{:S(2)}) copy-start(f32[64,128]{1,0:T(8,128)} %get-tuple-element.55) | copy-start | bytes 98308
  256.2 6.5 %copy-start = (f32[384,1024]{1,0:T(8,128)S(1)}, f32[384,1024]{1,0:T(8,128)}, u32[]{:S(2)}) copy-start(f32[384,1024]{1,0:T(8,128)} %get-tuple-element.79) | copy-start | bytes 4718596
  262.7 2.0 copy-start.1
  264.7 1.6 copy-start.2
  264.7 2.5 copy-start.3

commit v8 on v7

--- a/solution.py
+++ b/solution.py
@@ -810,7 +810,7 @@
         place, [gate_up_full, down_full], [gate_up_share, down_share], sems[5:], FORWARD_SUMS,
         inside=True,
     )
-    sum_table = {(18, 0): "c0 c1", (18, 3): "f0 f1", (19, 3): "s0"}
+    sum_table = {(18, 0): "c0 c1", (18, 3): "f0 f1", (19, 2): "s0"}
 
     def communicate(unit, point):
         for (at_unit, at_point), ops in table.items():

time: 268 us -> 268 us (level)
  no operation moved by 1% of the time
where the time goes in v8:
time: 268 us
  Pallas kernels  253 us (94%)
  local copies, waits for them, and re-layouts  13.3 us (5%)
    pallas_call x1, Pallas kernels, forward(): pl.pallas_call(partial(forward_kernel, mp_size, group), out_shape=tuple((...  144 us
    pallas_call x1, Pallas kernels, backward(): pl.pallas_call(partial(backward_kernel, mp_size, group), out_shape=(shape...  109 us
    unnamed x18, local copies, waits for them, and re-layouts  8.14 us

profile of v8, /device:TPU:0, one launch (start us, length us, event | category | flops | bytes accessed | tf_op | source)
XLA Modules:
  0.0 267.9 jit_solution(4913849963260499011)
XLA Ops:
  0.7 1.0 constant_dynamic-slice_fusion.2
  1.7 0.7 copy.24
  2.3 1.3 bitcast_convert_fusion.table_ref
  3.6 143.7 %forward.1 = (bf16[4,1024,1024]{2,1,0:T(8,128)(2,1)}, bf16[1024,384]{1,0:T(8,128)(2,1)}, bf16[1024,768]{1,0:T(8,128)(2,1)}, bf16[1024,768]{1,0:T(8,128)(2,1)}, b...) custom-call(bf16[1024,256]{1,0:T(8,128)(2,1)} %query_ref.1, ...), custom_call_target="tpu_custom_call" | custom-call | tf_op jit(solution)/shard_map/forward/pallas_call | solution.py:1069
  147.3 108.9 %backward.1 = (f32[384,1024]{1,0:T(8,128)}, f32[64,128]{1,0:T(8,128)}, f32[2,704,128]{2,1,0:T(8,128)}, f32[1,704,128]{2,1,0:T(8,128)}, f32[4,256,128]{2,1,0:T(8,128)}) custom-call(bf16[2,2816,1024]{2,1,0:T(8,128)(2,1)} %get-tuple-element.35.refs_0_, bf16[1,2816,1024]{2,1,0:T(8,128)(2,1)} %get-tuple-element.36.refs_1_, ...), custom_call_target="tpu_custom_call" | custom-call | tf_op jit(solution)/shard_map/backward/pallas_call | solution.py:1498
  256.2 0.0 copy-start.4
  256.2 0.0 copy-start
  256.2 0.8 slice.15
  257.1 0.6 constant_dynamic-slice_fusion.1
  257.7 1.6 slice_bitcast_fusion.1
  259.4 0.8 copy.21
  260.1 1.0 slice_bitcast_fusion
  261.1 0.8 copy.22
  261.9 0.0 copy-done.4
  261.9 0.1 constant_dynamic-slice_fusion
  262.0 0.7 copy.23
  262.7 0.0 copy-done
  262.7 0.0 copy-start.1
  262.7 1.1 copy.29
  263.8 0.8 copy-done.1
  264.7 0.0 copy-start.2
  264.7 0.0 copy-start.3
  264.7 1.1 copy.30
  265.8 0.5 copy-done.2
  266.3 0.9 copy.31
  267.1 0.0 copy-done.3
  267.1 0.7 copy.32
  (2 shorter events, 0.0 us)
Async XLA Ops:
  256.2 5.7 %copy-start.4 = (f32[64,128]{1,0:T(8,128)S(1)}, f32[64,128]{1,0:T(8,128)}, u32[]{:S(2)}) copy-start(f32[64,128]{1,0:T(8,128)} %get-tuple-element.55) | copy-start | bytes 98308
  256.2 6.5 %copy-start = (f32[384,1024]{1,0:T(8,128)S(1)}, f32[384,1024]{1,0:T(8,128)}, u32[]{:S(2)}) copy-start(f32[384,1024]{1,0:T(8,128)} %get-tuple-element.79) | copy-start | bytes 4718596
  262.7 2.0 copy-start.1
  264.7 1.6 copy-start.2
  264.7 2.5 copy-start.3
